TPU v7x, 8 devices: a whole 2x2x1 slice. The times are simulated.
8 devices in a mesh: tg: 2 (over z, y), pp: 2 (over x), grp: 2 (over core).
Axes of the slice: x: 2, y: 2, z: 1, core: 2. Of those that a mesh axis runs over, the one named last changes fastest.
Arguments:
- hidden_in: bfloat16 [512, 1024], P(('pp', 'grp'))
- seq_lens: int32 [512], P(('pp', 'grp'))
- k_cache: bfloat16 [2, 512, 128, 16, 64], P(None, ('pp', 'grp'), None, 'tg')
- v_cache: bfloat16 [2, 512, 128, 16, 64], P(None, ('pp', 'grp'), None, 'tg')
- attn_gain: bfloat16 [2, 1024], P('pp')
- w_qkv: bfloat16 [2, 3072, 1024], P('pp', ('tg', 'grp'))
- w_o: bfloat16 [2, 1024, 1024], P('pp', None, ('tg', 'grp'))
- mlp_gain: bfloat16 [2, 1024], P('pp')
- w_gate_up: bfloat16 [2, 5632, 1024], P('pp', ('tg', 'grp'))
- w_down: bfloat16 [2, 1024, 2816], P('pp', None, ('tg', 'grp'))
Outputs:
- output 1: bfloat16 [512, 1024], P(('pp', 'grp'))
- output 2: bfloat16 [2, 512, 128, 16, 64], P(None, ('pp', 'grp'), None, 'tg')
- output 3: bfloat16 [2, 512, 128, 16, 64], P(None, ('pp', 'grp'), None, 'tg')
- output 4: bfloat16 [2, 3072, 1024], P(None, 'tg')
- output 5: bfloat16 [2, 5632, 1024], P(None, 'tg')
All inputs are finite; a program needn't handle non-finite values.
Results may differ from a plain program's by a relative error of at most 0.0160774.
Values are sent between devices in bfloat16 or wider.
A program may use at most 1 GiB of HBM per device.

v0:
```python
import functools

import jax
import jax.numpy as jnp
from jax import lax
from jax.experimental import pallas as pl
from jax.experimental.pallas import tpu as pltpu
from jax.sharding import PartitionSpec as P


ROPE_THETA = 500000.0
NORM_EPS = 1e-5
MASK_FILL = -1e30
UNROLL = 16
PARTS = 2
GU_CUTS = (17, 49, 71)
ROW_AXES = ("pp", "grp")
TRAIN_AXES = ("tg", "grp")
SWAP = ((0, 1), (1, 0))
F32 = jnp.float32
BF16 = jnp.bfloat16


def rms_norm(hidden, gain_vec):
    hidden_f32 = hidden.astype(F32)
    inv_rms = lax.rsqrt(jnp.mean(hidden_f32 * hidden_f32, axis=-1, keepdims=True) + NORM_EPS)
    return (hidden_f32 * inv_rms * gain_vec.astype(F32)).astype(BF16)


def rope_tables_t(seq_lens, head_dim):
    inv_freq = jnp.power(ROPE_THETA, -jnp.arange(0, head_dim, 2).astype(F32) / head_dim)
    angles = inv_freq[:, None] * seq_lens.astype(F32)[None, :]
    return jnp.cos(angles), jnp.sin(angles)


def place_kernel(spots_ref, *refs, count, blocks, alias):
    pieces = refs[:count]
    dst = refs[count + alias]
    bufs = refs[count + alias + 1:2 * count + alias + 1]
    sem_in, sem_out = refs[-2:]
    reads, writes = [], []
    for i, (p, src, _) in enumerate(blocks):
        reads.append(pltpu.make_async_copy(pieces[p].at[src], bufs[p].at[src], sem_in.at[i]))
        reads[-1].start()
    for i, (p, src, spot) in enumerate(blocks):
        reads[i].wait()
        target = dst.at[spot(spots_ref[p, 0], spots_ref[p, 1])]
        writes.append(pltpu.make_async_copy(bufs[p].at[src], target, sem_out.at[i]))
        writes[-1].start()
    for write in writes:
        write.wait()


def place(pieces, spots, dst, dst_shape, blocks):
    count, alias = len(pieces), int(dst is not None)
    size = sum(p.size for p in pieces)
    sems = pltpu.SemaphoreType.DMA((len(blocks),))
    return pl.pallas_call(
        functools.partial(place_kernel, count=count, blocks=blocks, alias=alias),
        in_specs=[pl.BlockSpec(memory_space=pltpu.SMEM)] + [pl.BlockSpec(memory_space=pl.ANY)] * (count + alias),
        out_specs=pl.BlockSpec(memory_space=pl.ANY),
        out_shape=jax.ShapeDtypeStruct(dst_shape, BF16),
        scratch_shapes=[pltpu.VMEM(p.shape, BF16) for p in pieces] + [sems, sems],
        input_output_aliases={count + 1: 0} if alias else {},
        compiler_params=pltpu.CompilerParams(vmem_limit_bytes=2 * size + (2 << 20)),
        cost_estimate=pl.CostEstimate(flops=size * 3000, bytes_accessed=size * 4, transcendentals=0),
        name="place",
    )(jnp.stack(spots), *pieces, *([dst] if alias else []))


def rope_t(vals, cos_t, sin_t):
    half = vals.shape[1] // 2
    lo, hi = vals[:, :half], vals[:, half:]
    return jnp.concatenate([lo * cos_t[None] - hi * sin_t[None], hi * cos_t[None] + lo * sin_t[None]], axis=1)


def project_kernel(half_ref, own_ref, away_ref, gain_ref, wa_ref, wb_ref, cos_ref, sin_ref, own_out, away_out):
    groups, _, head_dim, model = wa_ref.shape
    count = own_ref.shape[0]
    rows = groups * head_dim
    normed = rms_norm(jnp.concatenate([own_ref[...], away_ref[...]], axis=0), gain_ref[...])
    for ref, shard in ((wa_ref, half_ref[0]), (wb_ref, 1 - half_ref[0])):
        spot = pl.ds(pl.multiple_of(shard * rows, rows), rows)
        for t in range(3):
            w = ref[:, t].reshape(rows, model)
            vals = lax.dot_general(w, normed, (((1,), (1,)), ((), ())), preferred_element_type=F32)
            if t < 2:
                vals = rope_t(vals.reshape(groups, head_dim, 2 * count), cos_ref[...], sin_ref[...])
                vals = vals.reshape(rows, 2 * count)
            vals = vals.astype(BF16)
            own_out[t, spot, :] = vals[:, :count]
            away_out[t, spot, :] = vals[:, count:]


def project(half, own, away, gain, w_own, w_near, cos_t, sin_t):
    count = own.shape[0]
    out = jax.ShapeDtypeStruct((3, 2 * w_own.shape[0] * w_own.shape[2], count), BF16)
    vmem = pl.BlockSpec(memory_space=pltpu.VMEM)
    return pl.pallas_call(
        project_kernel,
        in_specs=[pl.BlockSpec(memory_space=pltpu.SMEM)] + [vmem] * 7,
        out_specs=[vmem] * 2, out_shape=[out, out],
        compiler_params=pltpu.CompilerParams(vmem_limit_bytes=24 << 20),
        cost_estimate=pl.CostEstimate(flops=3_000_000_000, bytes_accessed=w_own.size * 4, transcendentals=0),
        name="project",
    )(half, own, away, gain, w_own, w_near, cos_t, sin_t)


def mlp_kernel(rank_ref, hid_ref, away_ref, gain_ref, gu_a, gu_b, dn_a, dn_b, keep_ref, give_ref, base_ref,
               gu_s, dn_s, total, sems):
    count = hid_ref.shape[0]
    mid = count // 2
    copies = []
    for p, (gu, dn) in enumerate(((gu_a, dn_a), (gu_b, dn_b))):
        for t, (src, dst) in enumerate(((gu.at[0], gu_s.at[p, 0]), (gu.at[1], gu_s.at[p, 1]), (dn, dn_s.at[p]))):
            copies.append(pltpu.make_async_copy(src, dst, sems.at[3 * p + t]))
            copies[-1].start()
    normed = rms_norm(jnp.concatenate([hid_ref[...], away_ref[...]], axis=0), gain_ref[...])
    nt = (((1,), (1,)), ((), ()))
    for p in range(2):
        copies[3 * p].wait()
        gate = lax.dot_general(gu_s[p, 0], normed, nt, preferred_element_type=F32)
        copies[3 * p + 1].wait()
        up = lax.dot_general(gu_s[p, 1], normed, nt, preferred_element_type=F32)
        act = (jax.nn.silu(gate) * up).T.astype(BF16)
        copies[3 * p + 2].wait()
        part = jnp.dot(act, dn_s[p], preferred_element_type=F32)
        total[...] = part if p == 0 else total[...] + part
    rank = rank_ref[0]
    mine = pl.multiple_of(rank * mid, mid)
    peer = pl.multiple_of((1 - rank) * mid, mid)
    for i, ref in enumerate((hid_ref, away_ref)):
        keep_ref[i * mid:(i + 1) * mid, :] = total[pl.ds(i * count + mine, mid), :]
        give_ref[i * mid:(i + 1) * mid, :] = total[pl.ds(i * count + peer, mid), :]
        base_ref[i * mid:(i + 1) * mid, :] = ref[pl.ds(mine, mid), :]


def mlp(rank, hid, away, gain, gus, downs):
    count, model = hid.shape
    ffn = downs[0].shape[0]
    vmem, hbm = pl.BlockSpec(memory_space=pltpu.VMEM), pl.BlockSpec(memory_space=pl.ANY)
    half_f32 = jax.ShapeDtypeStruct((count, model), F32)
    return pl.pallas_call(
        mlp_kernel,
        in_specs=[pl.BlockSpec(memory_space=pltpu.SMEM)] + [vmem] * 3 + [hbm] * 4,
        out_specs=[vmem] * 3,
        out_shape=[half_f32, half_f32, jax.ShapeDtypeStruct((count, model), BF16)],
        scratch_shapes=[pltpu.VMEM((2, 2, ffn, model), BF16), pltpu.VMEM((2, ffn, model), BF16),
                        pltpu.VMEM((2 * count, model), F32), pltpu.SemaphoreType.DMA((6,))],
        compiler_params=pltpu.CompilerParams(vmem_limit_bytes=32 << 20),
        cost_estimate=pl.CostEstimate(flops=4_000_000_000, bytes_accessed=6 * ffn * model * 2, transcendentals=0),
        name="mlp",
    )(rank, hid, away, gain, *gus, *downs)


def attn_kernel(lens_ref, *rest, heads, head_dim, scale, row0, ready):
    heads_in, rest = rest[:1 if ready else 5], rest[1 if ready else 5:]
    k_ref, v_ref = rest[:2]
    o_ref, ko_ref, vo_ref, q_s, kt_s, vt_s, o_s, p_s = rest[-8:]
    rows = heads * head_dim
    per = k_ref.shape[1]
    seq = k_ref.shape[-1]
    batch = seq
    step = pl.program_id(0)

    @pl.when(step == 0)
    def _():
        if ready:
            for t, ref in enumerate((None, kt_s, vt_s)):
                vals = heads_in[0][t].astype(F32)
                if t:
                    ref[...] = vals
                else:
                    q_s[...] = vals.T
            return
        h_ref, gain_ref, w_ref, cos_ref, sin_ref = heads_in
        normed = rms_norm(h_ref[...], gain_ref[...])
        normed = jnp.concatenate([normed] * (batch // h_ref.shape[0]), axis=0)

        def proj(t, turn):
            vals = lax.dot_general(w_ref[0, t * rows:(t + 1) * rows, :], normed, (((1,), (1,)), ((), ())),
                                   preferred_element_type=F32)
            if turn:
                vals = rope_t(vals.reshape(heads, head_dim, batch), cos_ref[...], sin_ref[...])
            return vals.reshape(rows, batch).astype(BF16).astype(F32)

        q_s[...] = proj(0, True).T
        kt_s[...] = proj(1, True)
        vt_s[...] = proj(2, False)

    lane = lax.broadcasted_iota(jnp.int32, (1, seq), 1)
    head_of = lax.broadcasted_iota(jnp.int32, (heads, rows), 1) // head_dim
    mine = head_of == lax.broadcasted_iota(jnp.int32, (heads, rows), 0)

    def insert(i, carry):
        b = row0 + step * per + i
        n = lens_ref[b]
        shift = lax.rem(n - b + seq, seq)
        at_n = jnp.broadcast_to(lane == n, (rows, seq))
        k_new = pltpu.roll(kt_s[...], shift, 1).astype(BF16)
        v_new = pltpu.roll(vt_s[...], shift, 1).astype(BF16)
        k_all = jnp.where(at_n, k_new, k_ref[0, i].reshape(rows, seq))
        v_all = jnp.where(at_n, v_new, v_ref[0, i].reshape(rows, seq))
        ko_ref[0, i] = k_all.reshape(heads, head_dim, seq)
        vo_ref[0, i] = v_all.reshape(heads, head_dim, seq)
        q_diag = jnp.where(mine, q_s[pl.ds(b, 1), :], 0.0).astype(BF16)
        scores = jnp.dot(q_diag, k_all, preferred_element_type=F32) * scale
        p_s[pl.ds(pl.multiple_of(i * heads, heads), heads), :] = jnp.where(lane <= n, scores, MASK_FILL)
        return carry

    lax.fori_loop(0, per, insert, 0, unroll=UNROLL)
    scores = p_s[...]
    expd = jnp.exp(scores - jnp.max(scores, axis=-1, keepdims=True))
    p_s[...] = (expd / jnp.sum(expd, axis=-1, keepdims=True)).astype(BF16).astype(F32)

    def combine(i, carry):
        probs = p_s[pl.ds(pl.multiple_of(i * heads, heads), heads), :].astype(BF16)
        outs = lax.dot_general(probs, vo_ref[0, i].reshape(rows, seq), (((1,), (1,)), ((), ())),
                               preferred_element_type=F32)
        o_s[pl.ds(i, 1), :] = jnp.sum(jnp.where(mine, outs, 0.0), axis=0, keepdims=True)
        return carry

    lax.fori_loop(0, per, combine, 0, unroll=UNROLL)
    o_ref[...] = o_s[...].astype(BF16)


def attention(layer, part, parts, heads_in, seq_lens, kc, vc, outs):
    _, batch, heads, head_dim, seq = kc.shape
    rows = heads * head_dim
    count = batch // parts
    ready = len(heads_in) == 1
    per = 16
    first = part * count // per
    whole = lambda *shape: pl.BlockSpec(shape, lambda s, n: (0,) * len(shape))
    cache_block = pl.BlockSpec((1, per, heads, head_dim, seq), lambda s, n: (layer, first + s, 0, 0, 0))
    if ready:
        in_specs = [whole(3, rows, seq)]
    else:
        model = heads_in[0].shape[1]
        in_specs = [whole(count, model), whole(1, model), pl.BlockSpec((1, 3 * rows, model), lambda s, n: (layer, 0, 0)),
                    whole(head_dim // 2, seq), whole(head_dim // 2, seq)]
    in_specs += [cache_block, cache_block]
    args = [seq_lens, *heads_in, kc, vc]
    aliases = {}
    if outs is not None:
        in_specs += [pl.BlockSpec(memory_space=pl.ANY)] * 2
        args += list(outs)
        aliases = {len(args) - 2: 1, len(args) - 1: 2}
    cache_shape = jax.ShapeDtypeStruct(kc.shape, kc.dtype)
    return pl.pallas_call(
        functools.partial(attn_kernel, heads=heads, head_dim=head_dim, scale=head_dim ** -0.5, row0=part * count,
                          ready=ready),
        grid_spec=pltpu.PrefetchScalarGridSpec(
            num_scalar_prefetch=1, grid=(count // per,), in_specs=in_specs,
            out_specs=[pl.BlockSpec((per, rows), lambda s, n: (s, 0)), cache_block, cache_block],
            scratch_shapes=[pltpu.VMEM((seq, rows), F32), pltpu.VMEM((rows, seq), F32),
                            pltpu.VMEM((rows, seq), F32), pltpu.VMEM((per, rows), F32),
                            pltpu.VMEM((per * heads, seq), F32)]),
        out_shape=[jax.ShapeDtypeStruct((count, rows), BF16), cache_shape, cache_shape],
        input_output_aliases=aliases,
        compiler_params=pltpu.CompilerParams(dimension_semantics=("arbitrary",), vmem_limit_bytes=48 << 20),
        cost_estimate=pl.CostEstimate(flops=30_000_000_000 // parts, bytes_accessed=kc.size * 4 // parts,
                                      transcendentals=0),
    )(*args)


def solution(mesh):
    cache_spec = P(None, ROW_AXES, None, "tg", None)
    in_specs = (P(ROW_AXES, None), P(ROW_AXES), cache_spec, cache_spec,
                P("pp", None), P("pp", TRAIN_AXES, None), P("pp", None, TRAIN_AXES),
                P("pp", None), P("pp", TRAIN_AXES, None), P("pp", None, TRAIN_AXES))
    out_specs = (P(ROW_AXES, None), cache_spec, cache_spec, P(None, "tg", None), P(None, "tg", None))

    def decode(hidden_in, seq_lens, k_cache, v_cache, attn_gain, w_qkv, w_o, mlp_gain, w_gate_up, w_down):
        layers, batch, _, _, head_dim = k_cache.shape
        model = hidden_in.shape[1]
        stage = lax.axis_index("pp")
        rank = lax.axis_index("tg")
        half = lax.axis_index("grp")
        groups = w_qkv.shape[1] // (3 * head_dim)
        ffn = w_gate_up.shape[1] // 2
        cols = w_o.shape[2]

        def swap(x, axis):
            return lax.ppermute(x, axis, SWAP)

        def after(x, *deps):
            return lax.optimization_barrier((x,) + deps)[0]

        kc = jnp.transpose(k_cache, (0, 1, 3, 4, 2))
        vc = jnp.transpose(v_cache, (0, 1, 3, 4, 2))

        away_lens = swap(seq_lens, "pp")
        away_in = swap(hidden_in, "pp")
        shard_qkv = w_qkv.reshape(groups, 3, head_dim, model)
        near_qkv = swap(shard_qkv, "grp")
        gains = jnp.stack([attn_gain[0], mlp_gain[0]])
        far_gains = swap(gains, "pp")
        cos_t, sin_t = rope_tables_t(seq_lens, head_dim)
        away_cos, away_sin = rope_tables_t(away_lens, head_dim)
        heads_own, heads_away = project(
            half[None], hidden_in, away_in, attn_gain, shard_qkv, near_qkv,
            jnp.concatenate([cos_t, away_cos], axis=1), jnp.concatenate([sin_t, away_sin], axis=1))
        heads_back = swap(heads_away, "pp")

        shard_o = w_o[0]
        peer_o = swap(shard_o, "tg")
        near_o = swap(shard_o, "grp")
        shard_gu = w_gate_up.reshape(2, ffn, model)
        shard_down = jnp.transpose(w_down[0])
        near_gu = swap(shard_gu, "grp")
        near_down = swap(shard_down, "grp")
        peer_near_o = swap(peer_o, "grp")

        spots = ((stage, half), (stage, 1 - half), (1 - stage, half), (1 - stage, 1 - half))
        spots = [jnp.stack(spot).astype(jnp.int32) for spot in spots]

        qkv_shape = (layers, 3, 2, groups, head_dim, model)
        gu_shape = (layers, 2, 2, ffn, model)

        def qkv_blocks(pieces, first, many):
            return [(p, (slice(None), t), lambda lay, sh, t=t: (lay, t, sh, pl.ds(first, many)))
                    for p in range(pieces) for t in range(3)]

        def gu_blocks(pieces, lo, hi):
            blocks = []
            for p in range(pieces):
                for t in range(2):
                    a, b = max(lo, t * ffn), min(hi, (t + 1) * ffn)
                    if a < b:
                        blocks.append((p, pl.ds(a - lo, b - a), lambda lay, sh, t=t, a=a, b=b: (
                            lay, t, sh, pl.ds(a - t * ffn, b - a))))
            return blocks

        def qkv_send(i, *deps):
            many = groups // 2
            return swap(after(shard_qkv[i * many:(i + 1) * many], *deps), "pp")

        def qkv_take(i, piece, dst):
            many = groups // 2
            near = swap(piece, "grp")
            return place([piece, near], spots[2:], dst, qkv_shape, qkv_blocks(2, i * many, many))

        cuts = [0, GU_CUTS[0] * ffn // 44, GU_CUTS[1] * ffn // 44, GU_CUTS[2] * ffn // 44, 2 * ffn]

        def gu_send(c, *deps):
            return swap(after(w_gate_up[0, cuts[c]:cuts[c + 1]], *deps), "pp")

        def gu_take(c, piece, dst):
            near = swap(piece, "grp")
            return place([piece, near], spots[2:], dst, gu_shape, gu_blocks(2, cuts[c], cuts[c + 1]))

        gen_qkv = place([shard_qkv, near_qkv], spots[:2], None, qkv_shape, qkv_blocks(2, 0, groups))
        flat_gu = lambda x: x.reshape(2 * ffn, model)
        gen_gu = place([flat_gu(shard_gu), flat_gu(near_gu)], spots[:2], None, gu_shape, gu_blocks(2, 0, 2 * ffn))
        heads_in = jnp.where(stage == 0, heads_own, after(heads_back, gen_qkv, gen_gu))

        first = jnp.where(stage == 0, gains, far_gains)
        second = jnp.where(stage == 0, far_gains, gains)
        far_o = swap(after(shard_o, heads_back), "pp")
        far_heads = [qkv_send(0, heads_back)]
        count = batch // PARTS
        mid = count // 2
        hidden = [hidden_in[i * count:(i + 1) * count] for i in range(PARTS)]
        caches = None
        by_half = lambda x: (jnp.where(half == 0, x[:, :cols], x[:, cols:]),
                             jnp.where(half == 0, x[:, cols:], x[:, :cols]))
        sent = {}
        for layer, gain in enumerate((first, second)):
            o_vals = []
            for i in range(PARTS):
                vals = (heads_in,) if layer == 0 else (
                    hidden[i], gain[0][None], gen_qkv.reshape(layers, 6 * groups * head_dim, model), cos_t, sin_t)
                o_part, *caches = attention(layer, i, PARTS, vals, seq_lens, kc, vc, caches)
                if i == 0 and layer == 0:
                    far_o = after(far_o, o_part)
                    far_peer_o = swap(far_o, "tg")
                    far_near_o = swap(far_o, "grp")
                    caches[0] = after(caches[0], far_o)
                    far_heads.append(qkv_send(1, o_part))
                if i == 0 and layer == 1:
                    sent[1] = after(sent[1], o_part)
                    caches[0] = after(caches[0], sent[1])
                    sent[2] = gu_send(2, o_part)
                o_vals.append(o_part)
            if layer == 0:
                far_heads[0] = after(far_heads[0], o_vals[1])
                gen_qkv = qkv_take(0, far_heads[0], gen_qkv)
                stage_o = (shard_o, near_o, peer_o, peer_near_o)
                away_o = (far_o, far_near_o, far_peer_o, swap(far_peer_o, "grp"))
                stage_o, away_o = jnp.concatenate(stage_o, axis=1), jnp.concatenate(away_o, axis=1)
                layer_o = (jnp.where(stage == 0, stage_o, away_o), jnp.where(stage == 0, away_o, stage_o))
            if layer == 1:
                sent[2] = after(sent[2], o_vals[1])
            backs, owns = [], []
            give = None
            for i in range(PARTS):
                o_peer = after(swap(o_vals[i], "tg"), o_vals[1])
                o_all = jnp.concatenate(by_half(o_vals[i]) + by_half(o_peer), axis=1)
                proj = jnp.einsum("bk,dk->bd", o_all, layer_o[layer], preferred_element_type=F32)
                hid = (hidden[i].astype(F32) + proj).astype(BF16)
                away = swap(hid, "pp")
                if i:
                    sent[3 * layer] = gu_send(3 * layer, away)
                    away = after(away, give)
                elif layer == 0:
                    far_heads[1] = after(far_heads[1], hid)
                    away = after(away, far_heads[1])
                    gen_qkv = qkv_take(1, far_heads[1], gen_qkv)
                keep, give, base = mlp(rank[None], hid, away, mlp_gain, (shard_gu, near_gu), (shard_down, near_down))
                if i:
                    if layer == 0:
                        keep = after(keep, gen_qkv)
                    else:
                        for c in (1, 2):
                            gen_gu = gu_take(c, sent[c], gen_gu)
                        keep = after(keep, gen_gu)
                done = (base.astype(F32) + (keep + swap(give, "tg"))).astype(BF16)
                owns.append(done[:mid])
                backs.append(swap(done[mid:], "pp"))
            if layer == 0:
                sent[1] = gu_send(1, *backs)
                gen_gu = gu_take(0, sent[0], gen_gu)
            hidden = []
            for own, back in zip(owns, backs):
                block = jnp.where(stage == layer, own, back)
                other = swap(block, "tg")
                hidden.append(jnp.concatenate([jnp.where(rank == 0, block, other),
                                               jnp.where(rank == 0, other, block)], axis=0))
        gen_gu = gu_take(3, sent[3], gen_gu)
        hidden = jnp.concatenate(hidden, axis=0)
        gen_qkv = gen_qkv.reshape(layers, 6 * groups * head_dim, model)

        restore = lambda x: jnp.transpose(x, (0, 1, 4, 2, 3))
        return (hidden, restore(caches[0]), restore(caches[1]), gen_qkv, gen_gu.reshape(layers, 4 * ffn, model))

    return jax.shard_map(decode, mesh=mesh, in_specs=in_specs, out_specs=out_specs, check_vma=False)
```

profile of v0, /device:TPU:0, one launch (start us, length us, event | category | flops | bytes accessed | tf_op | source)
XLA Modules:
  0.0 231.6 jit_solution(3159820300244677305)
XLA Ops:
  0.6 3.3 %collective-permute-start = (bf16[128,1024]{1,0:T(8,128)(2,1)}, bf16[128,1024]{1,0:T(8,128)(2,1)S(1)}, u32[]{:S(2)}, u32[]{:S(2)}) collective-permute-start(bf16[128,1024]{1,0:T(8,128)(2,1)} %own_ref.1), channel_id=1, source_target_pairs={{0,2},{2,0},{1,3},{3,1},{4,6},{6,4},{5,7},{7,5}} | collective-permute-start | bytes 786440 | tf_op jit(solution)/shard_map/ppermute | solution.py:285
  4.5 1.8 collective-permute-start.8
  6.6 2.0 slice_bitcast_fusion.1
  8.6 0.7 pad_maximum_fusion.6
  9.4 2.5 %slice_bitcast_fusion.2 = (bf16[272,1024]{1,0:T(8,128)(2,1)}, bf16[272,1024]{1,0:T(8,128)(2,1)}) fusion(bf16[1,1408,1024]{2,1,0:T(8,128)(2,1)} %param.18), kind=kLoop, calls=%fused_computation.13 | loop fusion | bytes 2228224 | tf_op jit(solution)/shard_map/squeeze | solution.py:347
  11.8 1.1 slice_bitcast_fusion
  12.9 1.3 fusion.36
  14.2 1.5 collective-permute-start.19
  15.9 1.9 collective-permute-done.19
  17.9 1.4 copy-done.2
  19.3 2.6 %project.1 = (bf16[3,512,128]{2,1,0:T(8,128)(2,1)S(1)}, bf16[3,512,128]{2,1,0:T(8,128)(2,1)S(1)}) custom-call(s32[1]{0:T(128)} %bitcast.1.half_ref, bf16[128,1024]{1,0:T(8,128)(2,1)S(1)} %copy-done.7, bf16[128,1024]{1,0:T(8,128)(2,1)S(1)} %collective-permute-done.away_ref, bf16[1,1024]{1,0:T(2,128)(2,1)S(1)} %copy-done.3, ...), custom_call_target="tpu_custom_call" | custom-call | flops 3000000000 | bytes 3145728 | tf_op jit(solution)/shard_map/project/pallas_call | solution.py:99
  21.9 1.5 collective-permute-start.3
  23.4 3.5 %place.8.refs_2_ = bf16[2,3,2,4,64,1024]{5,4,3,2,1,0:T(8,128)(2,1)} custom-call(s32[2,2]{1,0:T(2,128)S(1)} %pad_add_fusion.spots_ref, bf16[4,3,64,1024]{3,2,1,0:T(8,128)(2,1)S(1)} %bitcast.45, bf16[4,3,64,1024]{3,2,1,0:T(8,128)(2,1)} %collective-permute-done.1.wb_ref.refs_1_), custom_call_target="tpu_custom_call" | custom-call | flops 4718592000 | bytes 6291456 | tf_op jit(solution)/shard_map/place/pallas_call | solution.py:58
  26.9 6.5 %collective-permute-done.3 = bf16[3,512,128]{2,1,0:T(8,128)(2,1)S(1)} collective-permute-done((bf16[3,512,128]{2,1,0:T(8,128)(2,1)S(1)}, bf16[3,512,128]{2,1,0:T(8,128)(2,1)S(1)}, u32[]{:S(2)}, u32[]{:S(2)}) %collective-permute-start.3) | collective-permute-done | bytes 393248 | tf_op jit(solution)/shard_map/ppermute | solution.py:285
  33.5 1.5 collective-permute-start.6
  35.5 5.1 %place.9.refs_2_ = bf16[2,2,2,704,1024]{4,3,2,1,0:T(8,128)(2,1)} custom-call(s32[2,2]{1,0:T(2,128)S(1)} %pad_add_fusion.spots_ref, bf16[1408,1024]{1,0:T(8,128)(2,1)S(1)} %bitcast.38, bf16[1408,1024]{1,0:T(8,128)(2,1)} %bitcast.9.refs_1_), custom_call_target="tpu_custom_call" | custom-call | flops 8650752000 | bytes 11534336 | tf_op jit(solution)/shard_map/place/pallas_call | solution.py:58
  40.6 14.4 %shard_map.137 = (bf16[64,512]{1,0:T(8,128)(2,1)S(1)}, bf16[2,128,8,64,128]{4,3,2,1,0:T(8,128)(2,1)}, bf16[2,128,8,64,128]{4,3,2,1,0:T(8,128)(2,1)}) custom-call(s32[128]{0:T(128)S(1)} %copy-done.5, bf16[3,512,128]{2,1,0:T(8,128)(2,1)S(1)} %broadcast_select_fusion.6.rest_0_, bf16[2,128,8,64,128]{4,3,2,1,0:T(8,128)(2,1)} %bitcast.51, ...), custom_call_target="tpu_custom_call" | custom-call | flops 15000000512 | bytes 33554432 | tf_op jit(solution)/shard_map/pallas_call | solution.py:250
  55.4 14.5 %shard_map.138 = (bf16[64,512]{1,0:T(8,128)(2,1)S(1)}, bf16[2,128,8,64,128]{4,3,2,1,0:T(8,128)(2,1)}, bf16[2,128,8,64,128]{4,3,2,1,0:T(8,128)(2,1)}) custom-call(s32[128]{0:T(128)S(1)} %copy-done.5, bf16[3,512,128]{2,1,0:T(8,128)(2,1)S(1)} %broadcast_select_fusion.6.rest_0_, ...), custom_call_target="tpu_custom_call", output_to_operand_aliasing={{1}: (4, {}), {2}: (5, {})} | custom-call | flops 15000000512 | bytes 33554432 | tf_op jit(solution)/shard_map/pallas_call | solution.py:250
  69.9 1.8 collective-permute-start.24
  71.7 2.5 %collective-permute-done.24 = bf16[64,512]{1,0:T(8,128)(2,1)S(1)} collective-permute-done((bf16[64,512]{1,0:T(8,128)(2,1)S(1)}, bf16[64,512]{1,0:T(8,128)(2,1)S(1)}, u32[]{:S(2)}, u32[]{:S(2)}) %collective-permute-start.24) | collective-permute-done | bytes 65568 | tf_op jit(solution)/shard_map/ppermute | solution.py:285
  74.2 1.8 collective-permute-start.5
  76.6 1.9 collective-permute-done.5
  78.5 1.8 collective-permute-start.14
  80.8 1.9 fusion.hid_ref
  82.7 1.6 collective-permute-start.13
  84.3 14.6 %collective-permute-done.14.refs_0_ = bf16[2,3,64,1024]{3,2,1,0:T(8,128)(2,1)S(1)} collective-permute-done((bf16[2,3,64,1024]{3,2,1,0:T(8,128)(2,1)S(1)}, bf16[2,3,64,1024]{3,2,1,0:T(8,128)(2,1)S(1)}, u32[]{:S(2)}, u32[]{:S(2)}) %collective-permute-start.14) | collective-permute-done | bytes 786464 | tf_op jit(solution)/shard_map/ppermute | solution.py:285
  99.0 2.3 %collective-permute-done.13.away_ref = bf16[64,1024]{1,0:T(8,128)(2,1)S(1)} collective-permute-done((bf16[64,1024]{1,0:T(8,128)(2,1)S(1)}, bf16[64,1024]{1,0:T(8,128)(2,1)S(1)}, u32[]{:S(2)}, u32[]{:S(2)}) %collective-permute-start.13) | collective-permute-done | bytes 131104 | tf_op jit(solution)/shard_map/ppermute | solution.py:285
  101.3 5.7 %mlp.4 = (f32[64,1024]{1,0:T(8,128)S(1)}, f32[64,1024]{1,0:T(8,128)S(1)}, bf16[64,1024]{1,0:T(8,128)(2,1)S(1)}) custom-call(s32[1]{0:T(128)} %bitcast.rank_ref, bf16[64,1024]{1,0:T(8,128)(2,1)S(1)} %fusion.hid_ref, bf16[64,1024]{1,0:T(8,128)(2,1)S(1)} %collective-permute-done.13.away_ref, bf16[1,1024]{1,0:T(2,128)(2,1)S(1)} %copy-done.4, ...), custom_call_target="tpu_custom_call" | custom-call | flops 4000000000 | bytes 8650752 | tf_op jit(solution)/shard_map/mlp/pallas_call | solution.py:143
  107.0 1.8 collective-permute-start.16
  108.8 1.8 fusion.1.hid_ref
  110.6 1.5 collective-permute-start.25
  112.1 2.8 %collective-permute-done.16 = f32[64,1024]{1,0:T(8,128)S(1)} collective-permute-done((f32[64,1024]{1,0:T(8,128)S(1)}, f32[64,1024]{1,0:T(8,128)S(1)}, u32[]{:S(2)}, u32[]{:S(2)}) %collective-permute-start.16) | collective-permute-done | bytes 262176 | tf_op jit(solution)/shard_map/ppermute | solution.py:285
  115.0 1.7 collective-permute-start.17
  116.7 1.9 place.10.refs_2_
  119.3 1.8 collective-permute-start.18
  121.0 5.7 %mlp.5 = (f32[64,1024]{1,0:T(8,128)S(1)}, f32[64,1024]{1,0:T(8,128)S(1)}, bf16[64,1024]{1,0:T(8,128)(2,1)S(1)}) custom-call(s32[1]{0:T(128)} %bitcast.rank_ref, bf16[64,1024]{1,0:T(8,128)(2,1)S(1)} %fusion.1.hid_ref, bf16[64,1024]{1,0:T(8,128)(2,1)S(1)} %collective-permute-done.25.away_ref, bf16[1,1024]{1,0:T(2,128)(2,1)S(1)} %copy-done.4, ...), custom_call_target="tpu_custom_call" | custom-call | flops 4000000000 | bytes 8650752 | tf_op jit(solution)/shard_map/mlp/pallas_call | solution.py:143
  127.0 1.7 collective-permute-start.39
  128.7 1.9 place.11
  130.7 3.7 %collective-permute-done.26 = f32[64,1024]{1,0:T(8,128)S(1)} collective-permute-done((f32[64,1024]{1,0:T(8,128)S(1)}, f32[64,1024]{1,0:T(8,128)S(1)}, u32[]{:S(2)}, u32[]{:S(2)}) %collective-permute-start.26) | collective-permute-done | bytes 262176 | tf_op jit(solution)/shard_map/ppermute | solution.py:285
  134.9 6.6 %collective-permute-done.39.refs_0_ = bf16[272,1024]{1,0:T(8,128)(2,1)S(1)} collective-permute-done((bf16[272,1024]{1,0:T(8,128)(2,1)S(1)}, bf16[272,1024]{1,0:T(8,128)(2,1)S(1)}, u32[]{:S(2)}, u32[]{:S(2)}) %collective-permute-start.39) | collective-permute-done | bytes 557088 | tf_op jit(solution)/shard_map/ppermute | solution.py:285
  142.6 16.7 %shard_map.139 = (bf16[64,512]{1,0:T(8,128)(2,1)S(1)}, bf16[2,128,8,64,128]{4,3,2,1,0:T(8,128)(2,1)}, bf16[2,128,8,64,128]{4,3,2,1,0:T(8,128)(2,1)}) custom-call(s32[128]{0:T(128)S(1)} %copy-done.5, bf16[64,1024]{1,0:T(8,128)(2,1)S(1)} %pad_maximum_fusion.2.rest_0_, ...), custom_call_target="tpu_custom_call", output_to_operand_aliasing={{1}: (8, {}), {2}: (9, {})} | custom-call | flops 15000000512 | bytes 33554432 | tf_op jit(solution)/shard_map/pallas_call | solution.py:250
  159.3 1.7 collective-permute-start.23
  161.4 1.7 collective-permute-start.36
  163.1 2.2 collective-permute-done.28
  165.3 1.7 place.12.refs_2_
  167.1 1.2 collective-permute-done.29.refs_0_
  168.3 16.5 %shard_map.140 = (bf16[64,512]{1,0:T(8,128)(2,1)S(1)}, bf16[2,128,8,64,128]{4,3,2,1,0:T(8,128)(2,1)}, bf16[2,128,8,64,128]{4,3,2,1,0:T(8,128)(2,1)}) custom-call(s32[128]{0:T(128)S(1)} %copy-done.5, bf16[64,1024]{1,0:T(8,128)(2,1)S(1)} %pad_maximum_fusion.3.rest_0_, ...), custom_call_target="tpu_custom_call", output_to_operand_aliasing={{1}: (8, {}), {2}: (9, {})} | custom-call | flops 15000000512 | bytes 33554432 | tf_op jit(solution)/shard_map/pallas_call | solution.py:250
  184.8 1.5 collective-permute-start.34
  186.4 1.8 fusion.2.hid_ref
  189.1 1.8 fusion.3.hid_ref
  190.9 1.4 collective-permute-start.35
  192.3 2.2 collective-permute-done.30.away_ref
  194.5 5.7 %mlp.6 = (f32[64,1024]{1,0:T(8,128)S(1)}, f32[64,1024]{1,0:T(8,128)S(1)}, bf16[64,1024]{1,0:T(8,128)(2,1)S(1)}) custom-call(s32[1]{0:T(128)} %bitcast.rank_ref, bf16[64,1024]{1,0:T(8,128)(2,1)S(1)} %fusion.2.hid_ref, bf16[64,1024]{1,0:T(8,128)(2,1)S(1)} %collective-permute-done.30.away_ref, bf16[1,1024]{1,0:T(2,128)(2,1)S(1)} %copy-done.4, ...), custom_call_target="tpu_custom_call" | custom-call | flops 4000000000 | bytes 8650752 | tf_op jit(solution)/shard_map/mlp/pallas_call | solution.py:143
  200.8 5.7 %mlp.7 = (f32[64,1024]{1,0:T(8,128)S(1)}, f32[64,1024]{1,0:T(8,128)S(1)}, bf16[64,1024]{1,0:T(8,128)(2,1)S(1)}) custom-call(s32[1]{0:T(128)} %bitcast.rank_ref, bf16[64,1024]{1,0:T(8,128)(2,1)S(1)} %fusion.3.hid_ref, bf16[64,1024]{1,0:T(8,128)(2,1)S(1)} %collective-permute-done.35.away_ref, bf16[1,1024]{1,0:T(2,128)(2,1)S(1)} %copy-done.4, ...), custom_call_target="tpu_custom_call" | custom-call | flops 4000000000 | bytes 8650752 | tf_op jit(solution)/shard_map/mlp/pallas_call | solution.py:143
  206.5 1.4 collective-permute-start.41
  208.1 1.9 collective-permute-start.32
  210.0 2.7 %place.13.refs_2_ = bf16[2,2,2,704,1024]{4,3,2,1,0:T(8,128)(2,1)} custom-call(s32[2,2]{1,0:T(2,128)S(1)} %pad_add_fusion.1.spots_ref, bf16[512,1024]{1,0:T(8,128)(2,1)S(1)} %collective-permute-done.29.refs_0_, bf16[512,1024]{1,0:T(8,128)(2,1)S(1)} %collective-permute-done.38.refs_1_, ...), custom_call_target="tpu_custom_call", output_to_operand_aliasing={{}: (3, {})} | custom-call | flops 3145728000 | bytes 4194304 | tf_op jit(solution)/shard_map/place/pallas_call | solution.py:58
  212.7 2.3 place.14.refs_2_
  215.3 8.0 %collective-permute-done.32 = bf16[32,1024]{1,0:T(8,128)(2,1)S(1)} collective-permute-done((bf16[32,1024]{1,0:T(8,128)(2,1)S(1)}, bf16[32,1024]{1,0:T(8,128)(2,1)S(1)}, u32[]{:S(2)}, u32[]{:S(2)}) %collective-permute-start.32) | collective-permute-done | bytes 65568 | tf_op jit(solution)/shard_map/ppermute | solution.py:285
  223.9 1.4 collective-permute-start.43
  225.3 2.8 %collective-permute-done.33 = bf16[32,1024]{1,0:T(8,128)(2,1)S(1)} collective-permute-done((bf16[32,1024]{1,0:T(8,128)(2,1)S(1)}, bf16[32,1024]{1,0:T(8,128)(2,1)S(1)}, u32[]{:S(2)}, u32[]{:S(2)}) %collective-permute-start.33) | collective-permute-done | bytes 65568 | tf_op jit(solution)/shard_map/ppermute | solution.py:285
  228.2 0.8 collective-permute-done.43
  229.0 0.7 pad_maximum_fusion.1
  229.7 1.7 place.15
  (128 shorter events, 8.9 us)
Async XLA Ops:
  0.6 11.2 %copy-start = (bf16[1,1408,1024]{2,1,0:T(8,128)(2,1)S(1)}, bf16[1,1408,1024]{2,1,0:T(8,128)(2,1)}, u32[]{:S(2)}) copy-start(bf16[1,1408,1024]{2,1,0:T(8,128)(2,1)} %param.18) | copy-start | bytes 8650756
  0.6 17.2 %collective-permute-start = (bf16[128,1024]{1,0:T(8,128)(2,1)}, bf16[128,1024]{1,0:T(8,128)(2,1)S(1)}, u32[]{:S(2)}, u32[]{:S(2)}) collective-permute-start(bf16[128,1024]{1,0:T(8,128)(2,1)} %own_ref.1), channel_id=1, source_target_pairs={{0,2},{2,0},{1,3},{3,1},{4,6},{6,4},{5,7},{7,5}} | collective-permute-start | bytes 786440 | tf_op jit(solution)/shard_map/ppermute | solution.py:285
  4.0 13.9 %collective-permute-start.1 = (bf16[4,3,64,1024]{3,2,1,0:T(8,128)(2,1)}, bf16[4,3,64,1024]{3,2,1,0:T(8,128)(2,1)}, u32[]{:S(2)}, u32[]{:S(2)}) collective-permute-start(bf16[4,3,64,1024]{3,2,1,0:T(8,128)(2,1)} %bitcast.43), channel_id=1, source_target_pairs={{0,1},{1,0},{2,3},{3,2},{4,5},{5,4},{6,7},{7,6}} | collective-permute-start | bytes 4718600 | tf_op jit(solution)/shard_map/ppermute | solution.py:285
  4.0 10.2 %collective-permute-start.2 = (s32[128]{0:T(128)}, s32[128]{0:T(128)S(1)}, u32[]{:S(2)}, u32[]{:S(2)}) collective-permute-start(s32[128]{0:T(128)} %lens_ref.7), channel_id=1, source_target_pairs={{0,2},{2,0},{1,3},{3,1},{4,6},{6,4},{5,7},{7,5}} | collective-permute-start | bytes 1544 | tf_op jit(solution)/shard_map/ppermute | solution.py:285
  4.0 31.5 %collective-permute-start.4 = (bf16[2,704,1024]{2,1,0:T(8,128)(2,1)}, bf16[2,704,1024]{2,1,0:T(8,128)(2,1)}, u32[]{:S(2)}, u32[]{:S(2)}) collective-permute-start(bf16[2,704,1024]{2,1,0:T(8,128)(2,1)} %bitcast.37), channel_id=1, source_target_pairs={{0,1},{1,0},{2,3},{3,2},{4,5},{5,4},{6,7},{7,6}} | collective-permute-start | bytes 8650760 | tf_op jit(solution)/shard_map/ppermute | solution.py:285
  4.5 71.6 %collective-permute-start.8 = (bf16[1024,256]{1,0:T(8,128)(2,1)}, bf16[1024,256]{1,0:T(8,128)(2,1)}, u32[]{:S(2)}, u32[]{:S(2)}) collective-permute-start(bf16[1024,256]{1,0:T(8,128)(2,1)} %bitcast.67), channel_id=1, source_target_pairs={{0,4},{4,0},{1,5},{5,1},{2,6},{6,2},{3,7},{7,3}} | collective-permute-start | bytes 1572872 | tf_op jit(solution)/shard_map/ppermute | solution.py:285
  9.3 3.6 %copy-start.1 = (bf16[1,768,1024]{2,1,0:T(8,128)(2,1)S(1)}, bf16[1,768,1024]{2,1,0:T(8,128)(2,1)}, u32[]{:S(2)}) copy-start(bf16[1,768,1024]{2,1,0:T(8,128)(2,1)} %param.15) | copy-start | bytes 4718596
  11.8 2.3 %copy-start.5 = (s32[128]{0:T(128)S(1)}, s32[128]{0:T(128)}, u32[]{:S(2)}) copy-start(s32[128]{0:T(128)} %lens_ref.7) | copy-start | bytes 1540
  12.9 4.9 %copy-start.3 = (bf16[1,1024]{1,0:T(2,128)(2,1)S(1)}, bf16[1,1024]{1,0:T(2,128)(2,1)}, u32[]{:S(2)}) copy-start(bf16[1,1024]{1,0:T(2,128)(2,1)} %gain_ref.5) | copy-start | bytes 6148
  12.9 4.9 %copy-start.4 = (bf16[1,1024]{1,0:T(2,128)(2,1)S(1)}, bf16[1,1024]{1,0:T(2,128)(2,1)}, u32[]{:S(2)}) copy-start(bf16[1,1024]{1,0:T(2,128)(2,1)} %gain_ref.9) | copy-start | bytes 6148
  12.9 5.0 %copy-start.7 = (bf16[128,1024]{1,0:T(8,128)(2,1)S(1)}, bf16[128,1024]{1,0:T(8,128)(2,1)}, u32[]{:S(2)}) copy-start(bf16[128,1024]{1,0:T(8,128)(2,1)} %own_ref.1) | copy-start | bytes 786436
  14.2 3.6 %collective-permute-start.19 = (bf16[2,1024]{1,0:T(2,128)(2,1)S(1)}, bf16[2,1024]{1,0:T(2,128)(2,1)S(1)}, u32[]{:S(2)}, u32[]{:S(2)}) collective-permute-start(bf16[2,1024]{1,0:T(2,128)(2,1)S(1)} %pad_maximum_fusion.6), channel_id=1, source_target_pairs={{0,2},{2,0},{1,3},{3,1},{4,6},{6,4},{5,7},{7,5}} | collective-permute-start | bytes 12296 | tf_op jit(solution)/shard_map/ppermute | solution.py:285
  17.8 83.5 %collective-permute-start.15 = (bf16[704,1024]{1,0:T(8,128)(2,1)}, bf16[704,1024]{1,0:T(8,128)(2,1)S(1)}, u32[]{:S(2)}, u32[]{:S(2)}) collective-permute-start(bf16[704,1024]{1,0:T(8,128)(2,1)} %bitcast.46), channel_id=1, source_target_pairs={{0,1},{1,0},{2,3},{3,2},{4,5},{5,4},{6,7},{7,6}} | collective-permute-start | bytes 4325384 | tf_op jit(solution)/shard_map/ppermute | solution.py:285
  17.9 1.4 copy-start.2
  21.9 11.6 %copy-start.14 = (bf16[1,1024,256]{2,1,0:T(8,128)(2,1)S(1)}, bf16[1,1024,256]{2,1,0:T(8,128)(2,1)}, u32[]{:S(2)}) copy-start(bf16[1,1024,256]{2,1,0:T(8,128)(2,1)} %param.16) | copy-start | bytes 1572868
  21.9 13.1 %copy-start.10 = (bf16[1,384,1024]{2,1,0:T(8,128)(2,1)S(1)}, bf16[1,384,1024]{2,1,0:T(8,128)(2,1)}, u32[]{:S(2)}) copy-start(bf16[1,384,1024]{2,1,0:T(8,128)(2,1)} %get-tuple-element.107) | copy-start | bytes 2359300
  21.9 11.5 %collective-permute-start.3 = (bf16[3,512,128]{2,1,0:T(8,128)(2,1)S(1)}, bf16[3,512,128]{2,1,0:T(8,128)(2,1)S(1)}, u32[]{:S(2)}, u32[]{:S(2)}) collective-permute-start(bf16[3,512,128]{2,1,0:T(8,128)(2,1)S(1)} %get-tuple-element.56), channel_id=1, source_target_pairs={{0,2},{2,0},{1,3},{3,1},{4,6},{6,4},{5,7},{7,5}} | collective-permute-start | bytes 1179656 | tf_op jit(solution)/shard_map/ppermute | solution.py:285
  33.5 21.6 %collective-permute-start.6 = (bf16[1024,256]{1,0:T(8,128)(2,1)S(1)}, bf16[1024,256]{1,0:T(8,128)(2,1)S(1)}, u32[]{:S(2)}, u32[]{:S(2)}) collective-permute-start(bf16[1024,256]{1,0:T(8,128)(2,1)S(1)} %bitcast.68), channel_id=1, source_target_pairs={{0,2},{2,0},{1,3},{3,1},{4,6},{6,4},{5,7},{7,5}} | collective-permute-start | bytes 1572872 | tf_op jit(solution)/shard_map/ppermute | solution.py:285
  35.0 35.0 %collective-permute-start.21 = (bf16[2,3,64,1024]{3,2,1,0:T(8,128)(2,1)S(1)}, bf16[2,3,64,1024]{3,2,1,0:T(8,128)(2,1)S(1)}, u32[]{:S(2)}, u32[]{:S(2)}) collective-permute-start(bf16[2,3,64,1024]{3,2,1,0:T(8,128)(2,1)S(1)} %bitcast.66), channel_id=1, source_target_pairs={{0,2},{2,0},{1,3},{3,1},{4,6},{6,4},{5,7},{7,5}} | collective-permute-start | bytes 2359304 | tf_op jit(solution)/shard_map/ppermute | solution.py:285
  55.1 23.4 %collective-permute-start.10 = (bf16[1024,256]{1,0:T(8,128)(2,1)S(1)}, bf16[1024,256]{1,0:T(8,128)(2,1)S(1)}, u32[]{:S(2)}, u32[]{:S(2)}) collective-permute-start(bf16[1024,256]{1,0:T(8,128)(2,1)S(1)} %collective-permute-done.6), channel_id=1, source_target_pairs={{0,1},{1,0},{2,3},{3,2},{4,5},{5,4},{6,7},{7,6}} | collective-permute-start | bytes 1572872 | tf_op jit(solution)/shard_map/ppermute | solution.py:285
  55.1 20.9 %collective-permute-start.11 = (bf16[1024,256]{1,0:T(8,128)(2,1)S(1)}, bf16[1024,256]{1,0:T(8,128)(2,1)S(1)}, u32[]{:S(2)}, u32[]{:S(2)}) collective-permute-start(bf16[1024,256]{1,0:T(8,128)(2,1)S(1)} %collective-permute-done.6), channel_id=1, source_target_pairs={{0,4},{4,0},{1,5},{5,1},{2,6},{6,2},{3,7},{7,3}} | collective-permute-start | bytes 1572872 | tf_op jit(solution)/shard_map/ppermute | solution.py:285
  55.4 23.1 %copy-start.9 = (bf16[1,384,1024]{2,1,0:T(8,128)(2,1)S(1)}, bf16[1,384,1024]{2,1,0:T(8,128)(2,1)}, u32[]{:S(2)}) copy-start(bf16[1,384,1024]{2,1,0:T(8,128)(2,1)} %get-tuple-element.108) | copy-start | bytes 2359300
  69.9 4.3 %collective-permute-start.24 = (bf16[64,512]{1,0:T(8,128)(2,1)S(1)}, bf16[64,512]{1,0:T(8,128)(2,1)S(1)}, u32[]{:S(2)}, u32[]{:S(2)}) collective-permute-start(bf16[64,512]{1,0:T(8,128)(2,1)S(1)} %get-tuple-element.64), channel_id=1, source_target_pairs={{0,4},{4,0},{1,5},{5,1},{2,6},{6,2},{3,7},{7,3}} | collective-permute-start | bytes 196616 | tf_op jit(solution)/shard_map/ppermute | solution.py:285
  74.2 4.3 %collective-permute-start.5 = (bf16[64,512]{1,0:T(8,128)(2,1)S(1)}, bf16[64,512]{1,0:T(8,128)(2,1)S(1)}, u32[]{:S(2)}, u32[]{:S(2)}) collective-permute-start(bf16[64,512]{1,0:T(8,128)(2,1)S(1)} %get-tuple-element.58), channel_id=1, source_target_pairs={{0,4},{4,0},{1,5},{5,1},{2,6},{6,2},{3,7},{7,3}} | collective-permute-start | bytes 196616 | tf_op jit(solution)/shard_map/ppermute | solution.py:285
  76.0 4.4 %collective-permute-start.12 = (bf16[1024,256]{1,0:T(8,128)(2,1)S(1)}, bf16[1024,256]{1,0:T(8,128)(2,1)S(1)}, u32[]{:S(2)}, u32[]{:S(2)}) collective-permute-start(bf16[1024,256]{1,0:T(8,128)(2,1)S(1)} %collective-permute-done.11), channel_id=1, source_target_pairs={{0,1},{1,0},{2,3},{3,2},{4,5},{5,4},{6,7},{7,6}} | collective-permute-start | bytes 1572872 | tf_op jit(solution)/shard_map/ppermute | solution.py:285
  76.1 4.7 %collective-permute-start.7 = (bf16[1024,256]{1,0:T(8,128)(2,1)S(1)}, bf16[1024,256]{1,0:T(8,128)(2,1)S(1)}, u32[]{:S(2)}, u32[]{:S(2)}) collective-permute-start(bf16[1024,256]{1,0:T(8,128)(2,1)S(1)} %bitcast.69), channel_id=1, source_target_pairs={{0,1},{1,0},{2,3},{3,2},{4,5},{5,4},{6,7},{7,6}} | collective-permute-start | bytes 1572872 | tf_op jit(solution)/shard_map/ppermute | solution.py:285
  78.5 2.3 collective-permute-start.9
  78.5 20.4 %collective-permute-start.14 = (bf16[2,3,64,1024]{3,2,1,0:T(8,128)(2,1)S(1)}, bf16[2,3,64,1024]{3,2,1,0:T(8,128)(2,1)S(1)}, u32[]{:S(2)}, u32[]{:S(2)}) collective-permute-start(bf16[2,3,64,1024]{3,2,1,0:T(8,128)(2,1)S(1)} %bitcast.65), channel_id=1, source_target_pairs={{0,2},{2,0},{1,3},{3,1},{4,6},{6,4},{5,7},{7,5}} | collective-permute-start | bytes 2359304 | tf_op jit(solution)/shard_map/ppermute | solution.py:285
  80.4 36.2 %collective-permute-start.22 = (bf16[2,3,64,1024]{3,2,1,0:T(8,128)(2,1)S(1)}, bf16[2,3,64,1024]{3,2,1,0:T(8,128)(2,1)S(1)}, u32[]{:S(2)}, u32[]{:S(2)}) collective-permute-start(bf16[2,3,64,1024]{3,2,1,0:T(8,128)(2,1)S(1)} %collective-permute-done.21.refs_0_), channel_id=1, source_target_pairs={{0,1},{1,0},{2,3},{3,2},{4,5},{5,4},{6,7},{7,6}} | collective-permute-start | bytes 2359304 | tf_op jit(solution)/shard_map/ppermute | solution.py:285
  80.8 20.5 %copy-start.6 = (bf16[1,1024,704]{1,2,0:T(8,128)(2,1)S(1)}, bf16[1,1024,704]{1,2,0:T(8,128)(2,1)}, u32[]{:S(2)}) copy-start(bf16[1,1024,704]{1,2,0:T(8,128)(2,1)} %param.19) | copy-start | bytes 4325380
  82.7 18.6 %collective-permute-start.13 = (bf16[64,1024]{1,0:T(8,128)(2,1)S(1)}, bf16[64,1024]{1,0:T(8,128)(2,1)S(1)}, u32[]{:S(2)}, u32[]{:S(2)}) collective-permute-start(bf16[64,1024]{1,0:T(8,128)(2,1)S(1)} %fusion.hid_ref), channel_id=1, source_target_pairs={{0,2},{2,0},{1,3},{3,1},{4,6},{6,4},{5,7},{7,5}} | collective-permute-start | bytes 393224 | tf_op jit(solution)/shard_map/ppermute | solution.py:285
  107.0 7.9 %collective-permute-start.16 = (f32[64,1024]{1,0:T(8,128)S(1)}, f32[64,1024]{1,0:T(8,128)S(1)}, u32[]{:S(2)}, u32[]{:S(2)}) collective-permute-start(f32[64,1024]{1,0:T(8,128)S(1)} %get-tuple-element.71), channel_id=1, source_target_pairs={{0,4},{4,0},{1,5},{5,1},{2,6},{6,2},{3,7},{7,3}} | collective-permute-start | bytes 786440 | tf_op jit(solution)/shard_map/ppermute | solution.py:285
  110.6 8.0 %collective-permute-start.25 = (bf16[64,1024]{1,0:T(8,128)(2,1)S(1)}, bf16[64,1024]{1,0:T(8,128)(2,1)S(1)}, u32[]{:S(2)}, u32[]{:S(2)}) collective-permute-start(bf16[64,1024]{1,0:T(8,128)(2,1)S(1)} %fusion.1.hid_ref), channel_id=1, source_target_pairs={{0,2},{2,0},{1,3},{3,1},{4,6},{6,4},{5,7},{7,5}} | collective-permute-start | bytes 393224 | tf_op jit(solution)/shard_map/ppermute | solution.py:285
  115.0 4.3 %collective-permute-start.17 = (bf16[32,1024]{1,0:T(8,128)(2,1)S(1)}, bf16[32,1024]{1,0:T(8,128)(2,1)S(1)}, u32[]{:S(2)}, u32[]{:S(2)}) collective-permute-start(bf16[32,1024]{1,0:T(8,128)(2,1)S(1)} %slice.158), channel_id=1, source_target_pairs={{0,2},{2,0},{1,3},{3,1},{4,6},{6,4},{5,7},{7,5}} | collective-permute-start | bytes 196616 | tf_op jit(solution)/shard_map/ppermute | solution.py:285
  118.6 10.1 %collective-permute-start.20 = (bf16[2,3,64,1024]{3,2,1,0:T(8,128)(2,1)S(1)}, bf16[2,3,64,1024]{3,2,1,0:T(8,128)(2,1)S(1)}, u32[]{:S(2)}, u32[]{:S(2)}) collective-permute-start(bf16[2,3,64,1024]{3,2,1,0:T(8,128)(2,1)S(1)} %collective-permute-done.14.refs_0_), channel_id=1, source_target_pairs={{0,1},{1,0},{2,3},{3,2},{4,5},{5,4},{6,7},{7,6}} | collective-permute-start | bytes 2359304 | tf_op jit(solution)/shard_map/ppermute | solution.py:285
  119.3 7.7 %copy-start.13 = (bf16[272,1024]{1,0:T(8,128)(2,1)S(1)}, bf16[272,1024]{1,0:T(8,128)(2,1)}, u32[]{:S(2)}) copy-start(bf16[272,1024]{1,0:T(8,128)(2,1)} %get-tuple-element.99) | copy-start | bytes 1671172
  119.3 9.4 %collective-permute-start.18 = (bf16[32,1024]{1,0:T(8,128)(2,1)S(1)}, bf16[32,1024]{1,0:T(8,128)(2,1)S(1)}, u32[]{:S(2)}, u32[]{:S(2)}) collective-permute-start(bf16[32,1024]{1,0:T(8,128)(2,1)S(1)} %slice_select_fusion.3), channel_id=1, source_target_pairs={{0,4},{4,0},{1,5},{5,1},{2,6},{6,2},{3,7},{7,3}} | collective-permute-start | bytes 196616 | tf_op jit(solution)/shard_map/ppermute | solution.py:285
  126.7 7.6 %collective-permute-start.26 = (f32[64,1024]{1,0:T(8,128)S(1)}, f32[64,1024]{1,0:T(8,128)S(1)}, u32[]{:S(2)}, u32[]{:S(2)}) collective-permute-start(f32[64,1024]{1,0:T(8,128)S(1)} %get-tuple-element.82), channel_id=1, source_target_pairs={{0,4},{4,0},{1,5},{5,1},{2,6},{6,2},{3,7},{7,3}} | collective-permute-start | bytes 786440 | tf_op jit(solution)/shard_map/ppermute | solution.py:285
  127.0 14.6 %collective-permute-start.39 = (bf16[272,1024]{1,0:T(8,128)(2,1)S(1)}, bf16[272,1024]{1,0:T(8,128)(2,1)S(1)}, u32[]{:S(2)}, u32[]{:S(2)}) collective-permute-start(bf16[272,1024]{1,0:T(8,128)(2,1)S(1)} %copy-done.13), channel_id=1, source_target_pairs={{0,2},{2,0},{1,3},{3,1},{4,6},{6,4},{5,7},{7,5}} | collective-permute-start | bytes 1671176 | tf_op jit(solution)/shard_map/ppermute | solution.py:285
  128.7 13.5 %copy-start.8 = (bf16[512,1024]{1,0:T(8,128)(2,1)S(1)}, bf16[512,1024]{1,0:T(8,128)(2,1)}, u32[]{:S(2)}) copy-start(bf16[512,1024]{1,0:T(8,128)(2,1)} %slice_bitcast_fusion) | copy-start | bytes 3145732
  134.4 7.9 %collective-permute-start.27 = (bf16[32,1024]{1,0:T(8,128)(2,1)S(1)}, bf16[32,1024]{1,0:T(8,128)(2,1)S(1)}, u32[]{:S(2)}, u32[]{:S(2)}) collective-permute-start(bf16[32,1024]{1,0:T(8,128)(2,1)S(1)} %slice.163), channel_id=1, source_target_pairs={{0,2},{2,0},{1,3},{3,1},{4,6},{6,4},{5,7},{7,5}} | collective-permute-start | bytes 196616 | tf_op jit(solution)/shard_map/ppermute | solution.py:285
  141.6 23.8 %collective-permute-start.40 = (bf16[272,1024]{1,0:T(8,128)(2,1)S(1)}, bf16[272,1024]{1,0:T(8,128)(2,1)S(1)}, u32[]{:S(2)}, u32[]{:S(2)}) collective-permute-start(bf16[272,1024]{1,0:T(8,128)(2,1)S(1)} %collective-permute-done.39.refs_0_), channel_id=1, source_target_pairs={{0,1},{1,0},{2,3},{3,2},{4,5},{5,4},{6,7},{7,6}} | collective-permute-start | bytes 1671176 | tf_op jit(solution)/shard_map/ppermute | solution.py:285
  142.3 26.0 %collective-permute-start.29 = (bf16[512,1024]{1,0:T(8,128)(2,1)S(1)}, bf16[512,1024]{1,0:T(8,128)(2,1)S(1)}, u32[]{:S(2)}, u32[]{:S(2)}) collective-permute-start(bf16[512,1024]{1,0:T(8,128)(2,1)S(1)} %copy-done.8), channel_id=1, source_target_pairs={{0,2},{2,0},{1,3},{3,1},{4,6},{6,4},{5,7},{7,5}} | collective-permute-start | bytes 3145736 | tf_op jit(solution)/shard_map/ppermute | solution.py:285
  142.6 18.7 %copy-start.11 = (bf16[352,1024]{1,0:T(8,128)(2,1)S(1)}, bf16[352,1024]{1,0:T(8,128)(2,1)}, u32[]{:S(2)}) copy-start(bf16[352,1024]{1,0:T(8,128)(2,1)} %slice_bitcast_fusion.1) | copy-start | bytes 2162692
  159.3 27.1 %collective-permute-start.23 = (bf16[64,512]{1,0:T(8,128)(2,1)S(1)}, bf16[64,512]{1,0:T(8,128)(2,1)S(1)}, u32[]{:S(2)}, u32[]{:S(2)}) collective-permute-start(bf16[64,512]{1,0:T(8,128)(2,1)S(1)} %get-tuple-element.76), channel_id=1, source_target_pairs={{0,4},{4,0},{1,5},{5,1},{2,6},{6,2},{3,7},{7,3}} | collective-permute-start | bytes 196616 | tf_op jit(solution)/shard_map/ppermute | solution.py:285
  161.0 4.3 %collective-permute-start.28 = (bf16[32,1024]{1,0:T(8,128)(2,1)S(1)}, bf16[32,1024]{1,0:T(8,128)(2,1)S(1)}, u32[]{:S(2)}, u32[]{:S(2)}) collective-permute-start(bf16[32,1024]{1,0:T(8,128)(2,1)S(1)} %slice_select_fusion.2), channel_id=1, source_target_pairs={{0,4},{4,0},{1,5},{5,1},{2,6},{6,2},{3,7},{7,3}} | collective-permute-start | bytes 196616 | tf_op jit(solution)/shard_map/ppermute | solution.py:285
  161.4 27.4 %collective-permute-start.36 = (bf16[352,1024]{1,0:T(8,128)(2,1)S(1)}, bf16[352,1024]{1,0:T(8,128)(2,1)S(1)}, u32[]{:S(2)}, u32[]{:S(2)}) collective-permute-start(bf16[352,1024]{1,0:T(8,128)(2,1)S(1)} %copy-done.11), channel_id=1, source_target_pairs={{0,2},{2,0},{1,3},{3,1},{4,6},{6,4},{5,7},{7,5}} | collective-permute-start | bytes 2162696 | tf_op jit(solution)/shard_map/ppermute | solution.py:285
  184.8 4.3 %collective-permute-start.34 = (bf16[64,512]{1,0:T(8,128)(2,1)S(1)}, bf16[64,512]{1,0:T(8,128)(2,1)S(1)}, u32[]{:S(2)}, u32[]{:S(2)}) collective-permute-start(bf16[64,512]{1,0:T(8,128)(2,1)S(1)} %get-tuple-element.88), channel_id=1, source_target_pairs={{0,4},{4,0},{1,5},{5,1},{2,6},{6,2},{3,7},{7,3}} | collective-permute-start | bytes 196616 | tf_op jit(solution)/shard_map/ppermute | solution.py:285
  186.3 23.7 %collective-permute-start.38 = (bf16[512,1024]{1,0:T(8,128)(2,1)S(1)}, bf16[512,1024]{1,0:T(8,128)(2,1)S(1)}, u32[]{:S(2)}, u32[]{:S(2)}) collective-permute-start(bf16[512,1024]{1,0:T(8,128)(2,1)S(1)} %collective-permute-done.29.refs_0_), channel_id=1, source_target_pairs={{0,1},{1,0},{2,3},{3,2},{4,5},{5,4},{6,7},{7,6}} | collective-permute-start | bytes 3145736 | tf_op jit(solution)/shard_map/ppermute | solution.py:285
  188.2 6.3 %collective-permute-start.30 = (bf16[64,1024]{1,0:T(8,128)(2,1)S(1)}, bf16[64,1024]{1,0:T(8,128)(2,1)S(1)}, u32[]{:S(2)}, u32[]{:S(2)}) collective-permute-start(bf16[64,1024]{1,0:T(8,128)(2,1)S(1)} %fusion.2.hid_ref), channel_id=1, source_target_pairs={{0,2},{2,0},{1,3},{3,1},{4,6},{6,4},{5,7},{7,5}} | collective-permute-start | bytes 393224 | tf_op jit(solution)/shard_map/ppermute | solution.py:285
  188.8 24.0 %collective-permute-start.37 = (bf16[352,1024]{1,0:T(8,128)(2,1)S(1)}, bf16[352,1024]{1,0:T(8,128)(2,1)S(1)}, u32[]{:S(2)}, u32[]{:S(2)}) collective-permute-start(bf16[352,1024]{1,0:T(8,128)(2,1)S(1)} %collective-permute-done.36.refs_0_), channel_id=1, source_target_pairs={{0,1},{1,0},{2,3},{3,2},{4,5},{5,4},{6,7},{7,6}} | collective-permute-start | bytes 2162696 | tf_op jit(solution)/shard_map/ppermute | solution.py:285
  190.9 9.9 %collective-permute-start.35 = (bf16[64,1024]{1,0:T(8,128)(2,1)S(1)}, bf16[64,1024]{1,0:T(8,128)(2,1)S(1)}, u32[]{:S(2)}, u32[]{:S(2)}) collective-permute-start(bf16[64,1024]{1,0:T(8,128)(2,1)S(1)} %fusion.3.hid_ref), channel_id=1, source_target_pairs={{0,2},{2,0},{1,3},{3,1},{4,6},{6,4},{5,7},{7,5}} | collective-permute-start | bytes 393224 | tf_op jit(solution)/shard_map/ppermute | solution.py:285
  200.2 7.8 %copy-start.12 = (bf16[272,1024]{1,0:T(8,128)(2,1)S(1)}, bf16[272,1024]{1,0:T(8,128)(2,1)}, u32[]{:S(2)}) copy-start(bf16[272,1024]{1,0:T(8,128)(2,1)} %get-tuple-element.104) | copy-start | bytes 1671172
  200.2 7.9 %collective-permute-start.31 = (f32[64,1024]{1,0:T(8,128)S(1)}, f32[64,1024]{1,0:T(8,128)S(1)}, u32[]{:S(2)}, u32[]{:S(2)}) collective-permute-start(f32[64,1024]{1,0:T(8,128)S(1)} %get-tuple-element.92), channel_id=1, source_target_pairs={{0,4},{4,0},{1,5},{5,1},{2,6},{6,2},{3,7},{7,3}} | collective-permute-start | bytes 786440 | tf_op jit(solution)/shard_map/ppermute | solution.py:285
  206.5 8.5 %collective-permute-start.41 = (f32[64,1024]{1,0:T(8,128)S(1)}, f32[64,1024]{1,0:T(8,128)S(1)}, u32[]{:S(2)}, u32[]{:S(2)}) collective-permute-start(f32[64,1024]{1,0:T(8,128)S(1)} %get-tuple-element.101), channel_id=1, source_target_pairs={{0,4},{4,0},{1,5},{5,1},{2,6},{6,2},{3,7},{7,3}} | collective-permute-start | bytes 786440 | tf_op jit(solution)/shard_map/ppermute | solution.py:285
  207.9 15.9 %collective-permute-start.44 = (bf16[272,1024]{1,0:T(8,128)(2,1)S(1)}, bf16[272,1024]{1,0:T(8,128)(2,1)S(1)}, u32[]{:S(2)}, u32[]{:S(2)}) collective-permute-start(bf16[272,1024]{1,0:T(8,128)(2,1)S(1)} %copy-done.12), channel_id=1, source_target_pairs={{0,2},{2,0},{1,3},{3,1},{4,6},{6,4},{5,7},{7,5}} | collective-permute-start | bytes 1671176 | tf_op jit(solution)/shard_map/ppermute | solution.py:285
  208.1 15.1 %collective-permute-start.32 = (bf16[32,1024]{1,0:T(8,128)(2,1)S(1)}, bf16[32,1024]{1,0:T(8,128)(2,1)S(1)}, u32[]{:S(2)}, u32[]{:S(2)}) collective-permute-start(bf16[32,1024]{1,0:T(8,128)(2,1)S(1)} %slice.165), channel_id=1, source_target_pairs={{0,2},{2,0},{1,3},{3,1},{4,6},{6,4},{5,7},{7,5}} | collective-permute-start | bytes 196616 | tf_op jit(solution)/shard_map/ppermute | solution.py:285
  215.1 8.8 %collective-permute-start.42 = (bf16[32,1024]{1,0:T(8,128)(2,1)S(1)}, bf16[32,1024]{1,0:T(8,128)(2,1)S(1)}, u32[]{:S(2)}, u32[]{:S(2)}) collective-permute-start(bf16[32,1024]{1,0:T(8,128)(2,1)S(1)} %slice.167), channel_id=1, source_target_pairs={{0,2},{2,0},{1,3},{3,1},{4,6},{6,4},{5,7},{7,5}} | collective-permute-start | bytes 196616 | tf_op jit(solution)/shard_map/ppermute | solution.py:285
  223.2 4.9 %collective-permute-start.33 = (bf16[32,1024]{1,0:T(8,128)(2,1)S(1)}, bf16[32,1024]{1,0:T(8,128)(2,1)S(1)}, u32[]{:S(2)}, u32[]{:S(2)}) collective-permute-start(bf16[32,1024]{1,0:T(8,128)(2,1)S(1)} %slice_select_fusion.1), channel_id=1, source_target_pairs={{0,4},{4,0},{1,5},{5,1},{2,6},{6,2},{3,7},{7,3}} | collective-permute-start | bytes 196616 | tf_op jit(solution)/shard_map/ppermute | solution.py:285
  223.8 5.9 %collective-permute-start.45 = (bf16[272,1024]{1,0:T(8,128)(2,1)S(1)}, bf16[272,1024]{1,0:T(8,128)(2,1)S(1)}, u32[]{:S(2)}, u32[]{:S(2)}) collective-permute-start(bf16[272,1024]{1,0:T(8,128)(2,1)S(1)} %collective-permute-done.44.refs_0_), channel_id=1, source_target_pairs={{0,1},{1,0},{2,3},{3,2},{4,5},{5,4},{6,7},{7,6}} | collective-permute-start | bytes 1671176 | tf_op jit(solution)/shard_map/ppermute | solution.py:285
  223.9 5.0 %collective-permute-start.43 = (bf16[32,1024]{1,0:T(8,128)(2,1)S(1)}, bf16[32,1024]{1,0:T(8,128)(2,1)S(1)}, u32[]{:S(2)}, u32[]{:S(2)}) collective-permute-start(bf16[32,1024]{1,0:T(8,128)(2,1)S(1)} %slice_select_fusion), channel_id=1, source_target_pairs={{0,4},{4,0},{1,5},{5,1},{2,6},{6,2},{3,7},{7,3}} | collective-permute-start | bytes 196616 | tf_op jit(solution)/shard_map/ppermute | solution.py:285
where the time goes:
time: 232 us
  Pallas kernels  108 us (47%)
  waiting for transfers between devices  61.6 us (27%)
  starting transfers between devices  42.1 us (18%)
  local copies, waits for them, and re-layouts  8.59 us (4%)
  matrix products  7.42 us (3%)
  other arithmetic  2.4 us (1%)
    pallas_call x4, Pallas kernels, attention(): pl.pallas_call(functools.partial(attn_kernel, heads=heads, head_dim=head_...  62.1 us
    ppermute x46, waiting for transfers between devices, swap(): return lax.ppermute(x, axis, SWAP)  61.6 us
    ppermute x46, starting transfers between devices, swap(): return lax.ppermute(x, axis, SWAP)  42.1 us
    pallas_call x4, Pallas kernels, mlp(): pl.pallas_call(mlp_kernel, in_specs=[pl.BlockSpec(memory_space=pltpu.SMEM...  22.6 us
    pallas_call x8, Pallas kernels, place(): pl.pallas_call(functools.partial(place_kernel, count=count, blocks=blocks...  20.8 us
    dot_general x4, matrix products, decode(): jnp.einsum('bk,dk->bd', o_all, layer_o[layer], preferred_element_type=F32)  7.42 us
    squeeze x3, local copies, waits for them, and re-layouts, gu_send(): return swap(after(w_gate_up[0, cuts[c]:cuts[c + 1]], *deps), 'pp')  5.59 us
  transfers between devices with their start and end apart: 46, of which 19 were waited for; matrix products, arithmetic and copies ran while one was open for 7% of the time, Pallas kernels for 46%

commit v1 on v0

--- a/solution.py
+++ b/solution.py
@@ -106,26 +106,17 @@
     )(half, own, away, gain, w_own, w_near, cos_t, sin_t)
 
 
-def mlp_kernel(rank_ref, hid_ref, away_ref, gain_ref, gu_a, gu_b, dn_a, dn_b, keep_ref, give_ref, base_ref,
-               gu_s, dn_s, total, sems):
+def mlp_kernel(rank_ref, hid_ref, away_ref, gain_ref, gu_a, gu_b, dn_a, dn_b, keep_ref, give_ref, base_ref, total):
     count = hid_ref.shape[0]
     mid = count // 2
-    copies = []
-    for p, (gu, dn) in enumerate(((gu_a, dn_a), (gu_b, dn_b))):
-        for t, (src, dst) in enumerate(((gu.at[0], gu_s.at[p, 0]), (gu.at[1], gu_s.at[p, 1]), (dn, dn_s.at[p]))):
-            copies.append(pltpu.make_async_copy(src, dst, sems.at[3 * p + t]))
-            copies[-1].start()
     normed = rms_norm(jnp.concatenate([hid_ref[...], away_ref[...]], axis=0), gain_ref[...])
     nt = (((1,), (1,)), ((), ()))
-    for p in range(2):
-        copies[3 * p].wait()
-        gate = lax.dot_general(gu_s[p, 0], normed, nt, preferred_element_type=F32)
-        copies[3 * p + 1].wait()
-        up = lax.dot_general(gu_s[p, 1], normed, nt, preferred_element_type=F32)
+    for gu, dn in ((gu_a, dn_a), (gu_b, dn_b)):
+        gate = lax.dot_general(gu[0], normed, nt, preferred_element_type=F32)
+        up = lax.dot_general(gu[1], normed, nt, preferred_element_type=F32)
         act = (jax.nn.silu(gate) * up).T.astype(BF16)
-        copies[3 * p + 2].wait()
-        part = jnp.dot(act, dn_s[p], preferred_element_type=F32)
-        total[...] = part if p == 0 else total[...] + part
+        part = jnp.dot(act, dn[...], preferred_element_type=F32)
+        total[...] = part if dn is dn_a else total[...] + part
     rank = rank_ref[0]
     mine = pl.multiple_of(rank * mid, mid)
     peer = pl.multiple_of((1 - rank) * mid, mid)
@@ -138,24 +129,26 @@
 def mlp(rank, hid, away, gain, gus, downs):
     count, model = hid.shape
     ffn = downs[0].shape[0]
-    vmem, hbm = pl.BlockSpec(memory_space=pltpu.VMEM), pl.BlockSpec(memory_space=pl.ANY)
+    vmem = pl.BlockSpec(memory_space=pltpu.VMEM)
     half_f32 = jax.ShapeDtypeStruct((count, model), F32)
     return pl.pallas_call(
         mlp_kernel,
-        in_specs=[pl.BlockSpec(memory_space=pltpu.SMEM)] + [vmem] * 3 + [hbm] * 4,
+        in_specs=[pl.BlockSpec(memory_space=pltpu.SMEM)] + [vmem] * 7,
         out_specs=[vmem] * 3,
         out_shape=[half_f32, half_f32, jax.ShapeDtypeStruct((count, model), BF16)],
-        scratch_shapes=[pltpu.VMEM((2, 2, ffn, model), BF16), pltpu.VMEM((2, ffn, model), BF16),
-                        pltpu.VMEM((2 * count, model), F32), pltpu.SemaphoreType.DMA((6,))],
+        scratch_shapes=[pltpu.VMEM((2 * count, model), F32)],
         compiler_params=pltpu.CompilerParams(vmem_limit_bytes=32 << 20),
         cost_estimate=pl.CostEstimate(flops=4_000_000_000, bytes_accessed=6 * ffn * model * 2, transcendentals=0),
         name="mlp",
     )(rank, hid, away, gain, *gus, *downs)
 
 
-def attn_kernel(lens_ref, *rest, heads, head_dim, scale, row0, ready):
+def attn_kernel(lens_ref, *rest, heads, head_dim, scale, row0, ready, layer):
     heads_in, rest = rest[:1 if ready else 5], rest[1 if ready else 5:]
     k_ref, v_ref = rest[:2]
+    if not ready:
+        w_s, w_sem = rest[-2:]
+        rest = rest[:-2]
     o_ref, ko_ref, vo_ref, q_s, kt_s, vt_s, o_s, p_s = rest[-8:]
     rows = heads * head_dim
     per = k_ref.shape[1]
@@ -174,11 +167,15 @@
                     q_s[...] = vals.T
             return
         h_ref, gain_ref, w_ref, cos_ref, sin_ref = heads_in
+        fetch = pltpu.make_async_copy(w_ref.at[layer], w_s, w_sem)
+        fetch.start()
         normed = rms_norm(h_ref[...], gain_ref[...])
         normed = jnp.concatenate([normed] * (batch // h_ref.shape[0]), axis=0)
 
+        fetch.wait()
+
         def proj(t, turn):
-            vals = lax.dot_general(w_ref[0, t * rows:(t + 1) * rows, :], normed, (((1,), (1,)), ((), ())),
+            vals = lax.dot_general(w_s[t * rows:(t + 1) * rows, :], normed, (((1,), (1,)), ((), ())),
                                    preferred_element_type=F32)
             if turn:
                 vals = rope_t(vals.reshape(heads, head_dim, batch), cos_ref[...], sin_ref[...])
@@ -237,7 +234,7 @@
         in_specs = [whole(3, rows, seq)]
     else:
         model = heads_in[0].shape[1]
-        in_specs = [whole(count, model), whole(1, model), pl.BlockSpec((1, 3 * rows, model), lambda s, n: (layer, 0, 0)),
+        in_specs = [whole(count, model), whole(1, model), pl.BlockSpec(memory_space=pltpu.HBM),
                     whole(head_dim // 2, seq), whole(head_dim // 2, seq)]
     in_specs += [cache_block, cache_block]
     args = [seq_lens, *heads_in, kc, vc]
@@ -249,16 +246,17 @@
     cache_shape = jax.ShapeDtypeStruct(kc.shape, kc.dtype)
     return pl.pallas_call(
         functools.partial(attn_kernel, heads=heads, head_dim=head_dim, scale=head_dim ** -0.5, row0=part * count,
-                          ready=ready),
+                          ready=ready, layer=layer),
         grid_spec=pltpu.PrefetchScalarGridSpec(
             num_scalar_prefetch=1, grid=(count // per,), in_specs=in_specs,
             out_specs=[pl.BlockSpec((per, rows), lambda s, n: (s, 0)), cache_block, cache_block],
             scratch_shapes=[pltpu.VMEM((seq, rows), F32), pltpu.VMEM((rows, seq), F32),
                             pltpu.VMEM((rows, seq), F32), pltpu.VMEM((per, rows), F32),
-                            pltpu.VMEM((per * heads, seq), F32)]),
+                            pltpu.VMEM((per * heads, seq), F32)] + ([] if ready else [
+                                pltpu.VMEM((3 * rows, heads_in[0].shape[1]), BF16), pltpu.SemaphoreType.DMA])),
         out_shape=[jax.ShapeDtypeStruct((count, rows), BF16), cache_shape, cache_shape],
         input_output_aliases=aliases,
-        compiler_params=pltpu.CompilerParams(dimension_semantics=("arbitrary",), vmem_limit_bytes=48 << 20),
+        compiler_params=pltpu.CompilerParams(dimension_semantics=("arbitrary",), vmem_limit_bytes=28 << 20),
         cost_estimate=pl.CostEstimate(flops=30_000_000_000 // parts, bytes_accessed=kc.size * 4 // parts,
                                       transcendentals=0),
     )(*args)
@@ -334,24 +332,26 @@
 
         def qkv_send(i, *deps):
             many = groups // 2
-            return swap(after(shard_qkv[i * many:(i + 1) * many], *deps), "pp")
+            return swap(after(late_qkv[i * many:(i + 1) * many], *deps), "pp")
 
         def qkv_take(i, piece, dst):
             many = groups // 2
             near = swap(piece, "grp")
             return place([piece, near], spots[2:], dst, qkv_shape, qkv_blocks(2, i * many, many))
 
+        late_gu = after(w_gate_up[0], heads_own)
+        late_qkv = after(shard_qkv, heads_own)
         cuts = [0, GU_CUTS[0] * ffn // 44, GU_CUTS[1] * ffn // 44, GU_CUTS[2] * ffn // 44, 2 * ffn]
 
         def gu_send(c, *deps):
-            return swap(after(w_gate_up[0, cuts[c]:cuts[c + 1]], *deps), "pp")
+            return swap(after(late_gu[cuts[c]:cuts[c + 1]], *deps), "pp")
 
         def gu_take(c, piece, dst):
             near = swap(piece, "grp")
             return place([piece, near], spots[2:], dst, gu_shape, gu_blocks(2, cuts[c], cuts[c + 1]))
 
+        flat_gu = lambda x: x.reshape(2 * ffn, model)
         gen_qkv = place([shard_qkv, near_qkv], spots[:2], None, qkv_shape, qkv_blocks(2, 0, groups))
-        flat_gu = lambda x: x.reshape(2 * ffn, model)
         gen_gu = place([flat_gu(shard_gu), flat_gu(near_gu)], spots[:2], None, gu_shape, gu_blocks(2, 0, 2 * ffn))
         heads_in = jnp.where(stage == 0, heads_own, after(heads_back, gen_qkv, gen_gu))
 
@@ -379,19 +379,20 @@
                     caches[0] = after(caches[0], far_o)
                     far_heads.append(qkv_send(1, o_part))
                 if i == 0 and layer == 1:
-                    sent[1] = after(sent[1], o_part)
-                    caches[0] = after(caches[0], sent[1])
+                    sent[0] = after(sent[0], o_part)
                     sent[2] = gu_send(2, o_part)
+                    sent[3] = gu_send(3, o_part)
                 o_vals.append(o_part)
             if layer == 0:
                 far_heads[0] = after(far_heads[0], o_vals[1])
                 gen_qkv = qkv_take(0, far_heads[0], gen_qkv)
                 stage_o = (shard_o, near_o, peer_o, peer_near_o)
                 away_o = (far_o, far_near_o, far_peer_o, swap(far_peer_o, "grp"))
-                stage_o, away_o = jnp.concatenate(stage_o, axis=1), jnp.concatenate(away_o, axis=1)
-                layer_o = (jnp.where(stage == 0, stage_o, away_o), jnp.where(stage == 0, away_o, stage_o))
+                all_o = jnp.stack([jnp.concatenate(stage_o, axis=1), jnp.concatenate(away_o, axis=1)])
+                layer_o = [lax.dynamic_index_in_dim(all_o, jnp.abs(stage - n), 0, False) for n in range(layers)]
             if layer == 1:
-                sent[2] = after(sent[2], o_vals[1])
+                for c in (1, 2, 3):
+                    sent[c] = after(sent[c], o_vals[1])
             backs, owns = [], []
             give = None
             for i in range(PARTS):
@@ -401,7 +402,8 @@
                 hid = (hidden[i].astype(F32) + proj).astype(BF16)
                 away = swap(hid, "pp")
                 if i:
-                    sent[3 * layer] = gu_send(3 * layer, away)
+                    if layer == 0:
+                        sent[0] = gu_send(0, away)
                     away = after(away, give)
                 elif layer == 0:
                     far_heads[1] = after(far_heads[1], hid)
@@ -412,7 +414,7 @@
                     if layer == 0:
                         keep = after(keep, gen_qkv)
                     else:
-                        for c in (1, 2):
+                        for c in range(4):
                             gen_gu = gu_take(c, sent[c], gen_gu)
                         keep = after(keep, gen_gu)
                 done = (base.astype(F32) + (keep + swap(give, "tg"))).astype(BF16)
@@ -420,14 +422,12 @@
                 backs.append(swap(done[mid:], "pp"))
             if layer == 0:
                 sent[1] = gu_send(1, *backs)
-                gen_gu = gu_take(0, sent[0], gen_gu)
             hidden = []
             for own, back in zip(owns, backs):
                 block = jnp.where(stage == layer, own, back)
                 other = swap(block, "tg")
                 hidden.append(jnp.concatenate([jnp.where(rank == 0, block, other),
                                                jnp.where(rank == 0, other, block)], axis=0))
-        gen_gu = gu_take(3, sent[3], gen_gu)
         hidden = jnp.concatenate(hidden, axis=0)
         gen_qkv = gen_qkv.reshape(layers, 6 * groups * head_dim, model)
 

time: 232 us -> 235 us (1.013)
  waiting for transfers between devices: 61.6 us -> 84.9 us
  Pallas kernels: 108 us -> 93 us
  local copies, waits for them, and re-layouts: 8.59 us -> 3.18 us
  other arithmetic: 2.4 us -> 5.64 us
  matrix products: 7.42 us -> 4.94 us
    ppermute x46, waiting for transfers between devices: 61.6 us -> 84.9 us  [swap(): return lax.ppermute(x, axis, SWAP)]
    pallas_call x4, Pallas kernels: 22.6 us -> 10 us  [mlp(): pl.pallas_call(mlp_kernel, in_specs=[pl.BlockSpec(memory_space=pltpu.SMEM...]
    squeeze x3 -> x0, local copies, waits for them, and re-layouts: 5.59 us -> none  [gu_send(): return swap(after(w_gate_up[0, cuts[c]:cuts[c + 1]], *deps), 'pp')]
    dot_general x4, matrix products: 7.42 us -> 4.94 us  [decode(): jnp.einsum('bk,dk->bd', o_all, layer_o[layer], preferred_element_type=F32)]
  transfers between devices with their start and end apart: 46 -> 46, of which waited for: 19 -> 17; matrix products, arithmetic and copies ran while one was open for 7% -> 4% of each run, Pallas kernels for 46% -> 40%
where the time goes in v1:
time: 235 us
  Pallas kernels  93 us (40%)
  waiting for transfers between devices  84.9 us (36%)
  starting transfers between devices  42.3 us (18%)
  other arithmetic  5.64 us (2%)
  matrix products  4.94 us (2%)
  local copies, waits for them, and re-layouts  3.18 us (1%)
    ppermute x46, waiting for transfers between devices, swap(): return lax.ppermute(x, axis, SWAP)  84.9 us
    pallas_call x4, Pallas kernels, attention(): pl.pallas_call(functools.partial(attn_kernel, heads=heads, head_dim=head_...  60.5 us
    ppermute x46, starting transfers between devices, swap(): return lax.ppermute(x, axis, SWAP)  42.3 us
    pallas_call x8, Pallas kernels, place(): pl.pallas_call(functools.partial(place_kernel, count=count, blocks=blocks...  19.9 us
    pallas_call x4, Pallas kernels, mlp(): pl.pallas_call(mlp_kernel, in_specs=[pl.BlockSpec(memory_space=pltpu.SMEM...  10 us
    dot_general x4, matrix products, decode(): jnp.einsum('bk,dk->bd', o_all, layer_o[layer], preferred_element_type=F32)  4.94 us
  transfers between devices with their start and end apart: 46, of which 17 were waited for; matrix products, arithmetic and copies ran while one was open for 4% of the time, Pallas kernels for 40%

profile of v1, /device:TPU:0, one launch (start us, length us, event | category | flops | bytes accessed | tf_op | source)
XLA Modules:
  0.0 235.2 jit_solution(12169659277728619987)
XLA Ops:
  0.6 3.4 %collective-permute-start.8 = (bf16[1024,256]{1,0:T(8,128)(2,1)}, bf16[1024,256]{1,0:T(8,128)(2,1)S(1)}, u32[]{:S(2)}, u32[]{:S(2)}) collective-permute-start(bf16[1024,256]{1,0:T(8,128)(2,1)} %bitcast.72), channel_id=1, source_target_pairs={{0,4},{4,0},{1,5},{5,1},{2,6},{6,2},{3,7},{7,3}} | collective-permute-start | bytes 1572872 | tf_op jit(solution)/shard_map/ppermute | solution.py:283
  4.5 1.5 collective-permute-start.2
  8.2 1.5 collective-permute-start.19
  9.7 6.4 %collective-permute-done.8 = bf16[1024,256]{1,0:T(8,128)(2,1)S(1)} collective-permute-done((bf16[1024,256]{1,0:T(8,128)(2,1)}, bf16[1024,256]{1,0:T(8,128)(2,1)S(1)}, u32[]{:S(2)}, u32[]{:S(2)}) %collective-permute-start.8) | collective-permute-done | bytes 524320 | tf_op jit(solution)/shard_map/ppermute | solution.py:283
  16.4 1.7 collective-permute-start
  19.1 1.6 maximum_bitcast_fusion
  20.7 4.6 %collective-permute-done.away_ref = bf16[128,1024]{1,0:T(8,128)(2,1)S(1)} collective-permute-done((bf16[128,1024]{1,0:T(8,128)(2,1)}, bf16[128,1024]{1,0:T(8,128)(2,1)S(1)}, u32[]{:S(2)}, u32[]{:S(2)}) %collective-permute-start) | collective-permute-done | bytes 262176 | tf_op jit(solution)/shard_map/ppermute | solution.py:283
  25.3 2.6 %project.1 = (bf16[3,512,128]{2,1,0:T(8,128)(2,1)S(1)}, bf16[3,512,128]{2,1,0:T(8,128)(2,1)S(1)}) custom-call(s32[1]{0:T(128)} %bitcast.1.half_ref, bf16[128,1024]{1,0:T(8,128)(2,1)S(1)} %copy-done.7, bf16[128,1024]{1,0:T(8,128)(2,1)S(1)} %collective-permute-done.away_ref, bf16[1,1024]{1,0:T(2,128)(2,1)S(1)} %copy-done.3, ...), custom_call_target="tpu_custom_call" | custom-call | flops 3000000000 | bytes 3145728 | tf_op jit(solution)/shard_map/project/pallas_call | solution.py:99
  28.1 1.7 collective-permute-start.3
  30.0 3.5 %place.8.refs_2_ = bf16[2,3,2,4,64,1024]{5,4,3,2,1,0:T(8,128)(2,1)} custom-call(s32[2,2]{1,0:T(2,128)S(1)} %pad_add_fusion.spots_ref, bf16[4,3,64,1024]{3,2,1,0:T(8,128)(2,1)S(1)} %bitcast.54, bf16[4,3,64,1024]{3,2,1,0:T(8,128)(2,1)} %collective-permute-done.1.wb_ref.refs_1_), custom_call_target="tpu_custom_call" | custom-call | flops 4718592000 | bytes 6291456 | tf_op jit(solution)/shard_map/place/pallas_call | solution.py:58
  33.5 5.2 %collective-permute-done.3 = bf16[3,512,128]{2,1,0:T(8,128)(2,1)S(1)} collective-permute-done((bf16[3,512,128]{2,1,0:T(8,128)(2,1)S(1)}, bf16[3,512,128]{2,1,0:T(8,128)(2,1)S(1)}, u32[]{:S(2)}, u32[]{:S(2)}) %collective-permute-start.3) | collective-permute-done | bytes 393248 | tf_op jit(solution)/shard_map/ppermute | solution.py:283
  38.8 1.7 collective-permute-start.6
  40.8 4.2 %place.9.refs_2_ = bf16[2,2,2,704,1024]{4,3,2,1,0:T(8,128)(2,1)} custom-call(s32[2,2]{1,0:T(2,128)S(1)} %pad_add_fusion.spots_ref, bf16[1408,1024]{1,0:T(8,128)(2,1)S(1)} %bitcast.46, bf16[1408,1024]{1,0:T(8,128)(2,1)S(1)} %bitcast.55), custom_call_target="tpu_custom_call" | custom-call | flops 8650752000 | bytes 11534336 | tf_op jit(solution)/shard_map/place/pallas_call | solution.py:58
  45.0 14.4 %shard_map.137 = (bf16[64,512]{1,0:T(8,128)(2,1)S(1)}, bf16[2,128,8,64,128]{4,3,2,1,0:T(8,128)(2,1)}, bf16[2,128,8,64,128]{4,3,2,1,0:T(8,128)(2,1)}) custom-call(s32[128]{0:T(128)S(1)} %copy-done.5, bf16[3,512,128]{2,1,0:T(8,128)(2,1)S(1)} %broadcast_select_fusion.rest_0_, bf16[2,128,8,64,128]{4,3,2,1,0:T(8,128)(2,1)} %bitcast.61, ...), custom_call_target="tpu_custom_call" | custom-call | flops 15000000512 | bytes 33554432 | tf_op jit(solution)/shard_map/pallas_call | solution.py:247
  59.5 1.7 collective-permute-start.5
  61.5 14.5 %shard_map.138 = (bf16[64,512]{1,0:T(8,128)(2,1)S(1)}, bf16[2,128,8,64,128]{4,3,2,1,0:T(8,128)(2,1)}, bf16[2,128,8,64,128]{4,3,2,1,0:T(8,128)(2,1)}) custom-call(s32[128]{0:T(128)S(1)} %copy-done.5, bf16[3,512,128]{2,1,0:T(8,128)(2,1)S(1)} %broadcast_select_fusion.rest_0_, ...), custom_call_target="tpu_custom_call", output_to_operand_aliasing={{1}: (4, {}), {2}: (5, {})} | custom-call | flops 15000000512 | bytes 33554432 | tf_op jit(solution)/shard_map/pallas_call | solution.py:247
  76.6 1.8 collective-permute-start.24
  78.4 1.5 collective-permute-start.14
  79.9 1.0 collective-permute-done.24
  81.2 1.2 fusion.4.hid_ref
  82.5 1.7 collective-permute-start.13
  84.2 14.6 %collective-permute-done.14.refs_0_ = bf16[2,3,64,1024]{3,2,1,0:T(8,128)(2,1)S(1)} collective-permute-done((bf16[2,3,64,1024]{3,2,1,0:T(8,128)(2,1)S(1)}, bf16[2,3,64,1024]{3,2,1,0:T(8,128)(2,1)S(1)}, u32[]{:S(2)}, u32[]{:S(2)}) %collective-permute-start.14) | collective-permute-done | bytes 786464 | tf_op jit(solution)/shard_map/ppermute | solution.py:283
  98.8 1.6 collective-permute-done.13.away_ref
  100.4 2.5 %mlp.4 = (f32[64,1024]{1,0:T(8,128)S(1)}, f32[64,1024]{1,0:T(8,128)S(1)}, bf16[64,1024]{1,0:T(8,128)(2,1)S(1)}) custom-call(s32[1]{0:T(128)} %bitcast.rank_ref, bf16[64,1024]{1,0:T(8,128)(2,1)S(1)} %fusion.4.hid_ref, bf16[64,1024]{1,0:T(8,128)(2,1)S(1)} %collective-permute-done.13.away_ref, bf16[1,1024]{1,0:T(2,128)(2,1)S(1)} %copy-done.4, ...), custom_call_target="tpu_custom_call" | custom-call | flops 4000000000 | bytes 8650752 | tf_op jit(solution)/shard_map/mlp/pallas_call | solution.py:134
  103.2 1.2 fusion.5.hid_ref
  104.5 1.7 collective-permute-start.25
  106.2 3.8 %collective-permute-done.16 = f32[64,1024]{1,0:T(8,128)S(1)} collective-permute-done((f32[64,1024]{1,0:T(8,128)S(1)}, f32[64,1024]{1,0:T(8,128)S(1)}, u32[]{:S(2)}, u32[]{:S(2)}) %collective-permute-start.16) | collective-permute-done | bytes 262176 | tf_op jit(solution)/shard_map/ppermute | solution.py:283
  110.0 1.5 collective-permute-start.17
  111.6 1.9 place.10.refs_2_
  113.5 0.8 collective-permute-done.17
  114.7 2.5 %mlp.5 = (f32[64,1024]{1,0:T(8,128)S(1)}, f32[64,1024]{1,0:T(8,128)S(1)}, bf16[64,1024]{1,0:T(8,128)(2,1)S(1)}) custom-call(s32[1]{0:T(128)} %bitcast.rank_ref, bf16[64,1024]{1,0:T(8,128)(2,1)S(1)} %fusion.5.hid_ref, bf16[64,1024]{1,0:T(8,128)(2,1)S(1)} %collective-permute-done.25.away_ref, bf16[1,1024]{1,0:T(2,128)(2,1)S(1)} %copy-done.4, ...), custom_call_target="tpu_custom_call" | custom-call | flops 4000000000 | bytes 8650752 | tf_op jit(solution)/shard_map/mlp/pallas_call | solution.py:134
  117.2 1.7 collective-permute-start.26
  118.9 1.5 collective-permute-start.41
  120.5 1.9 place.11
  122.4 2.6 %collective-permute-done.26 = f32[64,1024]{1,0:T(8,128)S(1)} collective-permute-done((f32[64,1024]{1,0:T(8,128)S(1)}, f32[64,1024]{1,0:T(8,128)S(1)}, u32[]{:S(2)}, u32[]{:S(2)}) %collective-permute-start.26) | collective-permute-done | bytes 262176 | tf_op jit(solution)/shard_map/ppermute | solution.py:283
  125.1 0.8 collective-permute-start.27
  125.8 2.8 %copy-done = bf16[2,3,2,4,64,1024]{5,4,3,2,1,0:T(8,128)(2,1)S(1)} copy-done((bf16[2,3,2,4,64,1024]{5,4,3,2,1,0:T(8,128)(2,1)S(1)}, bf16[2,3,2,4,64,1024]{5,4,3,2,1,0:T(8,128)(2,1)}, u32[]{:S(2)}) %copy-start) | copy-done | bytes 6291480
  128.6 15.8 %shard_map.139 = (bf16[64,512]{1,0:T(8,128)(2,1)S(1)}, bf16[2,128,8,64,128]{4,3,2,1,0:T(8,128)(2,1)}, bf16[2,128,8,64,128]{4,3,2,1,0:T(8,128)(2,1)}) custom-call(s32[128]{0:T(128)S(1)} %copy-done.5, bf16[64,1024]{1,0:T(8,128)(2,1)S(1)} %pad_maximum_fusion.1.rest_0_, ...), custom_call_target="tpu_custom_call", output_to_operand_aliasing={{1}: (8, {}), {2}: (9, {})} | custom-call | flops 15000000512 | bytes 33554432 | tf_op jit(solution)/shard_map/pallas_call | solution.py:247
  144.4 1.3 collective-permute-start.23
  145.8 0.7 collective-permute-start.28
  146.6 1.3 collective-permute-start.37
  147.9 0.7 collective-permute-start.35
  148.6 1.5 collective-permute-done.28
  150.1 1.5 collective-permute-start.39
  151.6 15.7 %shard_map.140 = (bf16[64,512]{1,0:T(8,128)(2,1)S(1)}, bf16[2,128,8,64,128]{4,3,2,1,0:T(8,128)(2,1)}, bf16[2,128,8,64,128]{4,3,2,1,0:T(8,128)(2,1)}) custom-call(s32[128]{0:T(128)S(1)} %copy-done.5, bf16[64,1024]{1,0:T(8,128)(2,1)S(1)} %pad_maximum_fusion.2.rest_0_, ...), custom_call_target="tpu_custom_call", output_to_operand_aliasing={{1}: (8, {}), {2}: (9, {})} | custom-call | flops 15000000512 | bytes 33554432 | tf_op jit(solution)/shard_map/pallas_call | solution.py:247
  168.0 1.2 add_convert_fusion.3.hid_ref
  169.2 2.3 collective-permute-done.33
  172.1 1.2 add_convert_fusion.1.hid_ref
  173.4 26.6 %collective-permute-done.39.refs_0_ = bf16[512,1024]{1,0:T(8,128)(2,1)S(1)} collective-permute-done((bf16[512,1024]{1,0:T(8,128)(2,1)S(1)}, bf16[512,1024]{1,0:T(8,128)(2,1)S(1)}, u32[]{:S(2)}, u32[]{:S(2)}) %collective-permute-start.39) | collective-permute-done | bytes 1048608 | tf_op jit(solution)/shard_map/ppermute | solution.py:283
  200.0 1.3 collective-permute-start.34
  201.3 1.5 collective-permute-done.29.away_ref
  202.8 2.5 %mlp.6 = (f32[64,1024]{1,0:T(8,128)S(1)}, f32[64,1024]{1,0:T(8,128)S(1)}, bf16[64,1024]{1,0:T(8,128)(2,1)S(1)}) custom-call(s32[1]{0:T(128)} %bitcast.rank_ref, bf16[64,1024]{1,0:T(8,128)(2,1)S(1)} %add_convert_fusion.3.hid_ref, bf16[64,1024]{1,0:T(8,128)(2,1)S(1)} %collective-permute-done.29.away_ref, bf16[1,1024]{1,0:T(2,128)(2,1)S(1)} %copy-done.4, ...), custom_call_target="tpu_custom_call" | custom-call | flops 4000000000 | bytes 8650752 | tf_op jit(solution)/shard_map/mlp/pallas_call | solution.py:134
  205.4 1.3 collective-permute-start.30
  206.9 2.5 %mlp.7 = (f32[64,1024]{1,0:T(8,128)S(1)}, f32[64,1024]{1,0:T(8,128)S(1)}, bf16[64,1024]{1,0:T(8,128)(2,1)S(1)}) custom-call(s32[1]{0:T(128)} %bitcast.rank_ref, bf16[64,1024]{1,0:T(8,128)(2,1)S(1)} %add_convert_fusion.1.hid_ref, bf16[64,1024]{1,0:T(8,128)(2,1)S(1)} %collective-permute-done.34.away_ref, bf16[1,1024]{1,0:T(2,128)(2,1)S(1)} %copy-done.4, ...), custom_call_target="tpu_custom_call" | custom-call | flops 4000000000 | bytes 8650752 | tf_op jit(solution)/shard_map/mlp/pallas_call | solution.py:134
  209.4 4.7 %collective-permute-done.30 = f32[64,1024]{1,0:T(8,128)S(1)} collective-permute-done((f32[64,1024]{1,0:T(8,128)S(1)}, f32[64,1024]{1,0:T(8,128)S(1)}, u32[]{:S(2)}, u32[]{:S(2)}) %collective-permute-start.30) | collective-permute-done | bytes 262176 | tf_op jit(solution)/shard_map/ppermute | solution.py:283
  214.1 1.3 collective-permute-start.43
  215.5 1.5 collective-permute-start.31
  217.0 1.7 place.12.refs_2_
  218.8 2.7 %place.13.refs_2_ = bf16[2,2,2,704,1024]{4,3,2,1,0:T(8,128)(2,1)} custom-call(s32[2,2]{1,0:T(2,128)S(1)} %pad_add_fusion.1.spots_ref, bf16[512,1024]{1,0:T(8,128)(2,1)S(1)} %collective-permute-done.39.refs_0_, bf16[512,1024]{1,0:T(8,128)(2,1)S(1)} %collective-permute-done.40.refs_1_, ...), custom_call_target="tpu_custom_call", output_to_operand_aliasing={{}: (3, {})} | custom-call | flops 3145728000 | bytes 4194304 | tf_op jit(solution)/shard_map/place/pallas_call | solution.py:58
  221.5 2.3 place.14.refs_2_
  223.8 1.7 place.15
  226.9 3.2 %collective-permute-done.44 = bf16[32,1024]{1,0:T(8,128)(2,1)S(1)} collective-permute-done((bf16[32,1024]{1,0:T(8,128)(2,1)S(1)}, bf16[32,1024]{1,0:T(8,128)(2,1)S(1)}, u32[]{:S(2)}, u32[]{:S(2)}) %collective-permute-start.44) | collective-permute-done | bytes 65568 | tf_op jit(solution)/shard_map/ppermute | solution.py:283
  230.7 3.7 %collective-permute-done.45 = bf16[32,1024]{1,0:T(8,128)(2,1)S(1)} collective-permute-done((bf16[32,1024]{1,0:T(8,128)(2,1)S(1)}, bf16[32,1024]{1,0:T(8,128)(2,1)S(1)}, u32[]{:S(2)}, u32[]{:S(2)}) %collective-permute-start.45) | collective-permute-done | bytes 65568 | tf_op jit(solution)/shard_map/ppermute | solution.py:283
  234.4 0.7 pad_maximum_fusion
  (114 shorter events, 10.1 us)
Async XLA Ops:
  0.6 15.5 %collective-permute-start.8 = (bf16[1024,256]{1,0:T(8,128)(2,1)}, bf16[1024,256]{1,0:T(8,128)(2,1)S(1)}, u32[]{:S(2)}, u32[]{:S(2)}) collective-permute-start(bf16[1024,256]{1,0:T(8,128)(2,1)} %bitcast.72), channel_id=1, source_target_pairs={{0,4},{4,0},{1,5},{5,1},{2,6},{6,2},{3,7},{7,3}} | collective-permute-start | bytes 1572872 | tf_op jit(solution)/shard_map/ppermute | solution.py:283
  4.0 14.8 %collective-permute-start.7 = (bf16[1024,256]{1,0:T(8,128)(2,1)}, bf16[1024,256]{1,0:T(8,128)(2,1)}, u32[]{:S(2)}, u32[]{:S(2)}) collective-permute-start(bf16[1024,256]{1,0:T(8,128)(2,1)} %bitcast.73), channel_id=1, source_target_pairs={{0,1},{1,0},{2,3},{3,2},{4,5},{5,4},{6,7},{7,6}} | collective-permute-start | bytes 1572872 | tf_op jit(solution)/shard_map/ppermute | solution.py:283
  4.0 36.8 %collective-permute-start.4 = (bf16[2,704,1024]{2,1,0:T(8,128)(2,1)}, bf16[2,704,1024]{2,1,0:T(8,128)(2,1)S(1)}, u32[]{:S(2)}, u32[]{:S(2)}) collective-permute-start(bf16[2,704,1024]{2,1,0:T(8,128)(2,1)} %bitcast.42), channel_id=1, source_target_pairs={{0,1},{1,0},{2,3},{3,2},{4,5},{5,4},{6,7},{7,6}} | collective-permute-start | bytes 8650760 | tf_op jit(solution)/shard_map/ppermute | solution.py:283
  4.5 20.8 %collective-permute-start.1 = (bf16[4,3,64,1024]{3,2,1,0:T(8,128)(2,1)}, bf16[4,3,64,1024]{3,2,1,0:T(8,128)(2,1)}, u32[]{:S(2)}, u32[]{:S(2)}) collective-permute-start(bf16[4,3,64,1024]{3,2,1,0:T(8,128)(2,1)} %bitcast.51), channel_id=1, source_target_pairs={{0,1},{1,0},{2,3},{3,2},{4,5},{5,4},{6,7},{7,6}} | collective-permute-start | bytes 4718600 | tf_op jit(solution)/shard_map/ppermute | solution.py:283
  4.5 3.7 %collective-permute-start.2 = (s32[128]{0:T(128)}, s32[128]{0:T(128)S(1)}, u32[]{:S(2)}, u32[]{:S(2)}) collective-permute-start(s32[128]{0:T(128)} %lens_ref.7), channel_id=1, source_target_pairs={{0,2},{2,0},{1,3},{3,1},{4,6},{6,4},{5,7},{7,5}} | collective-permute-start | bytes 1544 | tf_op jit(solution)/shard_map/ppermute | solution.py:283
  8.2 8.1 %collective-permute-start.19 = (bf16[2,1024]{1,0:T(2,128)(2,1)S(1)}, bf16[2,1024]{1,0:T(2,128)(2,1)S(1)}, u32[]{:S(2)}, u32[]{:S(2)}) collective-permute-start(bf16[2,1024]{1,0:T(2,128)(2,1)S(1)} %pad_maximum_fusion.5), channel_id=1, source_target_pairs={{0,2},{2,0},{1,3},{3,1},{4,6},{6,4},{5,7},{7,5}} | collective-permute-start | bytes 12296 | tf_op jit(solution)/shard_map/ppermute | solution.py:283
  16.1 3.0 %collective-permute-start.9 = (bf16[1024,256]{1,0:T(8,128)(2,1)S(1)}, bf16[1024,256]{1,0:T(8,128)(2,1)S(1)}, u32[]{:S(2)}, u32[]{:S(2)}) collective-permute-start(bf16[1024,256]{1,0:T(8,128)(2,1)S(1)} %collective-permute-done.8), channel_id=1, source_target_pairs={{0,1},{1,0},{2,3},{3,2},{4,5},{5,4},{6,7},{7,6}} | collective-permute-start | bytes 1572872 | tf_op jit(solution)/shard_map/ppermute | solution.py:283
  16.4 8.9 %collective-permute-start = (bf16[128,1024]{1,0:T(8,128)(2,1)}, bf16[128,1024]{1,0:T(8,128)(2,1)S(1)}, u32[]{:S(2)}, u32[]{:S(2)}) collective-permute-start(bf16[128,1024]{1,0:T(8,128)(2,1)} %own_ref.1), channel_id=1, source_target_pairs={{0,2},{2,0},{1,3},{3,1},{4,6},{6,4},{5,7},{7,5}} | collective-permute-start | bytes 786440 | tf_op jit(solution)/shard_map/ppermute | solution.py:283
  18.8 6.5 %copy-start.2 = (bf16[1,768,1024]{2,1,0:T(8,128)(2,1)S(1)}, bf16[1,768,1024]{2,1,0:T(8,128)(2,1)}, u32[]{:S(2)}) copy-start(bf16[1,768,1024]{2,1,0:T(8,128)(2,1)} %param.15) | copy-start | bytes 4718596
  18.8 6.5 %copy-start.3 = (bf16[1,1024]{1,0:T(2,128)(2,1)S(1)}, bf16[1,1024]{1,0:T(2,128)(2,1)}, u32[]{:S(2)}) copy-start(bf16[1,1024]{1,0:T(2,128)(2,1)} %gain_ref.5) | copy-start | bytes 6148
  18.9 6.5 %copy-start.7 = (bf16[128,1024]{1,0:T(8,128)(2,1)S(1)}, bf16[128,1024]{1,0:T(8,128)(2,1)}, u32[]{:S(2)}) copy-start(bf16[128,1024]{1,0:T(8,128)(2,1)} %own_ref.1) | copy-start | bytes 786436
  18.9 81.5 %collective-permute-start.15 = (bf16[704,1024]{1,0:T(8,128)(2,1)}, bf16[704,1024]{1,0:T(8,128)(2,1)S(1)}, u32[]{:S(2)}, u32[]{:S(2)}) collective-permute-start(bf16[704,1024]{1,0:T(8,128)(2,1)} %bitcast.56), channel_id=1, source_target_pairs={{0,1},{1,0},{2,3},{3,2},{4,5},{5,4},{6,7},{7,6}} | collective-permute-start | bytes 4325384 | tf_op jit(solution)/shard_map/ppermute | solution.py:283
  20.7 7.2 %copy-start.1 = (bf16[1,1408,1024]{2,1,0:T(8,128)(2,1)S(1)}, bf16[1,1408,1024]{2,1,0:T(8,128)(2,1)}, u32[]{:S(2)}) copy-start(bf16[1,1408,1024]{2,1,0:T(8,128)(2,1)} %param.18) | copy-start | bytes 8650756
  28.1 10.7 %collective-permute-start.3 = (bf16[3,512,128]{2,1,0:T(8,128)(2,1)S(1)}, bf16[3,512,128]{2,1,0:T(8,128)(2,1)S(1)}, u32[]{:S(2)}, u32[]{:S(2)}) collective-permute-start(bf16[3,512,128]{2,1,0:T(8,128)(2,1)S(1)} %get-tuple-element.59), channel_id=1, source_target_pairs={{0,2},{2,0},{1,3},{3,1},{4,6},{6,4},{5,7},{7,5}} | collective-permute-start | bytes 1179656 | tf_op jit(solution)/shard_map/ppermute | solution.py:283
  30.0 8.7 %copy-start.8 = (bf16[1,1024,256]{2,1,0:T(8,128)(2,1)S(1)}, bf16[1,1024,256]{2,1,0:T(8,128)(2,1)}, u32[]{:S(2)}) copy-start(bf16[1,1024,256]{2,1,0:T(8,128)(2,1)} %param.16) | copy-start | bytes 1572868
  38.8 22.5 %collective-permute-start.6 = (bf16[1024,256]{1,0:T(8,128)(2,1)S(1)}, bf16[1024,256]{1,0:T(8,128)(2,1)S(1)}, u32[]{:S(2)}, u32[]{:S(2)}) collective-permute-start(bf16[1024,256]{1,0:T(8,128)(2,1)S(1)} %bitcast.75), channel_id=1, source_target_pairs={{0,2},{2,0},{1,3},{3,1},{4,6},{6,4},{5,7},{7,5}} | collective-permute-start | bytes 1572872 | tf_op jit(solution)/shard_map/ppermute | solution.py:283
  40.5 36.1 %collective-permute-start.21 = (bf16[2,3,64,1024]{3,2,1,0:T(8,128)(2,1)S(1)}, bf16[2,3,64,1024]{3,2,1,0:T(8,128)(2,1)S(1)}, u32[]{:S(2)}, u32[]{:S(2)}) collective-permute-start(bf16[2,3,64,1024]{3,2,1,0:T(8,128)(2,1)S(1)} %get-tuple-element.76), channel_id=1, source_target_pairs={{0,2},{2,0},{1,3},{3,1},{4,6},{6,4},{5,7},{7,5}} | collective-permute-start | bytes 2359304 | tf_op jit(solution)/shard_map/ppermute | solution.py:283
  40.8 4.2 %copy-start.5 = (s32[128]{0:T(128)S(1)}, s32[128]{0:T(128)}, u32[]{:S(2)}) copy-start(s32[128]{0:T(128)} %lens_ref.7) | copy-start | bytes 1540
  59.5 18.9 %collective-permute-start.5 = (bf16[64,512]{1,0:T(8,128)(2,1)S(1)}, bf16[64,512]{1,0:T(8,128)(2,1)S(1)}, u32[]{:S(2)}, u32[]{:S(2)}) collective-permute-start(bf16[64,512]{1,0:T(8,128)(2,1)S(1)} %get-tuple-element.61), channel_id=1, source_target_pairs={{0,4},{4,0},{1,5},{5,1},{2,6},{6,2},{3,7},{7,3}} | collective-permute-start | bytes 196616 | tf_op jit(solution)/shard_map/ppermute | solution.py:283
  61.2 14.8 %collective-permute-start.11 = (bf16[1024,256]{1,0:T(8,128)(2,1)S(1)}, bf16[1024,256]{1,0:T(8,128)(2,1)S(1)}, u32[]{:S(2)}, u32[]{:S(2)}) collective-permute-start(bf16[1024,256]{1,0:T(8,128)(2,1)S(1)} %collective-permute-done.6), channel_id=1, source_target_pairs={{0,4},{4,0},{1,5},{5,1},{2,6},{6,2},{3,7},{7,3}} | collective-permute-start | bytes 1572872 | tf_op jit(solution)/shard_map/ppermute | solution.py:283
  61.5 19.4 %collective-permute-start.10 = (bf16[1024,256]{1,0:T(8,128)(2,1)S(1)}, bf16[1024,256]{1,0:T(8,128)(2,1)S(1)}, u32[]{:S(2)}, u32[]{:S(2)}) collective-permute-start(bf16[1024,256]{1,0:T(8,128)(2,1)S(1)} %collective-permute-done.6), channel_id=1, source_target_pairs={{0,1},{1,0},{2,3},{3,2},{4,5},{5,4},{6,7},{7,6}} | collective-permute-start | bytes 1572872 | tf_op jit(solution)/shard_map/ppermute | solution.py:283
  76.1 4.8 %collective-permute-start.12 = (bf16[1024,256]{1,0:T(8,128)(2,1)S(1)}, bf16[1024,256]{1,0:T(8,128)(2,1)S(1)}, u32[]{:S(2)}, u32[]{:S(2)}) collective-permute-start(bf16[1024,256]{1,0:T(8,128)(2,1)S(1)} %collective-permute-done.11), channel_id=1, source_target_pairs={{0,1},{1,0},{2,3},{3,2},{4,5},{5,4},{6,7},{7,6}} | collective-permute-start | bytes 1572872 | tf_op jit(solution)/shard_map/ppermute | solution.py:283
  76.6 4.3 %collective-permute-start.24 = (bf16[64,512]{1,0:T(8,128)(2,1)S(1)}, bf16[64,512]{1,0:T(8,128)(2,1)S(1)}, u32[]{:S(2)}, u32[]{:S(2)}) collective-permute-start(bf16[64,512]{1,0:T(8,128)(2,1)S(1)} %get-tuple-element.67), channel_id=1, source_target_pairs={{0,4},{4,0},{1,5},{5,1},{2,6},{6,2},{3,7},{7,3}} | collective-permute-start | bytes 196616 | tf_op jit(solution)/shard_map/ppermute | solution.py:283
  78.4 20.4 %collective-permute-start.14 = (bf16[2,3,64,1024]{3,2,1,0:T(8,128)(2,1)S(1)}, bf16[2,3,64,1024]{3,2,1,0:T(8,128)(2,1)S(1)}, u32[]{:S(2)}, u32[]{:S(2)}) collective-permute-start(bf16[2,3,64,1024]{3,2,1,0:T(8,128)(2,1)S(1)} %get-tuple-element.70), channel_id=1, source_target_pairs={{0,2},{2,0},{1,3},{3,1},{4,6},{6,4},{5,7},{7,5}} | collective-permute-start | bytes 2359304 | tf_op jit(solution)/shard_map/ppermute | solution.py:283
  80.9 30.7 %collective-permute-start.22 = (bf16[2,3,64,1024]{3,2,1,0:T(8,128)(2,1)S(1)}, bf16[2,3,64,1024]{3,2,1,0:T(8,128)(2,1)S(1)}, u32[]{:S(2)}, u32[]{:S(2)}) collective-permute-start(bf16[2,3,64,1024]{3,2,1,0:T(8,128)(2,1)S(1)} %collective-permute-done.21.refs_0_), channel_id=1, source_target_pairs={{0,1},{1,0},{2,3},{3,2},{4,5},{5,4},{6,7},{7,6}} | collective-permute-start | bytes 2359304 | tf_op jit(solution)/shard_map/ppermute | solution.py:283
  81.2 19.2 %copy-start.4 = (bf16[1,1024]{1,0:T(2,128)(2,1)S(1)}, bf16[1,1024]{1,0:T(2,128)(2,1)}, u32[]{:S(2)}) copy-start(bf16[1,1024]{1,0:T(2,128)(2,1)} %gain_ref.9) | copy-start | bytes 6148
  81.2 19.2 %copy-start.6 = (bf16[1,1024,704]{1,2,0:T(8,128)(2,1)S(1)}, bf16[1,1024,704]{1,2,0:T(8,128)(2,1)}, u32[]{:S(2)}) copy-start(bf16[1,1024,704]{1,2,0:T(8,128)(2,1)} %param.19) | copy-start | bytes 4325380
  82.5 17.9 %collective-permute-start.13 = (bf16[64,1024]{1,0:T(8,128)(2,1)S(1)}, bf16[64,1024]{1,0:T(8,128)(2,1)S(1)}, u32[]{:S(2)}, u32[]{:S(2)}) collective-permute-start(bf16[64,1024]{1,0:T(8,128)(2,1)S(1)} %fusion.4.hid_ref), channel_id=1, source_target_pairs={{0,2},{2,0},{1,3},{3,1},{4,6},{6,4},{5,7},{7,5}} | collective-permute-start | bytes 393224 | tf_op jit(solution)/shard_map/ppermute | solution.py:283
  102.9 7.1 %collective-permute-start.16 = (f32[64,1024]{1,0:T(8,128)S(1)}, f32[64,1024]{1,0:T(8,128)S(1)}, u32[]{:S(2)}, u32[]{:S(2)}) collective-permute-start(f32[64,1024]{1,0:T(8,128)S(1)} %get-tuple-element.75), channel_id=1, source_target_pairs={{0,4},{4,0},{1,5},{5,1},{2,6},{6,2},{3,7},{7,3}} | collective-permute-start | bytes 786440 | tf_op jit(solution)/shard_map/ppermute | solution.py:283
  104.5 9.1 %collective-permute-start.25 = (bf16[64,1024]{1,0:T(8,128)(2,1)S(1)}, bf16[64,1024]{1,0:T(8,128)(2,1)S(1)}, u32[]{:S(2)}, u32[]{:S(2)}) collective-permute-start(bf16[64,1024]{1,0:T(8,128)(2,1)S(1)} %fusion.5.hid_ref), channel_id=1, source_target_pairs={{0,2},{2,0},{1,3},{3,1},{4,6},{6,4},{5,7},{7,5}} | collective-permute-start | bytes 393224 | tf_op jit(solution)/shard_map/ppermute | solution.py:283
  110.0 4.3 %collective-permute-start.17 = (bf16[32,1024]{1,0:T(8,128)(2,1)S(1)}, bf16[32,1024]{1,0:T(8,128)(2,1)S(1)}, u32[]{:S(2)}, u32[]{:S(2)}) collective-permute-start(bf16[32,1024]{1,0:T(8,128)(2,1)S(1)} %slice.150), channel_id=1, source_target_pairs={{0,2},{2,0},{1,3},{3,1},{4,6},{6,4},{5,7},{7,5}} | collective-permute-start | bytes 196616 | tf_op jit(solution)/shard_map/ppermute | solution.py:283
  113.5 7.0 %collective-permute-start.20 = (bf16[2,3,64,1024]{3,2,1,0:T(8,128)(2,1)S(1)}, bf16[2,3,64,1024]{3,2,1,0:T(8,128)(2,1)S(1)}, u32[]{:S(2)}, u32[]{:S(2)}) collective-permute-start(bf16[2,3,64,1024]{3,2,1,0:T(8,128)(2,1)S(1)} %collective-permute-done.14.refs_0_), channel_id=1, source_target_pairs={{0,1},{1,0},{2,3},{3,2},{4,5},{5,4},{6,7},{7,6}} | collective-permute-start | bytes 2359304 | tf_op jit(solution)/shard_map/ppermute | solution.py:283
  114.3 6.1 %collective-permute-start.18 = (bf16[32,1024]{1,0:T(8,128)(2,1)S(1)}, bf16[32,1024]{1,0:T(8,128)(2,1)S(1)}, u32[]{:S(2)}, u32[]{:S(2)}) collective-permute-start(bf16[32,1024]{1,0:T(8,128)(2,1)S(1)} %slice_select_fusion.3), channel_id=1, source_target_pairs={{0,4},{4,0},{1,5},{5,1},{2,6},{6,2},{3,7},{7,3}} | collective-permute-start | bytes 196616 | tf_op jit(solution)/shard_map/ppermute | solution.py:283
  117.2 7.8 %collective-permute-start.26 = (f32[64,1024]{1,0:T(8,128)S(1)}, f32[64,1024]{1,0:T(8,128)S(1)}, u32[]{:S(2)}, u32[]{:S(2)}) collective-permute-start(f32[64,1024]{1,0:T(8,128)S(1)} %get-tuple-element.86), channel_id=1, source_target_pairs={{0,4},{4,0},{1,5},{5,1},{2,6},{6,2},{3,7},{7,3}} | collective-permute-start | bytes 786440 | tf_op jit(solution)/shard_map/ppermute | solution.py:283
  118.9 27.6 %collective-permute-start.41 = (bf16[272,1024]{1,0:T(8,128)(2,1)S(1)}, bf16[272,1024]{1,0:T(8,128)(2,1)S(1)}, u32[]{:S(2)}, u32[]{:S(2)}) collective-permute-start(bf16[272,1024]{1,0:T(8,128)(2,1)S(1)} %get-tuple-element.105), channel_id=1, source_target_pairs={{0,2},{2,0},{1,3},{3,1},{4,6},{6,4},{5,7},{7,5}} | collective-permute-start | bytes 1671176 | tf_op jit(solution)/shard_map/ppermute | solution.py:283
  125.1 20.7 %collective-permute-start.27 = (bf16[32,1024]{1,0:T(8,128)(2,1)S(1)}, bf16[32,1024]{1,0:T(8,128)(2,1)S(1)}, u32[]{:S(2)}, u32[]{:S(2)}) collective-permute-start(bf16[32,1024]{1,0:T(8,128)(2,1)S(1)} %slice.155), channel_id=1, source_target_pairs={{0,2},{2,0},{1,3},{3,1},{4,6},{6,4},{5,7},{7,5}} | collective-permute-start | bytes 196616 | tf_op jit(solution)/shard_map/ppermute | solution.py:283
  125.8 2.8 %copy-start = (bf16[2,3,2,4,64,1024]{5,4,3,2,1,0:T(8,128)(2,1)S(1)}, bf16[2,3,2,4,64,1024]{5,4,3,2,1,0:T(8,128)(2,1)}, u32[]{:S(2)}) copy-start(bf16[2,3,2,4,64,1024]{5,4,3,2,1,0:T(8,128)(2,1)} %place.11) | copy-start | bytes 18874372
  144.4 22.8 %collective-permute-start.23 = (bf16[64,512]{1,0:T(8,128)(2,1)S(1)}, bf16[64,512]{1,0:T(8,128)(2,1)S(1)}, u32[]{:S(2)}, u32[]{:S(2)}) collective-permute-start(bf16[64,512]{1,0:T(8,128)(2,1)S(1)} %get-tuple-element.80), channel_id=1, source_target_pairs={{0,4},{4,0},{1,5},{5,1},{2,6},{6,2},{3,7},{7,3}} | collective-permute-start | bytes 196616 | tf_op jit(solution)/shard_map/ppermute | solution.py:283
  145.8 4.3 %collective-permute-start.28 = (bf16[32,1024]{1,0:T(8,128)(2,1)S(1)}, bf16[32,1024]{1,0:T(8,128)(2,1)S(1)}, u32[]{:S(2)}, u32[]{:S(2)}) collective-permute-start(bf16[32,1024]{1,0:T(8,128)(2,1)S(1)} %slice_select_fusion.2), channel_id=1, source_target_pairs={{0,4},{4,0},{1,5},{5,1},{2,6},{6,2},{3,7},{7,3}} | collective-permute-start | bytes 196616 | tf_op jit(solution)/shard_map/ppermute | solution.py:283
  146.6 70.5 %collective-permute-start.42 = (bf16[272,1024]{1,0:T(8,128)(2,1)S(1)}, bf16[272,1024]{1,0:T(8,128)(2,1)S(1)}, u32[]{:S(2)}, u32[]{:S(2)}) collective-permute-start(bf16[272,1024]{1,0:T(8,128)(2,1)S(1)} %collective-permute-done.41.refs_0_), channel_id=1, source_target_pairs={{0,1},{1,0},{2,3},{3,2},{4,5},{5,4},{6,7},{7,6}} | collective-permute-start | bytes 1671176 | tf_op jit(solution)/shard_map/ppermute | solution.py:283
  146.6 60.1 %collective-permute-start.37 = (bf16[352,1024]{1,0:T(8,128)(2,1)S(1)}, bf16[352,1024]{1,0:T(8,128)(2,1)S(1)}, u32[]{:S(2)}, u32[]{:S(2)}) collective-permute-start(bf16[352,1024]{1,0:T(8,128)(2,1)S(1)} %slice.144), channel_id=1, source_target_pairs={{0,2},{2,0},{1,3},{3,1},{4,6},{6,4},{5,7},{7,5}} | collective-permute-start | bytes 2162696 | tf_op jit(solution)/shard_map/ppermute | solution.py:283
  147.9 67.6 %collective-permute-start.35 = (bf16[272,1024]{1,0:T(8,128)(2,1)S(1)}, bf16[272,1024]{1,0:T(8,128)(2,1)S(1)}, u32[]{:S(2)}, u32[]{:S(2)}) collective-permute-start(bf16[272,1024]{1,0:T(8,128)(2,1)S(1)} %get-tuple-element.99), channel_id=1, source_target_pairs={{0,2},{2,0},{1,3},{3,1},{4,6},{6,4},{5,7},{7,5}} | collective-permute-start | bytes 1671176 | tf_op jit(solution)/shard_map/ppermute | solution.py:283
  150.1 49.9 %collective-permute-start.39 = (bf16[512,1024]{1,0:T(8,128)(2,1)S(1)}, bf16[512,1024]{1,0:T(8,128)(2,1)S(1)}, u32[]{:S(2)}, u32[]{:S(2)}) collective-permute-start(bf16[512,1024]{1,0:T(8,128)(2,1)S(1)} %slice.145), channel_id=1, source_target_pairs={{0,2},{2,0},{1,3},{3,1},{4,6},{6,4},{5,7},{7,5}} | collective-permute-start | bytes 3145736 | tf_op jit(solution)/shard_map/ppermute | solution.py:283
  167.3 4.3 %collective-permute-start.33 = (bf16[64,512]{1,0:T(8,128)(2,1)S(1)}, bf16[64,512]{1,0:T(8,128)(2,1)S(1)}, u32[]{:S(2)}, u32[]{:S(2)}) collective-permute-start(bf16[64,512]{1,0:T(8,128)(2,1)S(1)} %get-tuple-element.89), channel_id=1, source_target_pairs={{0,4},{4,0},{1,5},{5,1},{2,6},{6,2},{3,7},{7,3}} | collective-permute-start | bytes 196616 | tf_op jit(solution)/shard_map/ppermute | solution.py:283
  171.6 31.2 %collective-permute-start.29 = (bf16[64,1024]{1,0:T(8,128)(2,1)S(1)}, bf16[64,1024]{1,0:T(8,128)(2,1)S(1)}, u32[]{:S(2)}, u32[]{:S(2)}) collective-permute-start(bf16[64,1024]{1,0:T(8,128)(2,1)S(1)} %add_convert_fusion.3.hid_ref), channel_id=1, source_target_pairs={{0,2},{2,0},{1,3},{3,1},{4,6},{6,4},{5,7},{7,5}} | collective-permute-start | bytes 393224 | tf_op jit(solution)/shard_map/ppermute | solution.py:283
  200.0 5.3 %collective-permute-start.34 = (bf16[64,1024]{1,0:T(8,128)(2,1)S(1)}, bf16[64,1024]{1,0:T(8,128)(2,1)S(1)}, u32[]{:S(2)}, u32[]{:S(2)}) collective-permute-start(bf16[64,1024]{1,0:T(8,128)(2,1)S(1)} %add_convert_fusion.1.hid_ref), channel_id=1, source_target_pairs={{0,2},{2,0},{1,3},{3,1},{4,6},{6,4},{5,7},{7,5}} | collective-permute-start | bytes 393224 | tf_op jit(solution)/shard_map/ppermute | solution.py:283
  202.8 15.9 %collective-permute-start.40 = (bf16[512,1024]{1,0:T(8,128)(2,1)S(1)}, bf16[512,1024]{1,0:T(8,128)(2,1)S(1)}, u32[]{:S(2)}, u32[]{:S(2)}) collective-permute-start(bf16[512,1024]{1,0:T(8,128)(2,1)S(1)} %collective-permute-done.39.refs_0_), channel_id=1, source_target_pairs={{0,1},{1,0},{2,3},{3,2},{4,5},{5,4},{6,7},{7,6}} | collective-permute-start | bytes 3145736 | tf_op jit(solution)/shard_map/ppermute | solution.py:283
  205.4 8.7 %collective-permute-start.30 = (f32[64,1024]{1,0:T(8,128)S(1)}, f32[64,1024]{1,0:T(8,128)S(1)}, u32[]{:S(2)}, u32[]{:S(2)}) collective-permute-start(f32[64,1024]{1,0:T(8,128)S(1)} %get-tuple-element.93), channel_id=1, source_target_pairs={{0,4},{4,0},{1,5},{5,1},{2,6},{6,2},{3,7},{7,3}} | collective-permute-start | bytes 786440 | tf_op jit(solution)/shard_map/ppermute | solution.py:283
  206.7 14.8 %collective-permute-start.38 = (bf16[352,1024]{1,0:T(8,128)(2,1)S(1)}, bf16[352,1024]{1,0:T(8,128)(2,1)S(1)}, u32[]{:S(2)}, u32[]{:S(2)}) collective-permute-start(bf16[352,1024]{1,0:T(8,128)(2,1)S(1)} %collective-permute-done.37.refs_0_), channel_id=1, source_target_pairs={{0,1},{1,0},{2,3},{3,2},{4,5},{5,4},{6,7},{7,6}} | collective-permute-start | bytes 2162696 | tf_op jit(solution)/shard_map/ppermute | solution.py:283
  214.1 11.4 %collective-permute-start.43 = (f32[64,1024]{1,0:T(8,128)S(1)}, f32[64,1024]{1,0:T(8,128)S(1)}, u32[]{:S(2)}, u32[]{:S(2)}) collective-permute-start(f32[64,1024]{1,0:T(8,128)S(1)} %get-tuple-element.108), channel_id=1, source_target_pairs={{0,4},{4,0},{1,5},{5,1},{2,6},{6,2},{3,7},{7,3}} | collective-permute-start | bytes 786440 | tf_op jit(solution)/shard_map/ppermute | solution.py:283
  215.5 10.7 %collective-permute-start.31 = (bf16[32,1024]{1,0:T(8,128)(2,1)S(1)}, bf16[32,1024]{1,0:T(8,128)(2,1)S(1)}, u32[]{:S(2)}, u32[]{:S(2)}) collective-permute-start(bf16[32,1024]{1,0:T(8,128)(2,1)S(1)} %slice.157), channel_id=1, source_target_pairs={{0,2},{2,0},{1,3},{3,1},{4,6},{6,4},{5,7},{7,5}} | collective-permute-start | bytes 196616 | tf_op jit(solution)/shard_map/ppermute | solution.py:283
  217.0 6.8 %collective-permute-start.36 = (bf16[272,1024]{1,0:T(8,128)(2,1)S(1)}, bf16[272,1024]{1,0:T(8,128)(2,1)S(1)}, u32[]{:S(2)}, u32[]{:S(2)}) collective-permute-start(bf16[272,1024]{1,0:T(8,128)(2,1)S(1)} %collective-permute-done.35.refs_0_), channel_id=1, source_target_pairs={{0,1},{1,0},{2,3},{3,2},{4,5},{5,4},{6,7},{7,6}} | collective-permute-start | bytes 1671176 | tf_op jit(solution)/shard_map/ppermute | solution.py:283
  225.6 4.5 %collective-permute-start.44 = (bf16[32,1024]{1,0:T(8,128)(2,1)S(1)}, bf16[32,1024]{1,0:T(8,128)(2,1)S(1)}, u32[]{:S(2)}, u32[]{:S(2)}) collective-permute-start(bf16[32,1024]{1,0:T(8,128)(2,1)S(1)} %slice.159), channel_id=1, source_target_pairs={{0,2},{2,0},{1,3},{3,1},{4,6},{6,4},{5,7},{7,5}} | collective-permute-start | bytes 196616 | tf_op jit(solution)/shard_map/ppermute | solution.py:283
  226.2 4.5 %collective-permute-start.32 = (bf16[32,1024]{1,0:T(8,128)(2,1)S(1)}, bf16[32,1024]{1,0:T(8,128)(2,1)S(1)}, u32[]{:S(2)}, u32[]{:S(2)}) collective-permute-start(bf16[32,1024]{1,0:T(8,128)(2,1)S(1)} %slice_select_fusion.1), channel_id=1, source_target_pairs={{0,4},{4,0},{1,5},{5,1},{2,6},{6,2},{3,7},{7,3}} | collective-permute-start | bytes 196616 | tf_op jit(solution)/shard_map/ppermute | solution.py:283
  230.1 4.3 %collective-permute-start.45 = (bf16[32,1024]{1,0:T(8,128)(2,1)S(1)}, bf16[32,1024]{1,0:T(8,128)(2,1)S(1)}, u32[]{:S(2)}, u32[]{:S(2)}) collective-permute-start(bf16[32,1024]{1,0:T(8,128)(2,1)S(1)} %slice_select_fusion), channel_id=1, source_target_pairs={{0,4},{4,0},{1,5},{5,1},{2,6},{6,2},{3,7},{7,3}} | collective-permute-start | bytes 196616 | tf_op jit(solution)/shard_map/ppermute | solution.py:283

commit v2 on v1

--- a/solution.py
+++ b/solution.py
@@ -13,7 +13,7 @@
 MASK_FILL = -1e30
 UNROLL = 16
 PARTS = 2
-GU_CUTS = (17, 49, 71)
+GU_CUTS = (0, 10, 26, 50, 72, 88)
 ROW_AXES = ("pp", "grp")
 TRAIN_AXES = ("tg", "grp")
 SWAP = ((0, 1), (1, 0))
@@ -106,41 +106,55 @@
     )(half, own, away, gain, w_own, w_near, cos_t, sin_t)
 
 
-def mlp_kernel(rank_ref, hid_ref, away_ref, gain_ref, gu_a, gu_b, dn_a, dn_b, keep_ref, give_ref, base_ref, total):
+def block_kernel(place_ref, o_own, o_own_peer, o_away, o_away_peer, hid_ref, away_ref, gain_ref, wo_a, wo_b, wo_c, wo_d,
+                 gu_a, gu_b, dn_a, dn_b, keep_ref, give_ref, base_ref, total, rows_s):
     count = hid_ref.shape[0]
     mid = count // 2
-    normed = rms_norm(jnp.concatenate([hid_ref[...], away_ref[...]], axis=0), gain_ref[...])
+    cols = wo_a.shape[1]
+    rank, half = place_ref[0], place_ref[1]
     nt = (((1,), (1,)), ((), ()))
+    proj = jnp.concatenate([hid_ref[...], away_ref[...]], axis=0).astype(F32)
+    out = None
+    for (own, away), (near, far) in (((o_own, o_away), (wo_a, wo_b)), ((o_own_peer, o_away_peer), (wo_c, wo_d))):
+        o_vals = jnp.concatenate([own[...], away[...]], axis=0).astype(F32)
+        lo, hi = o_vals[:, :cols], o_vals[:, cols:]
+        mine = jnp.where(half == 0, lo, hi).astype(BF16)
+        other = jnp.where(half == 0, hi, lo).astype(BF16)
+        for vals, w in ((mine, near), (other, far)):
+            part = lax.dot_general(vals, w[...], nt, preferred_element_type=F32)
+            out = part if out is None else out + part
+    rows = (proj + out).astype(BF16)
+    rows_s[...] = rows.astype(F32)
+    normed = rms_norm(rows, gain_ref[...])
     for gu, dn in ((gu_a, dn_a), (gu_b, dn_b)):
         gate = lax.dot_general(gu[0], normed, nt, preferred_element_type=F32)
         up = lax.dot_general(gu[1], normed, nt, preferred_element_type=F32)
         act = (jax.nn.silu(gate) * up).T.astype(BF16)
         part = jnp.dot(act, dn[...], preferred_element_type=F32)
         total[...] = part if dn is dn_a else total[...] + part
-    rank = rank_ref[0]
     mine = pl.multiple_of(rank * mid, mid)
     peer = pl.multiple_of((1 - rank) * mid, mid)
-    for i, ref in enumerate((hid_ref, away_ref)):
+    for i in range(2):
         keep_ref[i * mid:(i + 1) * mid, :] = total[pl.ds(i * count + mine, mid), :]
         give_ref[i * mid:(i + 1) * mid, :] = total[pl.ds(i * count + peer, mid), :]
-        base_ref[i * mid:(i + 1) * mid, :] = ref[pl.ds(mine, mid), :]
-
-
-def mlp(rank, hid, away, gain, gus, downs):
+        base_ref[i * mid:(i + 1) * mid, :] = rows_s[pl.ds(i * count + mine, mid), :].astype(BF16)
+
+
+def block(spot, o_vals, hid, away, gain, w_o, gus, downs):
     count, model = hid.shape
     ffn = downs[0].shape[0]
     vmem = pl.BlockSpec(memory_space=pltpu.VMEM)
     half_f32 = jax.ShapeDtypeStruct((count, model), F32)
     return pl.pallas_call(
-        mlp_kernel,
-        in_specs=[pl.BlockSpec(memory_space=pltpu.SMEM)] + [vmem] * 7,
+        block_kernel,
+        in_specs=[pl.BlockSpec(memory_space=pltpu.SMEM)] + [vmem] * 15,
         out_specs=[vmem] * 3,
         out_shape=[half_f32, half_f32, jax.ShapeDtypeStruct((count, model), BF16)],
-        scratch_shapes=[pltpu.VMEM((2 * count, model), F32)],
+        scratch_shapes=[pltpu.VMEM((2 * count, model), F32)] * 2,
         compiler_params=pltpu.CompilerParams(vmem_limit_bytes=32 << 20),
         cost_estimate=pl.CostEstimate(flops=4_000_000_000, bytes_accessed=6 * ffn * model * 2, transcendentals=0),
-        name="mlp",
-    )(rank, hid, away, gain, *gus, *downs)
+        name="block",
+    )(spot, *o_vals, hid, away, gain, *w_o, *gus, *downs)
 
 
 def attn_kernel(lens_ref, *rest, heads, head_dim, scale, row0, ready, layer):
@@ -148,7 +162,7 @@
     k_ref, v_ref = rest[:2]
     if not ready:
         w_s, w_sem = rest[-2:]
-        rest = rest[:-2]
+        rest = rest[:-8] + rest[-7:-2]
     o_ref, ko_ref, vo_ref, q_s, kt_s, vt_s, o_s, p_s = rest[-8:]
     rows = heads * head_dim
     per = k_ref.shape[1]
@@ -243,18 +257,22 @@
         in_specs += [pl.BlockSpec(memory_space=pl.ANY)] * 2
         args += list(outs)
         aliases = {len(args) - 2: 1, len(args) - 1: 2}
+    if not ready:
+        aliases[3] = 3
+    w_out = [] if ready else [jax.ShapeDtypeStruct(heads_in[2].shape, BF16)]
     cache_shape = jax.ShapeDtypeStruct(kc.shape, kc.dtype)
     return pl.pallas_call(
         functools.partial(attn_kernel, heads=heads, head_dim=head_dim, scale=head_dim ** -0.5, row0=part * count,
                           ready=ready, layer=layer),
         grid_spec=pltpu.PrefetchScalarGridSpec(
             num_scalar_prefetch=1, grid=(count // per,), in_specs=in_specs,
-            out_specs=[pl.BlockSpec((per, rows), lambda s, n: (s, 0)), cache_block, cache_block],
+            out_specs=[pl.BlockSpec((per, rows), lambda s, n: (s, 0)), cache_block, cache_block] + [
+                pl.BlockSpec(memory_space=pl.ANY)] * len(w_out),
             scratch_shapes=[pltpu.VMEM((seq, rows), F32), pltpu.VMEM((rows, seq), F32),
                             pltpu.VMEM((rows, seq), F32), pltpu.VMEM((per, rows), F32),
                             pltpu.VMEM((per * heads, seq), F32)] + ([] if ready else [
                                 pltpu.VMEM((3 * rows, heads_in[0].shape[1]), BF16), pltpu.SemaphoreType.DMA])),
-        out_shape=[jax.ShapeDtypeStruct((count, rows), BF16), cache_shape, cache_shape],
+        out_shape=[jax.ShapeDtypeStruct((count, rows), BF16), cache_shape, cache_shape] + w_out,
         input_output_aliases=aliases,
         compiler_params=pltpu.CompilerParams(dimension_semantics=("arbitrary",), vmem_limit_bytes=28 << 20),
         cost_estimate=pl.CostEstimate(flops=30_000_000_000 // parts, bytes_accessed=kc.size * 4 // parts,
@@ -277,7 +295,6 @@
         half = lax.axis_index("grp")
         groups = w_qkv.shape[1] // (3 * head_dim)
         ffn = w_gate_up.shape[1] // 2
-        cols = w_o.shape[2]
 
         def swap(x, axis):
             return lax.ppermute(x, axis, SWAP)
@@ -308,7 +325,7 @@
         shard_down = jnp.transpose(w_down[0])
         near_gu = swap(shard_gu, "grp")
         near_down = swap(shard_down, "grp")
-        peer_near_o = swap(peer_o, "grp")
+        peer_near_o = swap(after(peer_o, heads_own), "grp")
 
         spots = ((stage, half), (stage, 1 - half), (1 - stage, half), (1 - stage, 1 - half))
         spots = [jnp.stack(spot).astype(jnp.int32) for spot in spots]
@@ -341,10 +358,10 @@
 
         late_gu = after(w_gate_up[0], heads_own)
         late_qkv = after(shard_qkv, heads_own)
-        cuts = [0, GU_CUTS[0] * ffn // 44, GU_CUTS[1] * ffn // 44, GU_CUTS[2] * ffn // 44, 2 * ffn]
+        cuts = [c * ffn // 44 for c in GU_CUTS]
 
         def gu_send(c, *deps):
-            return swap(after(late_gu[cuts[c]:cuts[c + 1]], *deps), "pp")
+            return swap(after((late_gu if c else w_gate_up[0])[cuts[c]:cuts[c + 1]], *deps), "pp")
 
         def gu_take(c, piece, dst):
             near = swap(piece, "grp")
@@ -353,83 +370,72 @@
         flat_gu = lambda x: x.reshape(2 * ffn, model)
         gen_qkv = place([shard_qkv, near_qkv], spots[:2], None, qkv_shape, qkv_blocks(2, 0, groups))
         gen_gu = place([flat_gu(shard_gu), flat_gu(near_gu)], spots[:2], None, gu_shape, gu_blocks(2, 0, 2 * ffn))
-        heads_in = jnp.where(stage == 0, heads_own, after(heads_back, gen_qkv, gen_gu))
+        sent = [gu_send(0)]
+        heads_back = after(heads_back, gen_qkv, gen_gu)
+        heads_in = jnp.where(stage == 0, heads_own, heads_back)
+        gen_gu = gu_take(0, after(sent[0], heads_own), gen_gu)
 
         first = jnp.where(stage == 0, gains, far_gains)
         second = jnp.where(stage == 0, far_gains, gains)
-        far_o = swap(after(shard_o, heads_back), "pp")
         far_heads = [qkv_send(0, heads_back)]
         count = batch // PARTS
         mid = count // 2
         hidden = [hidden_in[i * count:(i + 1) * count] for i in range(PARTS)]
+        away = [away_in[i * count:(i + 1) * count] for i in range(PARTS)]
         caches = None
-        by_half = lambda x: (jnp.where(half == 0, x[:, :cols], x[:, cols:]),
-                             jnp.where(half == 0, x[:, cols:], x[:, :cols]))
-        sent = {}
+        spot = jnp.stack([rank, half]).astype(jnp.int32)
         for layer, gain in enumerate((first, second)):
             o_vals = []
             for i in range(PARTS):
-                vals = (heads_in,) if layer == 0 else (
-                    hidden[i], gain[0][None], gen_qkv.reshape(layers, 6 * groups * head_dim, model), cos_t, sin_t)
+                if layer == 1 and i == 0:
+                    gen_qkv = gen_qkv.reshape(layers, 6 * groups * head_dim, model)
+                vals = (heads_in,) if layer == 0 else (hidden[i], gain[0][None], gen_qkv, cos_t, sin_t)
                 o_part, *caches = attention(layer, i, PARTS, vals, seq_lens, kc, vc, caches)
-                if i == 0 and layer == 0:
-                    far_o = after(far_o, o_part)
-                    far_peer_o = swap(far_o, "tg")
-                    far_near_o = swap(far_o, "grp")
-                    caches[0] = after(caches[0], far_o)
+                if layer == 1:
+                    gen_qkv = caches.pop()
+                if layer == 0 and i == 0:
                     far_heads.append(qkv_send(1, o_part))
-                if i == 0 and layer == 1:
-                    sent[0] = after(sent[0], o_part)
-                    sent[2] = gu_send(2, o_part)
-                    sent[3] = gu_send(3, o_part)
-                o_vals.append(o_part)
+                if layer == 1 and i == 0:
+                    sent.append(gu_send(3, o_part))
+                o_vals.append((o_part, swap(o_part, "tg"), swap(o_part, "pp"),
+                               lax.ppermute(o_part, ("tg", "pp"), ((0, 3), (1, 2), (2, 1), (3, 0)))))
+            last = o_vals[1][0]
             if layer == 0:
-                far_heads[0] = after(far_heads[0], o_vals[1])
-                gen_qkv = qkv_take(0, far_heads[0], gen_qkv)
-                stage_o = (shard_o, near_o, peer_o, peer_near_o)
-                away_o = (far_o, far_near_o, far_peer_o, swap(far_peer_o, "grp"))
-                all_o = jnp.stack([jnp.concatenate(stage_o, axis=1), jnp.concatenate(away_o, axis=1)])
-                layer_o = [lax.dynamic_index_in_dim(all_o, jnp.abs(stage - n), 0, False) for n in range(layers)]
-            if layer == 1:
+                far_heads = [after(x, last) for x in far_heads]
+                for i in range(2):
+                    gen_qkv = qkv_take(i, far_heads[i], gen_qkv)
+                sent.append(gu_send(1, *o_vals[1][1:]))
+            else:
                 for c in (1, 2, 3):
-                    sent[c] = after(sent[c], o_vals[1])
+                    sent[c] = after(sent[c], last)
+                    gen_gu = gu_take(c, sent[c], gen_gu)
+                sent.append(gu_send(4, *o_vals[1][1:]))
+                gen_gu = gu_take(4, sent[4], gen_gu)
             backs, owns = [], []
             give = None
             for i in range(PARTS):
-                o_peer = after(swap(o_vals[i], "tg"), o_vals[1])
-                o_all = jnp.concatenate(by_half(o_vals[i]) + by_half(o_peer), axis=1)
-                proj = jnp.einsum("bk,dk->bd", o_all, layer_o[layer], preferred_element_type=F32)
-                hid = (hidden[i].astype(F32) + proj).astype(BF16)
-                away = swap(hid, "pp")
+                o_in = tuple(after(x, last) for x in o_vals[i])
+                hid = hidden[i]
                 if i:
-                    if layer == 0:
-                        sent[0] = gu_send(0, away)
-                    away = after(away, give)
-                elif layer == 0:
-                    far_heads[1] = after(far_heads[1], hid)
-                    away = after(away, far_heads[1])
-                    gen_qkv = qkv_take(1, far_heads[1], gen_qkv)
-                keep, give, base = mlp(rank[None], hid, away, mlp_gain, (shard_gu, near_gu), (shard_down, near_down))
-                if i:
-                    if layer == 0:
-                        keep = after(keep, gen_qkv)
-                    else:
-                        for c in range(4):
-                            gen_gu = gu_take(c, sent[c], gen_gu)
-                        keep = after(keep, gen_gu)
+                    hid = after(hid, give)
+                keep, give, base = block(spot, o_in, hid, away[i], mlp_gain, (shard_o, near_o, peer_o, peer_near_o),
+                                         (shard_gu, near_gu), (shard_down, near_down))
+                if i and layer == 0:
+                    keep = after(keep, gen_qkv)
                 done = (base.astype(F32) + (keep + swap(give, "tg"))).astype(BF16)
                 owns.append(done[:mid])
                 backs.append(swap(done[mid:], "pp"))
             if layer == 0:
-                sent[1] = gu_send(1, *backs)
-            hidden = []
+                sent.append(gu_send(2, *backs))
+            hidden, away = [], []
             for own, back in zip(owns, backs):
-                block = jnp.where(stage == layer, own, back)
-                other = swap(block, "tg")
-                hidden.append(jnp.concatenate([jnp.where(rank == 0, block, other),
-                                               jnp.where(rank == 0, other, block)], axis=0))
+                part = jnp.where(stage == layer, own, back)
+                other = swap(part, "tg")
+                hidden.append(jnp.concatenate([jnp.where(rank == 0, part, other),
+                                               jnp.where(rank == 0, other, part)], axis=0))
+                if layer == 0:
+                    away.append(swap(hidden[-1], "pp"))
         hidden = jnp.concatenate(hidden, axis=0)
-        gen_qkv = gen_qkv.reshape(layers, 6 * groups * head_dim, model)
 
         restore = lambda x: jnp.transpose(x, (0, 1, 4, 2, 3))
         return (hidden, restore(caches[0]), restore(caches[1]), gen_qkv, gen_gu.reshape(layers, 4 * ffn, model))

time: 235 us -> 265 us (1.13)
  Pallas kernels: 93 us -> 111 us
  local copies, waits for them, and re-layouts: 3.18 us -> 21 us
  matrix products: 4.94 us -> 0 us
  waiting for transfers between devices: 84.9 us -> 80.9 us
  starting transfers between devices: 42.3 us -> 46.1 us
    unnamed x18 -> x60, local copies, waits for them, and re-layouts: 2.83 us -> 15.4 us
    pallas_call x4, Pallas kernels: 10 us -> 22.5 us  [block(): pl.pallas_call(block_kernel, in_specs=[pl.BlockSpec(memory_space=pltpu.SM...]
    ppermute x0 -> x4, starting transfers between devices: none -> 5.78 us  [decode(): lax.ppermute(o_part, ('tg', 'pp'), ((0, 3), (1, 2), (2, 1), (3, 0)))]
    dot_general x4 -> x0, matrix products: 4.94 us -> none  [decode(): jnp.einsum('bk,dk->bd', o_all, layer_o[layer], preferred_element_type=F32)]
    pallas_call x4, Pallas kernels: 60.5 us -> 65.2 us  [attention(): pl.pallas_call(functools.partial(attn_kernel, heads=heads, head_dim=head_...]
    ppermute x46, waiting for transfers between devices: 84.9 us -> 80.1 us  [swap(): return lax.ppermute(x, axis, SWAP)]
    slice x3 -> x6, local copies, waits for them, and re-layouts: 0.19 us -> 4.25 us  [the longest x4 1.89 us: gu_send(): (late_gu if c else w_gate_up[0])[cuts[c]:cuts[c + 1]]]
    pallas_call x8 -> x9, Pallas kernels: 19.9 us -> 21.9 us  [place(): pl.pallas_call(functools.partial(place_kernel, count=count, blocks=blocks...]
  transfers between devices with their start and end apart: 46 -> 50, of which waited for: 17 -> 14; matrix products, arithmetic and copies ran while one was open for 4% -> 4% of each run, Pallas kernels for 40% -> 41%
where the time goes in v2:
time: 265 us; the launch traced here: 264 us
  Pallas kernels  111 us (42%)
  waiting for transfers between devices  80.9 us (31%)
  starting transfers between devices  46.1 us (17%)
  local copies, waits for them, and re-layouts  21 us (8%)
  other arithmetic  4.03 us (2%)
    ppermute x46, waiting for transfers between devices, swap(): return lax.ppermute(x, axis, SWAP)  80.1 us
    pallas_call x4, Pallas kernels, attention(): pl.pallas_call(functools.partial(attn_kernel, heads=heads, head_dim=head_...  65.2 us
    ppermute x46, starting transfers between devices, swap(): return lax.ppermute(x, axis, SWAP)  40.4 us
    pallas_call x4, Pallas kernels, block(): pl.pallas_call(block_kernel, in_specs=[pl.BlockSpec(memory_space=pltpu.SM...  22.5 us
    pallas_call x9, Pallas kernels, place(): pl.pallas_call(functools.partial(place_kernel, count=count, blocks=blocks...  21.9 us
    unnamed x60, local copies, waits for them, and re-layouts  15.4 us
    ppermute x4, starting transfers between devices, decode(): lax.ppermute(o_part, ('tg', 'pp'), ((0, 3), (1, 2), (2, 1), (3, 0)))  5.78 us
  transfers between devices with their start and end apart: 50, of which 14 were waited for; matrix products, arithmetic and copies ran while one was open for 4% of the time, Pallas kernels for 41%

profile of v2, /device:TPU:0, one launch (start us, length us, event | category | flops | bytes accessed | tf_op | source)
XLA Modules:
  0.0 264.3 jit_solution(4820778168887170003)
XLA Ops:
  1.5 2.5 collective-permute-start
  5.6 1.7 fusion.3
  7.2 1.7 slice_bitcast_fusion
  9.7 1.5 collective-permute-done.2
  11.2 1.8 collective-permute-start.9
  14.0 1.1 copy-done.12
  15.1 1.4 copy-done.1
  18.1 1.4 copy-done.13
  19.6 1.2 project.1
  20.8 1.5 collective-permute-start.3
  22.3 2.8 %collective-permute-done.9.wo_c = bf16[1024,256]{1,0:T(8,128)(2,1)S(1)} collective-permute-done((bf16[1024,256]{1,0:T(8,128)(2,1)}, bf16[1024,256]{1,0:T(8,128)(2,1)S(1)}, u32[]{:S(2)}, u32[]{:S(2)}) %collective-permute-start.9) | collective-permute-done | bytes 524320 | tf_op jit(solution)/shard_map/ppermute | solution.py:300
  25.1 2.5 place.9.refs_2_
  27.7 5.1 %place.10.refs_2_ = bf16[2,2,2,704,1024]{4,3,2,1,0:T(8,128)(2,1)} custom-call(s32[2,2]{1,0:T(2,128)S(1)} %pad_add_fusion.spots_ref, bf16[1408,1024]{1,0:T(8,128)(2,1)S(1)} %bitcast.30, bf16[1408,1024]{1,0:T(8,128)(2,1)} %bitcast.9.refs_1_), custom_call_target="tpu_custom_call" | custom-call | flops 8650752000 | bytes 11534336 | tf_op jit(solution)/shard_map/place/pallas_call | solution.py:58
  32.8 14.5 %shard_map.137 = (bf16[64,512]{1,0:T(8,128)(2,1)S(1)}, bf16[2,128,8,64,128]{4,3,2,1,0:T(8,128)(2,1)}, bf16[2,128,8,64,128]{4,3,2,1,0:T(8,128)(2,1)}) custom-call(s32[128]{0:T(128)S(1)} %copy-done.11, bf16[3,512,128]{2,1,0:T(8,128)(2,1)S(1)} %broadcast_select_fusion.rest_0_, bf16[2,128,8,64,128]{4,3,2,1,0:T(8,128)(2,1)} %bitcast.53, ...), custom_call_target="tpu_custom_call" | custom-call | flops 15000000512 | bytes 33554432 | tf_op jit(solution)/shard_map/pallas_call | solution.py:264
  47.3 1.5 collective-permute-start.5
  48.8 1.3 fusion.1
  50.1 1.5 collective-permute-start.6
  51.8 2.4 collective-permute-start.7
  54.3 14.7 %shard_map.138 = (bf16[64,512]{1,0:T(8,128)(2,1)S(1)}, bf16[2,128,8,64,128]{4,3,2,1,0:T(8,128)(2,1)}, bf16[2,128,8,64,128]{4,3,2,1,0:T(8,128)(2,1)}) custom-call(s32[128]{0:T(128)S(1)} %copy-done.11, bf16[3,512,128]{2,1,0:T(8,128)(2,1)S(1)} %broadcast_select_fusion.rest_0_, ...), custom_call_target="tpu_custom_call", output_to_operand_aliasing={{1}: (4, {}), {2}: (5, {})} | custom-call | flops 15000000512 | bytes 33554432 | tf_op jit(solution)/shard_map/pallas_call | solution.py:264
  70.1 1.5 collective-permute-start.48
  72.2 6.6 %block.4 = (f32[64,1024]{1,0:T(8,128)S(1)}, f32[64,1024]{1,0:T(8,128)}, bf16[64,1024]{1,0:T(8,128)(2,1)S(1)}) custom-call(s32[2]{0:T(128)S(1)} %pad_add_fusion.2.place_ref, bf16[64,512]{1,0:T(8,128)(2,1)S(1)} %get-tuple-element.75.o_own, bf16[64,512]{1,0:T(8,128)(2,1)S(1)} %collective-permute-done.5.o_own_peer, ...), custom_call_target="tpu_custom_call" | custom-call | flops 4000000000 | bytes 8650752 | tf_op jit(solution)/shard_map/block/pallas_call | solution.py:148
  80.0 1.5 collective-permute-start.16
  81.6 1.5 collective-permute-start.20
  83.1 4.1 %collective-permute-done.12 = f32[64,1024]{1,0:T(8,128)} collective-permute-done((f32[64,1024]{1,0:T(8,128)}, f32[64,1024]{1,0:T(8,128)}, u32[]{:S(2)}, u32[]{:S(2)}) %collective-permute-start.12) | collective-permute-done | bytes 262176 | tf_op jit(solution)/shard_map/ppermute | solution.py:300
  87.2 1.5 collective-permute-start.21
  88.7 1.0 add_convert_fusion.3
  90.4 1.4 collective-permute-start.13
  92.0 23.6 %collective-permute-done.21.o_away = bf16[64,512]{1,0:T(8,128)(2,1)S(1)} collective-permute-done((bf16[64,512]{1,0:T(8,128)(2,1)}, bf16[64,512]{1,0:T(8,128)(2,1)S(1)}, u32[]{:S(2)}, u32[]{:S(2)}) %collective-permute-start.21) | collective-permute-done | bytes 65568 | tf_op jit(solution)/shard_map/ppermute | solution.py:300
  119.8 1.4 copy-done.15
  121.2 1.4 copy-done.18
  122.5 1.0 copy-done.21
  123.6 1.0 copy-done.24
  124.6 1.0 copy-done.27
  126.5 5.3 %block.5 = (f32[64,1024]{1,0:T(8,128)S(1)}, f32[64,1024]{1,0:T(8,128)S(1)}, bf16[64,1024]{1,0:T(8,128)(2,1)S(1)}) custom-call(s32[2]{0:T(128)S(1)} %pad_add_fusion.2.place_ref, bf16[64,512]{1,0:T(8,128)(2,1)S(1)} %copy-done.29, bf16[64,512]{1,0:T(8,128)(2,1)S(1)} %collective-permute-done.20.o_own_peer, bf16[64,512]{1,0:T(8,128)(2,1)S(1)} %collective-permute-done.21.o_away, ...), custom_call_target="tpu_custom_call" | custom-call | flops 4000000000 | bytes 8650752 | tf_op jit(solution)/shard_map/block/pallas_call | solution.py:148
  131.8 1.1 collective-permute-start.23
  132.9 2.7 %place.11.refs_2_ = bf16[2,3,2,4,64,1024]{5,4,3,2,1,0:T(8,128)(2,1)} custom-call(s32[2,2]{1,0:T(2,128)S(1)} %pad_add_fusion.1.spots_ref, bf16[2,3,64,1024]{3,2,1,0:T(8,128)(2,1)} %collective-permute-done.18.refs_0_, bf16[2,3,64,1024]{3,2,1,0:T(8,128)(2,1)S(1)} %collective-permute-done.19.refs_1_, ...), custom_call_target="tpu_custom_call", output_to_operand_aliasing={{}: (3, {})} | custom-call | flops 2359296000 | bytes 3145728 | tf_op jit(solution)/shard_map/place/pallas_call | solution.py:58
  135.6 1.9 place.12
  137.6 2.8 %collective-permute-done.23 = f32[64,1024]{1,0:T(8,128)S(1)} collective-permute-done((f32[64,1024]{1,0:T(8,128)S(1)}, f32[64,1024]{1,0:T(8,128)S(1)}, u32[]{:S(2)}, u32[]{:S(2)}) %collective-permute-start.23) | collective-permute-done | bytes 262176 | tf_op jit(solution)/shard_map/ppermute | solution.py:300
  140.4 1.5 collective-permute-start.24
  142.5 2.9 %collective-permute-done.24 = bf16[32,1024]{1,0:T(8,128)(2,1)S(1)} collective-permute-done((bf16[32,1024]{1,0:T(8,128)(2,1)S(1)}, bf16[32,1024]{1,0:T(8,128)(2,1)S(1)}, u32[]{:S(2)}, u32[]{:S(2)}) %collective-permute-start.24) | collective-permute-done | bytes 65568 | tf_op jit(solution)/shard_map/ppermute | solution.py:300
  145.4 1.3 collective-permute-start.25
  146.7 17.8 %shard_map.139 = (bf16[64,512]{1,0:T(8,128)(2,1)S(1)}, bf16[2,128,8,64,128]{4,3,2,1,0:T(8,128)(2,1)}, bf16[2,128,8,64,128]{4,3,2,1,0:T(8,128)(2,1)}, bf16[2,1536,1024]{2,1,0:T(8,128)(2,1)}) custom-call(s32[128]{0:T(128)S(1)} %copy-done.11, ...), custom_call_target="tpu_custom_call", output_to_operand_aliasing={{1}: (8, {}), {2}: (9, {}), {3}: (3, {})} | custom-call | flops 15000000512 | bytes 33554432 | tf_op jit(solution)/shard_map/pallas_call | solution.py:264
  165.3 1.3 collective-permute-start.27
  166.6 1.4 collective-permute-start.28
  168.1 18.3 %shard_map.140 = (bf16[64,512]{1,0:T(8,128)(2,1)S(1)}, bf16[2,128,8,64,128]{4,3,2,1,0:T(8,128)(2,1)}, bf16[2,128,8,64,128]{4,3,2,1,0:T(8,128)(2,1)}, bf16[2,1536,1024]{2,1,0:T(8,128)(2,1)}) custom-call(s32[128]{0:T(128)S(1)} %copy-done.11, ...), custom_call_target="tpu_custom_call", output_to_operand_aliasing={{1}: (8, {}), {2}: (9, {}), {3}: (3, {})} | custom-call | flops 15000000512 | bytes 33554432 | tf_op jit(solution)/shard_map/pallas_call | solution.py:264
  187.1 1.3 collective-permute-start.34
  188.5 1.4 collective-permute-start.35
  189.9 1.5 collective-permute-start.36
  191.4 5.3 %block.6 = (f32[64,1024]{1,0:T(8,128)S(1)}, f32[64,1024]{1,0:T(8,128)S(1)}, bf16[64,1024]{1,0:T(8,128)(2,1)S(1)}) custom-call(s32[2]{0:T(128)S(1)} %pad_add_fusion.2.place_ref, bf16[64,512]{1,0:T(8,128)(2,1)S(1)} %get-tuple-element.104.o_own, bf16[64,512]{1,0:T(8,128)(2,1)S(1)} %collective-permute-done.26.o_own_peer, ...), custom_call_target="tpu_custom_call" | custom-call | flops 4000000000 | bytes 8650752 | tf_op jit(solution)/shard_map/block/pallas_call | solution.py:148
  197.2 1.5 collective-permute-start.42
  200.1 5.3 %block.7 = (f32[64,1024]{1,0:T(8,128)S(1)}, f32[64,1024]{1,0:T(8,128)S(1)}, bf16[64,1024]{1,0:T(8,128)(2,1)S(1)}) custom-call(s32[2]{0:T(128)S(1)} %pad_add_fusion.2.place_ref, bf16[64,512]{1,0:T(8,128)(2,1)S(1)} %get-tuple-element.111.o_own, bf16[64,512]{1,0:T(8,128)(2,1)S(1)} %collective-permute-done.33.o_own_peer, ...), custom_call_target="tpu_custom_call" | custom-call | flops 4000000000 | bytes 8650752 | tf_op jit(solution)/shard_map/block/pallas_call | solution.py:148
  205.4 2.5 collective-permute-done.30
  207.8 1.3 collective-permute-start.37
  209.2 1.2 collective-permute-start.31
  210.5 1.6 place.13.refs_2_
  212.1 30.0 %collective-permute-done.31 = bf16[32,1024]{1,0:T(8,128)(2,1)S(1)} collective-permute-done((bf16[32,1024]{1,0:T(8,128)(2,1)S(1)}, bf16[32,1024]{1,0:T(8,128)(2,1)S(1)}, u32[]{:S(2)}, u32[]{:S(2)}) %collective-permute-start.31) | collective-permute-done | bytes 65568 | tf_op jit(solution)/shard_map/ppermute | solution.py:300
  243.9 1.1 collective-permute-start.38
  245.1 2.3 collective-permute-done.32
  247.9 4.7 %collective-permute-done.38 = bf16[32,1024]{1,0:T(8,128)(2,1)S(1)} collective-permute-done((bf16[32,1024]{1,0:T(8,128)(2,1)S(1)}, bf16[32,1024]{1,0:T(8,128)(2,1)S(1)}, u32[]{:S(2)}, u32[]{:S(2)}) %collective-permute-start.38) | collective-permute-done | bytes 65568 | tf_op jit(solution)/shard_map/ppermute | solution.py:300
  253.2 1.6 place.14.refs_2_
  254.9 2.0 collective-permute-done.39
  257.7 2.5 place.15.refs_2_
  260.2 2.3 place.16.refs_2_
  262.5 1.6 place.17
  (155 shorter events, 22.8 us)
Async XLA Ops:
  0.6 27.0 %collective-permute-start.4 = (bf16[2,704,1024]{2,1,0:T(8,128)(2,1)}, bf16[2,704,1024]{2,1,0:T(8,128)(2,1)}, u32[]{:S(2)}, u32[]{:S(2)}) collective-permute-start(bf16[2,704,1024]{2,1,0:T(8,128)(2,1)} %bitcast.29), channel_id=1, source_target_pairs={{0,1},{1,0},{2,3},{3,2},{4,5},{5,4},{6,7},{7,6}} | collective-permute-start | bytes 8650760 | tf_op jit(solution)/shard_map/ppermute | solution.py:300
  1.5 11.8 %collective-permute-start = (bf16[128,1024]{1,0:T(8,128)(2,1)}, bf16[128,1024]{1,0:T(8,128)(2,1)S(1)}, u32[]{:S(2)}, u32[]{:S(2)}) collective-permute-start(bf16[128,1024]{1,0:T(8,128)(2,1)} %own_ref.1), channel_id=1, source_target_pairs={{0,2},{2,0},{1,3},{3,1},{4,6},{6,4},{5,7},{7,5}} | collective-permute-start | bytes 786440 | tf_op jit(solution)/shard_map/ppermute | solution.py:300
  4.0 10.0 %collective-permute-start.1 = (bf16[4,3,64,1024]{3,2,1,0:T(8,128)(2,1)}, bf16[4,3,64,1024]{3,2,1,0:T(8,128)(2,1)S(1)}, u32[]{:S(2)}, u32[]{:S(2)}) collective-permute-start(bf16[4,3,64,1024]{3,2,1,0:T(8,128)(2,1)} %bitcast.38), channel_id=1, source_target_pairs={{0,1},{1,0},{2,3},{3,2},{4,5},{5,4},{6,7},{7,6}} | collective-permute-start | bytes 4718600 | tf_op jit(solution)/shard_map/ppermute | solution.py:300
  4.2 7.1 %collective-permute-start.2 = (s32[128]{0:T(128)}, s32[128]{0:T(128)S(1)}, u32[]{:S(2)}, u32[]{:S(2)}) collective-permute-start(s32[128]{0:T(128)} %lens_ref.7), channel_id=1, source_target_pairs={{0,2},{2,0},{1,3},{3,1},{4,6},{6,4},{5,7},{7,5}} | collective-permute-start | bytes 1544 | tf_op jit(solution)/shard_map/ppermute | solution.py:300
  4.5 67.1 %collective-permute-start.8 = (bf16[1024,256]{1,0:T(8,128)(2,1)}, bf16[1024,256]{1,0:T(8,128)(2,1)}, u32[]{:S(2)}, u32[]{:S(2)}) collective-permute-start(bf16[1024,256]{1,0:T(8,128)(2,1)} %bitcast.47), channel_id=1, source_target_pairs={{0,1},{1,0},{2,3},{3,2},{4,5},{5,4},{6,7},{7,6}} | collective-permute-start | bytes 1572872 | tf_op jit(solution)/shard_map/ppermute | solution.py:300
  11.2 13.8 %collective-permute-start.9 = (bf16[1024,256]{1,0:T(8,128)(2,1)}, bf16[1024,256]{1,0:T(8,128)(2,1)S(1)}, u32[]{:S(2)}, u32[]{:S(2)}) collective-permute-start(bf16[1024,256]{1,0:T(8,128)(2,1)} %bitcast.48), channel_id=1, source_target_pairs={{0,4},{4,0},{1,5},{5,1},{2,6},{6,2},{3,7},{7,3}} | collective-permute-start | bytes 1572872 | tf_op jit(solution)/shard_map/ppermute | solution.py:300
  13.2 58.9 %collective-permute-start.11 = (bf16[704,1024]{1,0:T(8,128)(2,1)}, bf16[704,1024]{1,0:T(8,128)(2,1)S(1)}, u32[]{:S(2)}, u32[]{:S(2)}) collective-permute-start(bf16[704,1024]{1,0:T(8,128)(2,1)} %bitcast.42), channel_id=1, source_target_pairs={{0,1},{1,0},{2,3},{3,2},{4,5},{5,4},{6,7},{7,6}} | collective-permute-start | bytes 4325384 | tf_op jit(solution)/shard_map/ppermute | solution.py:300
  19.6 8.1 %copy-start = (bf16[1,1408,1024]{2,1,0:T(8,128)(2,1)S(1)}, bf16[1,1408,1024]{2,1,0:T(8,128)(2,1)}, u32[]{:S(2)}) copy-start(bf16[1,1408,1024]{2,1,0:T(8,128)(2,1)} %param.18) | copy-start | bytes 8650756
  20.8 12.0 %collective-permute-start.3 = (bf16[3,512,128]{2,1,0:T(8,128)(2,1)S(1)}, bf16[3,512,128]{2,1,0:T(8,128)(2,1)S(1)}, u32[]{:S(2)}, u32[]{:S(2)}) collective-permute-start(bf16[3,512,128]{2,1,0:T(8,128)(2,1)S(1)} %get-tuple-element.69), channel_id=1, source_target_pairs={{0,2},{2,0},{1,3},{3,1},{4,6},{6,4},{5,7},{7,5}} | collective-permute-start | bytes 1179656 | tf_op jit(solution)/shard_map/ppermute | solution.py:300
  25.1 47.1 %copy-start.23 = (bf16[1024,256]{1,0:T(8,128)(2,1)}, bf16[1024,256]{1,0:T(8,128)(2,1)S(1)}, u32[]{:S(2)}) copy-start(bf16[1024,256]{1,0:T(8,128)(2,1)S(1)} %collective-permute-done.9.wo_c) | copy-start | bytes 1572868
  25.1 47.0 %collective-permute-start.10 = (bf16[1024,256]{1,0:T(8,128)(2,1)S(1)}, bf16[1024,256]{1,0:T(8,128)(2,1)S(1)}, u32[]{:S(2)}, u32[]{:S(2)}) collective-permute-start(bf16[1024,256]{1,0:T(8,128)(2,1)S(1)} %collective-permute-done.9.wo_c), channel_id=1, source_target_pairs={{0,1},{1,0},{2,3},{3,2},{4,5},{5,4},{6,7},{7,6}} | collective-permute-start | bytes 1572872 | tf_op jit(solution)/shard_map/ppermute | solution.py:300
  32.8 16.0 %copy-start.2 = (bf16[1,768,1024]{2,1,0:T(8,128)(2,1)S(1)}, bf16[1,768,1024]{2,1,0:T(8,128)(2,1)}, u32[]{:S(2)}) copy-start(bf16[1,768,1024]{2,1,0:T(8,128)(2,1)} %param.15) | copy-start | bytes 4718596
  47.3 4.5 %collective-permute-start.5 = (bf16[64,512]{1,0:T(8,128)(2,1)S(1)}, bf16[64,512]{1,0:T(8,128)(2,1)S(1)}, u32[]{:S(2)}, u32[]{:S(2)}) collective-permute-start(bf16[64,512]{1,0:T(8,128)(2,1)S(1)} %get-tuple-element.75.o_own), channel_id=1, source_target_pairs={{0,4},{4,0},{1,5},{5,1},{2,6},{6,2},{3,7},{7,3}} | collective-permute-start | bytes 196616 | tf_op jit(solution)/shard_map/ppermute | solution.py:300
  50.1 19.5 %collective-permute-start.6 = (bf16[64,512]{1,0:T(8,128)(2,1)S(1)}, bf16[64,512]{1,0:T(8,128)(2,1)S(1)}, u32[]{:S(2)}, u32[]{:S(2)}) collective-permute-start(bf16[64,512]{1,0:T(8,128)(2,1)S(1)} %get-tuple-element.75.o_own), channel_id=1, source_target_pairs={{0,2},{2,0},{1,3},{3,1},{4,6},{6,4},{5,7},{7,5}} | collective-permute-start | bytes 196616 | tf_op jit(solution)/shard_map/ppermute | solution.py:300
  51.8 18.3 %collective-permute-start.7 = (bf16[64,512]{1,0:T(8,128)(2,1)S(1)}, bf16[64,512]{1,0:T(8,128)(2,1)S(1)}, u32[]{:S(2)}, u32[]{:S(2)}) collective-permute-start(bf16[64,512]{1,0:T(8,128)(2,1)S(1)} %get-tuple-element.75.o_own), channel_id=1, source_target_pairs={{0,6},{2,4},{4,2},{6,0},{1,7},{3,5},{5,3},{7,1}} | collective-permute-start | bytes 196616 | tf_op jit(solution)/shard_map/ppermute | solution.py:401
  54.2 17.9 %copy-start.6 = (bf16[64,1024]{1,0:T(8,128)(2,1)S(1)}, bf16[64,1024]{1,0:T(8,128)(2,1)}, u32[]{:S(2)}) copy-start(bf16[64,1024]{1,0:T(8,128)(2,1)} %get-tuple-element.137.hid_ref) | copy-start | bytes 393220
  54.2 17.9 %copy-start.10 = (bf16[1,1024]{1,0:T(2,128)(2,1)S(1)}, bf16[1,1024]{1,0:T(2,128)(2,1)}, u32[]{:S(2)}) copy-start(bf16[1,1024]{1,0:T(2,128)(2,1)} %gain_ref.9) | copy-start | bytes 6148
  54.2 17.9 %copy-start.14 = (bf16[1,1024,704]{1,2,0:T(8,128)(2,1)S(1)}, bf16[1,1024,704]{1,2,0:T(8,128)(2,1)}, u32[]{:S(2)}) copy-start(bf16[1,1024,704]{1,2,0:T(8,128)(2,1)} %param.19) | copy-start | bytes 4325380
  54.2 17.9 %copy-start.20 = (bf16[1,1024,256]{2,1,0:T(8,128)(2,1)S(1)}, bf16[1,1024,256]{2,1,0:T(8,128)(2,1)}, u32[]{:S(2)}) copy-start(bf16[1,1024,256]{2,1,0:T(8,128)(2,1)} %param.16) | copy-start | bytes 1572868
  69.5 12.0 %copy-start.9 = (bf16[1,1024]{1,0:T(2,128)(2,1)S(1)}, bf16[1,1024]{1,0:T(2,128)(2,1)}, u32[]{:S(2)}) copy-start(bf16[1,1024]{1,0:T(2,128)(2,1)} %gain_ref.5) | copy-start | bytes 6148
  69.6 12.0 %collective-permute-start.15 = (bf16[2,1024]{1,0:T(2,128)(2,1)S(1)}, bf16[2,1024]{1,0:T(2,128)(2,1)S(1)}, u32[]{:S(2)}, u32[]{:S(2)}) collective-permute-start(bf16[2,1024]{1,0:T(2,128)(2,1)S(1)} %pad_maximum_fusion.5), channel_id=1, source_target_pairs={{0,2},{2,0},{1,3},{3,1},{4,6},{6,4},{5,7},{7,5}} | collective-permute-start | bytes 12296 | tf_op jit(solution)/shard_map/ppermute | solution.py:300
  70.1 19.7 %collective-permute-start.48 = (bf16[160,1024]{1,0:T(8,128)(2,1)}, bf16[160,1024]{1,0:T(8,128)(2,1)S(1)}, u32[]{:S(2)}, u32[]{:S(2)}) collective-permute-start(bf16[160,1024]{1,0:T(8,128)(2,1)} %slice_bitcast_fusion), channel_id=1, source_target_pairs={{0,2},{2,0},{1,3},{3,1},{4,6},{6,4},{5,7},{7,5}} | collective-permute-start | bytes 983048 | tf_op jit(solution)/shard_map/ppermute | solution.py:300
  71.6 44.7 %collective-permute-start.18 = (bf16[2,3,64,1024]{3,2,1,0:T(8,128)(2,1)}, bf16[2,3,64,1024]{3,2,1,0:T(8,128)(2,1)}, u32[]{:S(2)}, u32[]{:S(2)}) collective-permute-start(bf16[2,3,64,1024]{3,2,1,0:T(8,128)(2,1)} %get-tuple-element.86), channel_id=1, source_target_pairs={{0,2},{2,0},{1,3},{3,1},{4,6},{6,4},{5,7},{7,5}} | collective-permute-start | bytes 2359304 | tf_op jit(solution)/shard_map/ppermute | solution.py:300
  72.1 7.4 %copy-start.17 = (bf16[704,1024]{1,0:T(8,128)(2,1)}, bf16[704,1024]{1,0:T(8,128)(2,1)S(1)}, u32[]{:S(2)}) copy-start(bf16[704,1024]{1,0:T(8,128)(2,1)S(1)} %collective-permute-done.11.dn_b) | copy-start | bytes 4325380
  72.1 7.9 %copy-start.26 = (bf16[1024,256]{1,0:T(8,128)(2,1)}, bf16[1024,256]{1,0:T(8,128)(2,1)S(1)}, u32[]{:S(2)}) copy-start(bf16[1024,256]{1,0:T(8,128)(2,1)S(1)} %collective-permute-done.10.wo_d) | copy-start | bytes 1572868
  79.5 7.8 %collective-permute-start.12 = (f32[64,1024]{1,0:T(8,128)}, f32[64,1024]{1,0:T(8,128)}, u32[]{:S(2)}, u32[]{:S(2)}) collective-permute-start(f32[64,1024]{1,0:T(8,128)} %get-tuple-element.82), channel_id=1, source_target_pairs={{0,4},{4,0},{1,5},{5,1},{2,6},{6,2},{3,7},{7,3}} | collective-permute-start | bytes 786440 | tf_op jit(solution)/shard_map/ppermute | solution.py:300
  80.0 37.8 %collective-permute-start.16 = (bf16[2,3,64,1024]{3,2,1,0:T(8,128)(2,1)}, bf16[2,3,64,1024]{3,2,1,0:T(8,128)(2,1)S(1)}, u32[]{:S(2)}, u32[]{:S(2)}) collective-permute-start(bf16[2,3,64,1024]{3,2,1,0:T(8,128)(2,1)} %get-tuple-element.84), channel_id=1, source_target_pairs={{0,2},{2,0},{1,3},{3,1},{4,6},{6,4},{5,7},{7,5}} | collective-permute-start | bytes 2359304 | tf_op jit(solution)/shard_map/ppermute | solution.py:300
  81.6 8.8 %collective-permute-start.20 = (bf16[64,512]{1,0:T(8,128)(2,1)}, bf16[64,512]{1,0:T(8,128)(2,1)S(1)}, u32[]{:S(2)}, u32[]{:S(2)}) collective-permute-start(bf16[64,512]{1,0:T(8,128)(2,1)} %copy-done.28), channel_id=1, source_target_pairs={{0,4},{4,0},{1,5},{5,1},{2,6},{6,2},{3,7},{7,3}} | collective-permute-start | bytes 196616 | tf_op jit(solution)/shard_map/ppermute | solution.py:300
  87.2 28.3 %collective-permute-start.21 = (bf16[64,512]{1,0:T(8,128)(2,1)}, bf16[64,512]{1,0:T(8,128)(2,1)S(1)}, u32[]{:S(2)}, u32[]{:S(2)}) collective-permute-start(bf16[64,512]{1,0:T(8,128)(2,1)} %copy-done.28), channel_id=1, source_target_pairs={{0,2},{2,0},{1,3},{3,1},{4,6},{6,4},{5,7},{7,5}} | collective-permute-start | bytes 196616 | tf_op jit(solution)/shard_map/ppermute | solution.py:300
  89.8 26.5 %collective-permute-start.22 = (bf16[64,512]{1,0:T(8,128)(2,1)}, bf16[64,512]{1,0:T(8,128)(2,1)S(1)}, u32[]{:S(2)}, u32[]{:S(2)}) collective-permute-start(bf16[64,512]{1,0:T(8,128)(2,1)} %copy-done.28), channel_id=1, source_target_pairs={{0,6},{2,4},{4,2},{6,0},{1,7},{3,5},{5,3},{7,1}} | collective-permute-start | bytes 196616 | tf_op jit(solution)/shard_map/ppermute | solution.py:401
  90.4 26.6 %collective-permute-start.13 = (bf16[32,1024]{1,0:T(8,128)(2,1)S(1)}, bf16[32,1024]{1,0:T(8,128)(2,1)S(1)}, u32[]{:S(2)}, u32[]{:S(2)}) collective-permute-start(bf16[32,1024]{1,0:T(8,128)(2,1)S(1)} %slice.87), channel_id=1, source_target_pairs={{0,2},{2,0},{1,3},{3,1},{4,6},{6,4},{5,7},{7,5}} | collective-permute-start | bytes 196616 | tf_op jit(solution)/shard_map/ppermute | solution.py:300
  115.6 93.7 %collective-permute-start.49 = (bf16[160,1024]{1,0:T(8,128)(2,1)S(1)}, bf16[160,1024]{1,0:T(8,128)(2,1)S(1)}, u32[]{:S(2)}, u32[]{:S(2)}) collective-permute-start(bf16[160,1024]{1,0:T(8,128)(2,1)S(1)} %collective-permute-done.48.refs_0_), channel_id=1, source_target_pairs={{0,1},{1,0},{2,3},{3,2},{4,5},{5,4},{6,7},{7,6}} | collective-permute-start | bytes 983048 | tf_op jit(solution)/shard_map/ppermute | solution.py:300
  116.3 16.6 %collective-permute-start.19 = (bf16[2,3,64,1024]{3,2,1,0:T(8,128)(2,1)}, bf16[2,3,64,1024]{3,2,1,0:T(8,128)(2,1)S(1)}, u32[]{:S(2)}, u32[]{:S(2)}) collective-permute-start(bf16[2,3,64,1024]{3,2,1,0:T(8,128)(2,1)} %collective-permute-done.18.refs_0_), channel_id=1, source_target_pairs={{0,1},{1,0},{2,3},{3,2},{4,5},{5,4},{6,7},{7,6}} | collective-permute-start | bytes 2359304 | tf_op jit(solution)/shard_map/ppermute | solution.py:300
  117.0 15.9 %collective-permute-start.14 = (bf16[32,1024]{1,0:T(8,128)(2,1)S(1)}, bf16[32,1024]{1,0:T(8,128)(2,1)S(1)}, u32[]{:S(2)}, u32[]{:S(2)}) collective-permute-start(bf16[32,1024]{1,0:T(8,128)(2,1)S(1)} %slice_select_fusion.3), channel_id=1, source_target_pairs={{0,4},{4,0},{1,5},{5,1},{2,6},{6,2},{3,7},{7,3}} | collective-permute-start | bytes 196616 | tf_op jit(solution)/shard_map/ppermute | solution.py:300
  117.8 17.9 %collective-permute-start.17 = (bf16[2,3,64,1024]{3,2,1,0:T(8,128)(2,1)S(1)}, bf16[2,3,64,1024]{3,2,1,0:T(8,128)(2,1)S(1)}, u32[]{:S(2)}, u32[]{:S(2)}) collective-permute-start(bf16[2,3,64,1024]{3,2,1,0:T(8,128)(2,1)S(1)} %collective-permute-done.16.refs_0_), channel_id=1, source_target_pairs={{0,1},{1,0},{2,3},{3,2},{4,5},{5,4},{6,7},{7,6}} | collective-permute-start | bytes 2359304 | tf_op jit(solution)/shard_map/ppermute | solution.py:300
  131.8 8.5 %collective-permute-start.23 = (f32[64,1024]{1,0:T(8,128)S(1)}, f32[64,1024]{1,0:T(8,128)S(1)}, u32[]{:S(2)}, u32[]{:S(2)}) collective-permute-start(f32[64,1024]{1,0:T(8,128)S(1)} %get-tuple-element.99), channel_id=1, source_target_pairs={{0,4},{4,0},{1,5},{5,1},{2,6},{6,2},{3,7},{7,3}} | collective-permute-start | bytes 786440 | tf_op jit(solution)/shard_map/ppermute | solution.py:300
  140.4 5.0 %collective-permute-start.24 = (bf16[32,1024]{1,0:T(8,128)(2,1)S(1)}, bf16[32,1024]{1,0:T(8,128)(2,1)S(1)}, u32[]{:S(2)}, u32[]{:S(2)}) collective-permute-start(bf16[32,1024]{1,0:T(8,128)(2,1)S(1)} %slice.93), channel_id=1, source_target_pairs={{0,2},{2,0},{1,3},{3,1},{4,6},{6,4},{5,7},{7,5}} | collective-permute-start | bytes 196616 | tf_op jit(solution)/shard_map/ppermute | solution.py:300
  141.9 48.0 %collective-permute-start.29 = (bf16[64,1024]{1,0:T(8,128)(2,1)S(1)}, bf16[64,1024]{1,0:T(8,128)(2,1)S(1)}, u32[]{:S(2)}, u32[]{:S(2)}) collective-permute-start(bf16[64,1024]{1,0:T(8,128)(2,1)S(1)} %pad_maximum_fusion.1.rest_0_.hid_ref), channel_id=1, source_target_pairs={{0,2},{2,0},{1,3},{3,1},{4,6},{6,4},{5,7},{7,5}} | collective-permute-start | bytes 393224 | tf_op jit(solution)/shard_map/ppermute | solution.py:300
  145.4 21.2 %collective-permute-start.25 = (bf16[32,1024]{1,0:T(8,128)(2,1)S(1)}, bf16[32,1024]{1,0:T(8,128)(2,1)S(1)}, u32[]{:S(2)}, u32[]{:S(2)}) collective-permute-start(bf16[32,1024]{1,0:T(8,128)(2,1)S(1)} %slice_select_fusion.2), channel_id=1, source_target_pairs={{0,4},{4,0},{1,5},{5,1},{2,6},{6,2},{3,7},{7,3}} | collective-permute-start | bytes 196616 | tf_op jit(solution)/shard_map/ppermute | solution.py:300
  164.5 21.9 %collective-permute-start.26 = (bf16[64,512]{1,0:T(8,128)(2,1)S(1)}, bf16[64,512]{1,0:T(8,128)(2,1)S(1)}, u32[]{:S(2)}, u32[]{:S(2)}) collective-permute-start(bf16[64,512]{1,0:T(8,128)(2,1)S(1)} %get-tuple-element.104.o_own), channel_id=1, source_target_pairs={{0,4},{4,0},{1,5},{5,1},{2,6},{6,2},{3,7},{7,3}} | collective-permute-start | bytes 196616 | tf_op jit(solution)/shard_map/ppermute | solution.py:300
  165.3 21.9 %collective-permute-start.27 = (bf16[64,512]{1,0:T(8,128)(2,1)S(1)}, bf16[64,512]{1,0:T(8,128)(2,1)S(1)}, u32[]{:S(2)}, u32[]{:S(2)}) collective-permute-start(bf16[64,512]{1,0:T(8,128)(2,1)S(1)} %get-tuple-element.104.o_own), channel_id=1, source_target_pairs={{0,2},{2,0},{1,3},{3,1},{4,6},{6,4},{5,7},{7,5}} | collective-permute-start | bytes 196616 | tf_op jit(solution)/shard_map/ppermute | solution.py:300
  166.6 21.9 %collective-permute-start.28 = (bf16[64,512]{1,0:T(8,128)(2,1)S(1)}, bf16[64,512]{1,0:T(8,128)(2,1)S(1)}, u32[]{:S(2)}, u32[]{:S(2)}) collective-permute-start(bf16[64,512]{1,0:T(8,128)(2,1)S(1)} %get-tuple-element.104.o_own), channel_id=1, source_target_pairs={{0,6},{2,4},{4,2},{6,0},{1,7},{3,5},{5,3},{7,1}} | collective-permute-start | bytes 196616 | tf_op jit(solution)/shard_map/ppermute | solution.py:401
  168.0 23.3 %copy-start.16 = (bf16[1,1024,704]{1,2,0:T(8,128)(2,1)S(1)}, bf16[1,1024,704]{1,2,0:T(8,128)(2,1)}, u32[]{:S(2)}) copy-start(bf16[1,1024,704]{1,2,0:T(8,128)(2,1)} %param.19) | copy-start | bytes 4325380
  168.0 23.3 %copy-start.19 = (bf16[704,1024]{1,0:T(8,128)(2,1)S(1)}, bf16[704,1024]{1,0:T(8,128)(2,1)}, u32[]{:S(2)}) copy-start(bf16[704,1024]{1,0:T(8,128)(2,1)} %copy-done.17) | copy-start | bytes 4325380
  168.1 23.3 %copy-start.22 = (bf16[1,1024,256]{2,1,0:T(8,128)(2,1)S(1)}, bf16[1,1024,256]{2,1,0:T(8,128)(2,1)}, u32[]{:S(2)}) copy-start(bf16[1,1024,256]{2,1,0:T(8,128)(2,1)} %param.16) | copy-start | bytes 1572868
  186.3 13.7 %copy-start.25 = (bf16[1024,256]{1,0:T(8,128)(2,1)S(1)}, bf16[1024,256]{1,0:T(8,128)(2,1)}, u32[]{:S(2)}) copy-start(bf16[1024,256]{1,0:T(8,128)(2,1)} %copy-done.23) | copy-start | bytes 1572868
  186.4 10.3 %collective-permute-start.33 = (bf16[64,512]{1,0:T(8,128)(2,1)S(1)}, bf16[64,512]{1,0:T(8,128)(2,1)S(1)}, u32[]{:S(2)}, u32[]{:S(2)}) collective-permute-start(bf16[64,512]{1,0:T(8,128)(2,1)S(1)} %get-tuple-element.111.o_own), channel_id=1, source_target_pairs={{0,4},{4,0},{1,5},{5,1},{2,6},{6,2},{3,7},{7,3}} | collective-permute-start | bytes 196616 | tf_op jit(solution)/shard_map/ppermute | solution.py:300
  187.1 10.1 %collective-permute-start.34 = (bf16[64,512]{1,0:T(8,128)(2,1)S(1)}, bf16[64,512]{1,0:T(8,128)(2,1)S(1)}, u32[]{:S(2)}, u32[]{:S(2)}) collective-permute-start(bf16[64,512]{1,0:T(8,128)(2,1)S(1)} %get-tuple-element.111.o_own), channel_id=1, source_target_pairs={{0,2},{2,0},{1,3},{3,1},{4,6},{6,4},{5,7},{7,5}} | collective-permute-start | bytes 196616 | tf_op jit(solution)/shard_map/ppermute | solution.py:300
  188.5 10.2 %collective-permute-start.35 = (bf16[64,512]{1,0:T(8,128)(2,1)S(1)}, bf16[64,512]{1,0:T(8,128)(2,1)S(1)}, u32[]{:S(2)}, u32[]{:S(2)}) collective-permute-start(bf16[64,512]{1,0:T(8,128)(2,1)S(1)} %get-tuple-element.111.o_own), channel_id=1, source_target_pairs={{0,6},{2,4},{4,2},{6,0},{1,7},{3,5},{5,3},{7,1}} | collective-permute-start | bytes 196616 | tf_op jit(solution)/shard_map/ppermute | solution.py:401
  189.9 9.4 %collective-permute-start.36 = (bf16[64,1024]{1,0:T(8,128)(2,1)S(1)}, bf16[64,1024]{1,0:T(8,128)(2,1)S(1)}, u32[]{:S(2)}, u32[]{:S(2)}) collective-permute-start(bf16[64,1024]{1,0:T(8,128)(2,1)S(1)} %pad_maximum_fusion.2.rest_0_.hid_ref), channel_id=1, source_target_pairs={{0,2},{2,0},{1,3},{3,1},{4,6},{6,4},{5,7},{7,5}} | collective-permute-start | bytes 393224 | tf_op jit(solution)/shard_map/ppermute | solution.py:300
  196.7 15.4 %collective-permute-start.46 = (bf16[256,1024]{1,0:T(8,128)(2,1)S(1)}, bf16[256,1024]{1,0:T(8,128)(2,1)S(1)}, u32[]{:S(2)}, u32[]{:S(2)}) collective-permute-start(bf16[256,1024]{1,0:T(8,128)(2,1)S(1)} %get-tuple-element.128), channel_id=1, source_target_pairs={{0,2},{2,0},{1,3},{3,1},{4,6},{6,4},{5,7},{7,5}} | collective-permute-start | bytes 1572872 | tf_op jit(solution)/shard_map/ppermute | solution.py:300
  197.2 50.1 %collective-permute-start.42 = (bf16[352,1024]{1,0:T(8,128)(2,1)S(1)}, bf16[352,1024]{1,0:T(8,128)(2,1)S(1)}, u32[]{:S(2)}, u32[]{:S(2)}) collective-permute-start(bf16[352,1024]{1,0:T(8,128)(2,1)S(1)} %slice.80), channel_id=1, source_target_pairs={{0,2},{2,0},{1,3},{3,1},{4,6},{6,4},{5,7},{7,5}} | collective-permute-start | bytes 2162696 | tf_op jit(solution)/shard_map/ppermute | solution.py:300
  198.7 45.2 %collective-permute-start.44 = (bf16[384,1024]{1,0:T(8,128)(2,1)S(1)}, bf16[384,1024]{1,0:T(8,128)(2,1)S(1)}, u32[]{:S(2)}, u32[]{:S(2)}) collective-permute-start(bf16[384,1024]{1,0:T(8,128)(2,1)S(1)} %slice.81), channel_id=1, source_target_pairs={{0,2},{2,0},{1,3},{3,1},{4,6},{6,4},{5,7},{7,5}} | collective-permute-start | bytes 2359304 | tf_op jit(solution)/shard_map/ppermute | solution.py:300
  199.3 8.5 %collective-permute-start.30 = (f32[64,1024]{1,0:T(8,128)S(1)}, f32[64,1024]{1,0:T(8,128)S(1)}, u32[]{:S(2)}, u32[]{:S(2)}) collective-permute-start(f32[64,1024]{1,0:T(8,128)S(1)} %get-tuple-element.110), channel_id=1, source_target_pairs={{0,4},{4,0},{1,5},{5,1},{2,6},{6,2},{3,7},{7,3}} | collective-permute-start | bytes 786440 | tf_op jit(solution)/shard_map/ppermute | solution.py:300
  207.8 35.2 %collective-permute-start.37 = (f32[64,1024]{1,0:T(8,128)S(1)}, f32[64,1024]{1,0:T(8,128)S(1)}, u32[]{:S(2)}, u32[]{:S(2)}) collective-permute-start(f32[64,1024]{1,0:T(8,128)S(1)} %get-tuple-element.118), channel_id=1, source_target_pairs={{0,4},{4,0},{1,5},{5,1},{2,6},{6,2},{3,7},{7,3}} | collective-permute-start | bytes 786440 | tf_op jit(solution)/shard_map/ppermute | solution.py:300
  209.2 32.9 %collective-permute-start.31 = (bf16[32,1024]{1,0:T(8,128)(2,1)S(1)}, bf16[32,1024]{1,0:T(8,128)(2,1)S(1)}, u32[]{:S(2)}, u32[]{:S(2)}) collective-permute-start(bf16[32,1024]{1,0:T(8,128)(2,1)S(1)} %slice.95), channel_id=1, source_target_pairs={{0,2},{2,0},{1,3},{3,1},{4,6},{6,4},{5,7},{7,5}} | collective-permute-start | bytes 196616 | tf_op jit(solution)/shard_map/ppermute | solution.py:300
  212.1 41.1 %collective-permute-start.47 = (bf16[256,1024]{1,0:T(8,128)(2,1)S(1)}, bf16[256,1024]{1,0:T(8,128)(2,1)S(1)}, u32[]{:S(2)}, u32[]{:S(2)}) collective-permute-start(bf16[256,1024]{1,0:T(8,128)(2,1)S(1)} %collective-permute-done.46.refs_0_), channel_id=1, source_target_pairs={{0,1},{1,0},{2,3},{3,2},{4,5},{5,4},{6,7},{7,6}} | collective-permute-start | bytes 1572872 | tf_op jit(solution)/shard_map/ppermute | solution.py:300
  242.1 14.8 %collective-permute-start.40 = (bf16[256,1024]{1,0:T(8,128)(2,1)S(1)}, bf16[256,1024]{1,0:T(8,128)(2,1)S(1)}, u32[]{:S(2)}, u32[]{:S(2)}) collective-permute-start(bf16[256,1024]{1,0:T(8,128)(2,1)S(1)} %get-tuple-element.123), channel_id=1, source_target_pairs={{0,2},{2,0},{1,3},{3,1},{4,6},{6,4},{5,7},{7,5}} | collective-permute-start | bytes 1572872 | tf_op jit(solution)/shard_map/ppermute | solution.py:300
  243.1 4.3 %collective-permute-start.32 = (bf16[32,1024]{1,0:T(8,128)(2,1)S(1)}, bf16[32,1024]{1,0:T(8,128)(2,1)S(1)}, u32[]{:S(2)}, u32[]{:S(2)}) collective-permute-start(bf16[32,1024]{1,0:T(8,128)(2,1)S(1)} %slice_select_fusion.1), channel_id=1, source_target_pairs={{0,4},{4,0},{1,5},{5,1},{2,6},{6,2},{3,7},{7,3}} | collective-permute-start | bytes 196616 | tf_op jit(solution)/shard_map/ppermute | solution.py:300
  243.9 8.6 %collective-permute-start.38 = (bf16[32,1024]{1,0:T(8,128)(2,1)S(1)}, bf16[32,1024]{1,0:T(8,128)(2,1)S(1)}, u32[]{:S(2)}, u32[]{:S(2)}) collective-permute-start(bf16[32,1024]{1,0:T(8,128)(2,1)S(1)} %slice.97), channel_id=1, source_target_pairs={{0,2},{2,0},{1,3},{3,1},{4,6},{6,4},{5,7},{7,5}} | collective-permute-start | bytes 196616 | tf_op jit(solution)/shard_map/ppermute | solution.py:300
  247.3 10.3 %collective-permute-start.45 = (bf16[384,1024]{1,0:T(8,128)(2,1)S(1)}, bf16[384,1024]{1,0:T(8,128)(2,1)S(1)}, u32[]{:S(2)}, u32[]{:S(2)}) collective-permute-start(bf16[384,1024]{1,0:T(8,128)(2,1)S(1)} %collective-permute-done.44.refs_0_), channel_id=1, source_target_pairs={{0,1},{1,0},{2,3},{3,2},{4,5},{5,4},{6,7},{7,6}} | collective-permute-start | bytes 2359304 | tf_op jit(solution)/shard_map/ppermute | solution.py:300
  247.4 12.8 %collective-permute-start.43 = (bf16[352,1024]{1,0:T(8,128)(2,1)S(1)}, bf16[352,1024]{1,0:T(8,128)(2,1)S(1)}, u32[]{:S(2)}, u32[]{:S(2)}) collective-permute-start(bf16[352,1024]{1,0:T(8,128)(2,1)S(1)} %collective-permute-done.42.refs_0_), channel_id=1, source_target_pairs={{0,1},{1,0},{2,3},{3,2},{4,5},{5,4},{6,7},{7,6}} | collective-permute-start | bytes 2162696 | tf_op jit(solution)/shard_map/ppermute | solution.py:300
  252.6 4.3 %collective-permute-start.39 = (bf16[32,1024]{1,0:T(8,128)(2,1)S(1)}, bf16[32,1024]{1,0:T(8,128)(2,1)S(1)}, u32[]{:S(2)}, u32[]{:S(2)}) collective-permute-start(bf16[32,1024]{1,0:T(8,128)(2,1)S(1)} %slice_select_fusion), channel_id=1, source_target_pairs={{0,4},{4,0},{1,5},{5,1},{2,6},{6,2},{3,7},{7,3}} | collective-permute-start | bytes 196616 | tf_op jit(solution)/shard_map/ppermute | solution.py:300
  256.9 5.6 %collective-permute-start.41 = (bf16[256,1024]{1,0:T(8,128)(2,1)S(1)}, bf16[256,1024]{1,0:T(8,128)(2,1)S(1)}, u32[]{:S(2)}, u32[]{:S(2)}) collective-permute-start(bf16[256,1024]{1,0:T(8,128)(2,1)S(1)} %collective-permute-done.40.refs_0_), channel_id=1, source_target_pairs={{0,1},{1,0},{2,3},{3,2},{4,5},{5,4},{6,7},{7,6}} | collective-permute-start | bytes 1572872 | tf_op jit(solution)/shard_map/ppermute | solution.py:300
  (16 other events, 20.5 us)

commit v3 on v2

--- a/solution.py
+++ b/solution.py
@@ -13,7 +13,7 @@
 MASK_FILL = -1e30
 UNROLL = 16
 PARTS = 2
-GU_CUTS = (0, 10, 26, 50, 72, 88)
+GU_CUTS = (0, 10, 30, 54, 72, 88)
 ROW_AXES = ("pp", "grp")
 TRAIN_AXES = ("tg", "grp")
 SWAP = ((0, 1), (1, 0))
@@ -157,12 +157,11 @@
     )(spot, *o_vals, hid, away, gain, *w_o, *gus, *downs)
 
 
-def attn_kernel(lens_ref, *rest, heads, head_dim, scale, row0, ready, layer):
+def attn_kernel(lens_ref, *rest, heads, head_dim, scale, row0, ready):
     heads_in, rest = rest[:1 if ready else 5], rest[1 if ready else 5:]
     k_ref, v_ref = rest[:2]
     if not ready:
-        w_s, w_sem = rest[-2:]
-        rest = rest[:-8] + rest[-7:-2]
+        rest = rest[:-6] + rest[-5:]
     o_ref, ko_ref, vo_ref, q_s, kt_s, vt_s, o_s, p_s = rest[-8:]
     rows = heads * head_dim
     per = k_ref.shape[1]
@@ -181,15 +180,12 @@
                     q_s[...] = vals.T
             return
         h_ref, gain_ref, w_ref, cos_ref, sin_ref = heads_in
-        fetch = pltpu.make_async_copy(w_ref.at[layer], w_s, w_sem)
-        fetch.start()
         normed = rms_norm(h_ref[...], gain_ref[...])
         normed = jnp.concatenate([normed] * (batch // h_ref.shape[0]), axis=0)
 
-        fetch.wait()
 
         def proj(t, turn):
-            vals = lax.dot_general(w_s[t * rows:(t + 1) * rows, :], normed, (((1,), (1,)), ((), ())),
+            vals = lax.dot_general(w_ref[0, t * rows:(t + 1) * rows, :], normed, (((1,), (1,)), ((), ())),
                                    preferred_element_type=F32)
             if turn:
                 vals = rope_t(vals.reshape(heads, head_dim, batch), cos_ref[...], sin_ref[...])
@@ -248,7 +244,7 @@
         in_specs = [whole(3, rows, seq)]
     else:
         model = heads_in[0].shape[1]
-        in_specs = [whole(count, model), whole(1, model), pl.BlockSpec(memory_space=pltpu.HBM),
+        in_specs = [whole(count, model), whole(1, model), pl.BlockSpec((1, 3 * rows, model), lambda s, n: (layer, 0, 0)),
                     whole(head_dim // 2, seq), whole(head_dim // 2, seq)]
     in_specs += [cache_block, cache_block]
     args = [seq_lens, *heads_in, kc, vc]
@@ -263,15 +259,14 @@
     cache_shape = jax.ShapeDtypeStruct(kc.shape, kc.dtype)
     return pl.pallas_call(
         functools.partial(attn_kernel, heads=heads, head_dim=head_dim, scale=head_dim ** -0.5, row0=part * count,
-                          ready=ready, layer=layer),
+                          ready=ready),
         grid_spec=pltpu.PrefetchScalarGridSpec(
             num_scalar_prefetch=1, grid=(count // per,), in_specs=in_specs,
             out_specs=[pl.BlockSpec((per, rows), lambda s, n: (s, 0)), cache_block, cache_block] + [
                 pl.BlockSpec(memory_space=pl.ANY)] * len(w_out),
             scratch_shapes=[pltpu.VMEM((seq, rows), F32), pltpu.VMEM((rows, seq), F32),
                             pltpu.VMEM((rows, seq), F32), pltpu.VMEM((per, rows), F32),
-                            pltpu.VMEM((per * heads, seq), F32)] + ([] if ready else [
-                                pltpu.VMEM((3 * rows, heads_in[0].shape[1]), BF16), pltpu.SemaphoreType.DMA])),
+                            pltpu.VMEM((per * heads, seq), F32)]),
         out_shape=[jax.ShapeDtypeStruct((count, rows), BF16), cache_shape, cache_shape] + w_out,
         input_output_aliases=aliases,
         compiler_params=pltpu.CompilerParams(dimension_semantics=("arbitrary",), vmem_limit_bytes=28 << 20),
@@ -404,12 +399,12 @@
                 far_heads = [after(x, last) for x in far_heads]
                 for i in range(2):
                     gen_qkv = qkv_take(i, far_heads[i], gen_qkv)
-                sent.append(gu_send(1, *o_vals[1][1:]))
+                sent.append(gu_send(1, last))
             else:
                 for c in (1, 2, 3):
                     sent[c] = after(sent[c], last)
                     gen_gu = gu_take(c, sent[c], gen_gu)
-                sent.append(gu_send(4, *o_vals[1][1:]))
+                sent.append(gu_send(4, last))
                 gen_gu = gu_take(4, sent[4], gen_gu)
             backs, owns = [], []
             give = None
@@ -420,8 +415,6 @@
                     hid = after(hid, give)
                 keep, give, base = block(spot, o_in, hid, away[i], mlp_gain, (shard_o, near_o, peer_o, peer_near_o),
                                          (shard_gu, near_gu), (shard_down, near_down))
-                if i and layer == 0:
-                    keep = after(keep, gen_qkv)
                 done = (base.astype(F32) + (keep + swap(give, "tg"))).astype(BF16)
                 owns.append(done[:mid])
                 backs.append(swap(done[mid:], "pp"))

time: 265 us -> 273 us (1.030)
  waiting for transfers between devices: 80.9 us -> 96.2 us
  starting transfers between devices: 46.1 us -> 42.5 us
  local copies, waits for them, and re-layouts: 21 us -> 17.7 us
    ppermute x46, waiting for transfers between devices: 80.1 us -> 91.9 us  [swap(): return lax.ppermute(x, axis, SWAP)]
    ppermute x46, starting transfers between devices: 40.4 us -> 36 us  [swap(): return lax.ppermute(x, axis, SWAP)]
    unnamed x60 -> x42, local copies, waits for them, and re-layouts: 15.4 us -> 11.6 us
    ppermute x4, waiting for transfers between devices: 0.73 us -> 4.27 us  [decode(): lax.ppermute(o_part, ('tg', 'pp'), ((0, 3), (1, 2), (2, 1), (3, 0)))]
    pallas_call x4, Pallas kernels: 65.2 us -> 62.1 us  [attention(): pl.pallas_call(functools.partial(attn_kernel, heads=heads, head_dim=head_...]
  transfers between devices with their start and end apart: 50 -> 50, of which waited for: 14 -> 19; matrix products, arithmetic and copies ran while one was open for 4% -> 4% of each run, Pallas kernels for 41% -> 40%
where the time goes in v3:
time: 273 us; the launch traced here: 272 us
  Pallas kernels  110 us (40%)
  waiting for transfers between devices  96.2 us (35%)
  starting transfers between devices  42.5 us (16%)
  local copies, waits for them, and re-layouts  17.7 us (6%)
  other arithmetic  4.04 us (1%)
    ppermute x46, waiting for transfers between devices, swap(): return lax.ppermute(x, axis, SWAP)  91.9 us
    pallas_call x4, Pallas kernels, attention(): pl.pallas_call(functools.partial(attn_kernel, heads=heads, head_dim=head_...  62.1 us
    ppermute x46, starting transfers between devices, swap(): return lax.ppermute(x, axis, SWAP)  36 us
    pallas_call x4, Pallas kernels, block(): pl.pallas_call(block_kernel, in_specs=[pl.BlockSpec(memory_space=pltpu.SM...  24.9 us
    pallas_call x9, Pallas kernels, place(): pl.pallas_call(functools.partial(place_kernel, count=count, blocks=blocks...  22.1 us
    unnamed x42, local copies, waits for them, and re-layouts  11.6 us
    ppermute x4, starting transfers between devices, decode(): lax.ppermute(o_part, ('tg', 'pp'), ((0, 3), (1, 2), (2, 1), (3, 0)))  6.44 us
  transfers between devices with their start and end apart: 50, of which 19 were waited for; matrix products, arithmetic and copies ran while one was open for 4% of the time, Pallas kernels for 40%

profile of v3, /device:TPU:0, one launch (start us, length us, event | category | flops | bytes accessed | tf_op | source)
XLA Modules:
  0.0 272.0 jit_solution(7733390809162615219)
XLA Ops:
  1.5 2.5 collective-permute-start
  5.6 1.0 fusion.2
  6.5 1.7 slice_bitcast_fusion
  8.9 2.3 collective-permute-done.2
  11.2 1.8 collective-permute-start.9
  13.3 1.1 copy-done.14
  14.4 1.4 copy-done.1
  17.5 1.4 copy-done.15
  18.9 1.2 project.1
  20.1 1.5 collective-permute-start.3
  21.6 3.6 %collective-permute-done.9.wo_c = bf16[1024,256]{1,0:T(8,128)(2,1)} collective-permute-done((bf16[1024,256]{1,0:T(8,128)(2,1)}, bf16[1024,256]{1,0:T(8,128)(2,1)}, u32[]{:S(2)}, u32[]{:S(2)}) %collective-permute-start.9) | collective-permute-done | bytes 524320 | tf_op jit(solution)/shard_map/ppermute | solution.py:295
  25.2 2.5 place.9.refs_2_
  27.8 5.1 %place.10.refs_2_ = bf16[2,2,2,704,1024]{4,3,2,1,0:T(8,128)(2,1)} custom-call(s32[2,2]{1,0:T(2,128)S(1)} %pad_add_fusion.spots_ref, bf16[1408,1024]{1,0:T(8,128)(2,1)S(1)} %bitcast.30, bf16[1408,1024]{1,0:T(8,128)(2,1)} %bitcast.9.refs_1_), custom_call_target="tpu_custom_call" | custom-call | flops 8650752000 | bytes 11534336 | tf_op jit(solution)/shard_map/place/pallas_call | solution.py:58
  32.9 14.4 %shard_map.137 = (bf16[64,512]{1,0:T(8,128)(2,1)S(1)}, bf16[2,128,8,64,128]{4,3,2,1,0:T(8,128)(2,1)}, bf16[2,128,8,64,128]{4,3,2,1,0:T(8,128)(2,1)}) custom-call(s32[128]{0:T(128)S(1)} %copy-done.13, bf16[3,512,128]{2,1,0:T(8,128)(2,1)S(1)} %broadcast_select_fusion.rest_0_, bf16[2,128,8,64,128]{4,3,2,1,0:T(8,128)(2,1)} %bitcast.54, ...), custom_call_target="tpu_custom_call" | custom-call | flops 15000000512 | bytes 33554432 | tf_op jit(solution)/shard_map/pallas_call | solution.py:260
  48.0 14.5 %shard_map.138 = (bf16[64,512]{1,0:T(8,128)(2,1)S(1)}, bf16[2,128,8,64,128]{4,3,2,1,0:T(8,128)(2,1)}, bf16[2,128,8,64,128]{4,3,2,1,0:T(8,128)(2,1)}) custom-call(s32[128]{0:T(128)S(1)} %copy-done.13, bf16[3,512,128]{2,1,0:T(8,128)(2,1)S(1)} %broadcast_select_fusion.rest_0_, ...), custom_call_target="tpu_custom_call", output_to_operand_aliasing={{1}: (4, {}), {2}: (5, {})} | custom-call | flops 15000000512 | bytes 33554432 | tf_op jit(solution)/shard_map/pallas_call | solution.py:260
  62.6 1.5 collective-permute-start.20
  64.1 1.5 collective-permute-start.21
  65.6 1.5 collective-permute-done.20.o_own_peer
  67.2 2.4 collective-permute-start.22
  70.1 2.3 collective-permute-done.22.o_away_peer
  72.4 1.5 collective-permute-start.6
  74.1 1.3 collective-permute-start.7
  75.4 1.5 fusion
  77.3 1.1 collective-permute-start.15
  78.4 1.0 collective-permute-done.7.o_away_peer
  80.1 1.4 collective-permute-start.18
  81.5 1.4 copy-done.16
  82.9 1.0 copy-done.17
  84.7 6.0 %block.4 = (f32[64,1024]{1,0:T(8,128)S(1)}, f32[64,1024]{1,0:T(8,128)S(1)}, bf16[64,1024]{1,0:T(8,128)(2,1)S(1)}) custom-call(s32[2]{0:T(128)S(1)} %pad_add_fusion.2.place_ref, bf16[64,512]{1,0:T(8,128)(2,1)S(1)} %copy-done.20, bf16[64,512]{1,0:T(8,128)(2,1)S(1)} %collective-permute-done.5.o_own_peer, bf16[64,512]{1,0:T(8,128)(2,1)S(1)} %collective-permute-done.6.o_away, ...), custom_call_target="tpu_custom_call" | custom-call | flops 4000000000 | bytes 8650752 | tf_op jit(solution)/shard_map/block/pallas_call | solution.py:148
  90.8 1.4 collective-permute-start.12
  92.2 6.1 %block.5 = (f32[64,1024]{1,0:T(8,128)S(1)}, f32[64,1024]{1,0:T(8,128)S(1)}, bf16[64,1024]{1,0:T(8,128)(2,1)S(1)}) custom-call(s32[2]{0:T(128)S(1)} %pad_add_fusion.2.place_ref, bf16[64,512]{1,0:T(8,128)(2,1)S(1)} %get-tuple-element.90.o_own, bf16[64,512]{1,0:T(8,128)(2,1)} %collective-permute-done.20.o_own_peer, ...), custom_call_target="tpu_custom_call" | custom-call | flops 4000000000 | bytes 8650752 | tf_op jit(solution)/shard_map/block/pallas_call | solution.py:148
  99.7 1.4 collective-permute-start.13
  101.1 3.5 %collective-permute-done.23 = f32[64,1024]{1,0:T(8,128)S(1)} collective-permute-done((f32[64,1024]{1,0:T(8,128)S(1)}, f32[64,1024]{1,0:T(8,128)S(1)}, u32[]{:S(2)}, u32[]{:S(2)}) %collective-permute-start.23) | collective-permute-done | bytes 262176 | tf_op jit(solution)/shard_map/ppermute | solution.py:295
  105.2 17.7 %collective-permute-done.13 = bf16[32,1024]{1,0:T(8,128)(2,1)S(1)} collective-permute-done((bf16[32,1024]{1,0:T(8,128)(2,1)S(1)}, bf16[32,1024]{1,0:T(8,128)(2,1)S(1)}, u32[]{:S(2)}, u32[]{:S(2)}) %collective-permute-start.13) | collective-permute-done | bytes 65568 | tf_op jit(solution)/shard_map/ppermute | solution.py:295
  122.9 1.1 collective-permute-start.14
  124.0 1.0 collective-permute-start.25
  125.2 2.0 collective-permute-done.14
  128.7 1.9 place.11.refs_2_
  130.6 1.9 place.12
  132.5 16.5 %shard_map.139 = (bf16[64,512]{1,0:T(8,128)(2,1)S(1)}, bf16[2,128,8,64,128]{4,3,2,1,0:T(8,128)(2,1)}, bf16[2,128,8,64,128]{4,3,2,1,0:T(8,128)(2,1)}, bf16[2,1536,1024]{2,1,0:T(8,128)(2,1)}) custom-call(s32[128]{0:T(128)S(1)} %copy-done.13, ...), custom_call_target="tpu_custom_call", output_to_operand_aliasing={{1}: (8, {}), {2}: (9, {}), {3}: (3, {})} | custom-call | flops 15000000512 | bytes 33554432 | tf_op jit(solution)/shard_map/pallas_call | solution.py:260
  149.0 1.1 collective-permute-start.26
  150.9 1.6 collective-permute-start.28
  152.5 16.7 %shard_map.140 = (bf16[64,512]{1,0:T(8,128)(2,1)S(1)}, bf16[2,128,8,64,128]{4,3,2,1,0:T(8,128)(2,1)}, bf16[2,128,8,64,128]{4,3,2,1,0:T(8,128)(2,1)}, bf16[2,1536,1024]{2,1,0:T(8,128)(2,1)}) custom-call(s32[128]{0:T(128)S(1)} %copy-done.13, ...), custom_call_target="tpu_custom_call", output_to_operand_aliasing={{1}: (8, {}), {2}: (9, {}), {3}: (3, {})} | custom-call | flops 15000000512 | bytes 33554432 | tf_op jit(solution)/shard_map/pallas_call | solution.py:260
  169.1 1.1 collective-permute-start.33
  172.9 1.2 collective-permute-start.44
  174.9 1.2 collective-permute-start.34
  176.1 1.1 collective-permute-start.35
  177.2 6.1 %block.6 = (f32[64,1024]{1,0:T(8,128)S(1)}, f32[64,1024]{1,0:T(8,128)S(1)}, bf16[64,1024]{1,0:T(8,128)(2,1)S(1)}) custom-call(s32[2]{0:T(128)S(1)} %pad_add_fusion.2.place_ref, bf16[64,512]{1,0:T(8,128)(2,1)S(1)} %get-tuple-element.102.o_own, bf16[64,512]{1,0:T(8,128)(2,1)S(1)} %collective-permute-done.26.o_own_peer, ...), custom_call_target="tpu_custom_call" | custom-call | flops 4000000000 | bytes 8650752 | tf_op jit(solution)/shard_map/block/pallas_call | solution.py:148
  184.0 25.3 %collective-permute-done.34.o_away = bf16[64,512]{1,0:T(8,128)(2,1)S(1)} collective-permute-done((bf16[64,512]{1,0:T(8,128)(2,1)S(1)}, bf16[64,512]{1,0:T(8,128)(2,1)S(1)}, u32[]{:S(2)}, u32[]{:S(2)}) %collective-permute-start.34) | collective-permute-done | bytes 65568 | tf_op jit(solution)/shard_map/ppermute | solution.py:295
  210.3 6.8 %block.7 = (f32[64,1024]{1,0:T(8,128)S(1)}, f32[64,1024]{1,0:T(8,128)}, bf16[64,1024]{1,0:T(8,128)(2,1)S(1)}) custom-call(s32[2]{0:T(128)S(1)} %pad_add_fusion.2.place_ref, bf16[64,512]{1,0:T(8,128)(2,1)S(1)} %get-tuple-element.109.o_own, bf16[64,512]{1,0:T(8,128)(2,1)S(1)} %collective-permute-done.33.o_own_peer, ...), custom_call_target="tpu_custom_call" | custom-call | flops 4000000000 | bytes 8650752 | tf_op jit(solution)/shard_map/block/pallas_call | solution.py:148
  218.5 1.2 collective-permute-start.37
  220.6 2.4 place.13.refs_2_
  223.4 1.7 collective-permute-start.42
  225.1 2.9 %collective-permute-done.37 = f32[64,1024]{1,0:T(8,128)} collective-permute-done((f32[64,1024]{1,0:T(8,128)}, f32[64,1024]{1,0:T(8,128)}, u32[]{:S(2)}, u32[]{:S(2)}) %collective-permute-start.37) | collective-permute-done | bytes 262176 | tf_op jit(solution)/shard_map/ppermute | solution.py:295
  228.0 1.0 add_convert_fusion
  229.0 3.1 %collective-permute-done.30 = f32[64,1024]{1,0:T(8,128)S(1)} collective-permute-done((f32[64,1024]{1,0:T(8,128)}, f32[64,1024]{1,0:T(8,128)S(1)}, u32[]{:S(2)}, u32[]{:S(2)}) %collective-permute-start.30) | collective-permute-done | bytes 262176 | tf_op jit(solution)/shard_map/ppermute | solution.py:295
  232.4 17.5 %collective-permute-done.38 = bf16[32,1024]{1,0:T(8,128)(2,1)S(1)} collective-permute-done((bf16[32,1024]{1,0:T(8,128)(2,1)S(1)}, bf16[32,1024]{1,0:T(8,128)(2,1)S(1)}, u32[]{:S(2)}, u32[]{:S(2)}) %collective-permute-start.38) | collective-permute-done | bytes 65568 | tf_op jit(solution)/shard_map/ppermute | solution.py:295
  250.2 4.0 %collective-permute-done.31 = bf16[32,1024]{1,0:T(8,128)(2,1)S(1)} collective-permute-done((bf16[32,1024]{1,0:T(8,128)(2,1)S(1)}, bf16[32,1024]{1,0:T(8,128)(2,1)S(1)}, u32[]{:S(2)}, u32[]{:S(2)}) %collective-permute-start.31) | collective-permute-done | bytes 65568 | tf_op jit(solution)/shard_map/ppermute | solution.py:295
  255.0 3.4 %collective-permute-done.39 = bf16[32,1024]{1,0:T(8,128)(2,1)S(1)} collective-permute-done((bf16[32,1024]{1,0:T(8,128)(2,1)S(1)}, bf16[32,1024]{1,0:T(8,128)(2,1)S(1)}, u32[]{:S(2)}, u32[]{:S(2)}) %collective-permute-start.39) | collective-permute-done | bytes 65568 | tf_op jit(solution)/shard_map/ppermute | solution.py:295
  259.3 3.4 %collective-permute-done.32 = bf16[32,1024]{1,0:T(8,128)(2,1)S(1)} collective-permute-done((bf16[32,1024]{1,0:T(8,128)(2,1)S(1)}, bf16[32,1024]{1,0:T(8,128)(2,1)S(1)}, u32[]{:S(2)}, u32[]{:S(2)}) %collective-permute-start.32) | collective-permute-done | bytes 65568 | tf_op jit(solution)/shard_map/ppermute | solution.py:295
  263.5 2.1 place.14.refs_2_
  265.5 2.8 %place.15.refs_2_ = bf16[2,2,2,704,1024]{4,3,2,1,0:T(8,128)(2,1)} custom-call(s32[2,2]{1,0:T(2,128)S(1)} %pad_add_fusion.1.spots_ref, bf16[384,1024]{1,0:T(8,128)(2,1)} %collective-permute-done.44.refs_0_, bf16[384,1024]{1,0:T(8,128)(2,1)S(1)} %collective-permute-done.45.refs_1_, ...), custom_call_target="tpu_custom_call", output_to_operand_aliasing={{}: (3, {})} | custom-call | flops 2359296000 | bytes 3145728 | tf_op jit(solution)/shard_map/place/pallas_call | solution.py:58
  268.3 1.8 place.16.refs_2_
  270.2 1.6 place.17
  (138 shorter events, 23.8 us)
Async XLA Ops:
  0.6 27.1 %collective-permute-start.4 = (bf16[2,704,1024]{2,1,0:T(8,128)(2,1)}, bf16[2,704,1024]{2,1,0:T(8,128)(2,1)}, u32[]{:S(2)}, u32[]{:S(2)}) collective-permute-start(bf16[2,704,1024]{2,1,0:T(8,128)(2,1)} %bitcast.29), channel_id=1, source_target_pairs={{0,1},{1,0},{2,3},{3,2},{4,5},{5,4},{6,7},{7,6}} | collective-permute-start | bytes 8650760 | tf_op jit(solution)/shard_map/ppermute | solution.py:295
  1.5 11.8 %collective-permute-start = (bf16[128,1024]{1,0:T(8,128)(2,1)}, bf16[128,1024]{1,0:T(8,128)(2,1)S(1)}, u32[]{:S(2)}, u32[]{:S(2)}) collective-permute-start(bf16[128,1024]{1,0:T(8,128)(2,1)} %own_ref.1), channel_id=1, source_target_pairs={{0,2},{2,0},{1,3},{3,1},{4,6},{6,4},{5,7},{7,5}} | collective-permute-start | bytes 786440 | tf_op jit(solution)/shard_map/ppermute | solution.py:295
  4.0 9.3 %collective-permute-start.1 = (bf16[4,3,64,1024]{3,2,1,0:T(8,128)(2,1)}, bf16[4,3,64,1024]{3,2,1,0:T(8,128)(2,1)S(1)}, u32[]{:S(2)}, u32[]{:S(2)}) collective-permute-start(bf16[4,3,64,1024]{3,2,1,0:T(8,128)(2,1)} %bitcast.39), channel_id=1, source_target_pairs={{0,1},{1,0},{2,3},{3,2},{4,5},{5,4},{6,7},{7,6}} | collective-permute-start | bytes 4718600 | tf_op jit(solution)/shard_map/ppermute | solution.py:295
  4.2 7.1 %collective-permute-start.2 = (s32[128]{0:T(128)}, s32[128]{0:T(128)S(1)}, u32[]{:S(2)}, u32[]{:S(2)}) collective-permute-start(s32[128]{0:T(128)} %lens_ref.7), channel_id=1, source_target_pairs={{0,2},{2,0},{1,3},{3,1},{4,6},{6,4},{5,7},{7,5}} | collective-permute-start | bytes 1544 | tf_op jit(solution)/shard_map/ppermute | solution.py:295
  4.5 75.6 %collective-permute-start.8 = (bf16[1024,256]{1,0:T(8,128)(2,1)}, bf16[1024,256]{1,0:T(8,128)(2,1)}, u32[]{:S(2)}, u32[]{:S(2)}) collective-permute-start(bf16[1024,256]{1,0:T(8,128)(2,1)} %bitcast.48), channel_id=1, source_target_pairs={{0,1},{1,0},{2,3},{3,2},{4,5},{5,4},{6,7},{7,6}} | collective-permute-start | bytes 1572872 | tf_op jit(solution)/shard_map/ppermute | solution.py:295
  11.2 14.0 %collective-permute-start.9 = (bf16[1024,256]{1,0:T(8,128)(2,1)}, bf16[1024,256]{1,0:T(8,128)(2,1)}, u32[]{:S(2)}, u32[]{:S(2)}) collective-permute-start(bf16[1024,256]{1,0:T(8,128)(2,1)} %bitcast.49), channel_id=1, source_target_pairs={{0,4},{4,0},{1,5},{5,1},{2,6},{6,2},{3,7},{7,3}} | collective-permute-start | bytes 1572872 | tf_op jit(solution)/shard_map/ppermute | solution.py:295
  13.2 68.2 %collective-permute-start.11 = (bf16[704,1024]{1,0:T(8,128)(2,1)}, bf16[704,1024]{1,0:T(8,128)(2,1)}, u32[]{:S(2)}, u32[]{:S(2)}) collective-permute-start(bf16[704,1024]{1,0:T(8,128)(2,1)} %bitcast.43), channel_id=1, source_target_pairs={{0,1},{1,0},{2,3},{3,2},{4,5},{5,4},{6,7},{7,6}} | collective-permute-start | bytes 4325384 | tf_op jit(solution)/shard_map/ppermute | solution.py:295
  13.3 1.1 copy-start.14
  14.4 1.4 copy-start.1
  17.5 1.4 copy-start.15
  18.9 8.9 %copy-start = (bf16[1,1408,1024]{2,1,0:T(8,128)(2,1)S(1)}, bf16[1,1408,1024]{2,1,0:T(8,128)(2,1)}, u32[]{:S(2)}) copy-start(bf16[1,1408,1024]{2,1,0:T(8,128)(2,1)} %param.18) | copy-start | bytes 8650756
  20.1 12.8 %collective-permute-start.3 = (bf16[3,512,128]{2,1,0:T(8,128)(2,1)S(1)}, bf16[3,512,128]{2,1,0:T(8,128)(2,1)S(1)}, u32[]{:S(2)}, u32[]{:S(2)}) collective-permute-start(bf16[3,512,128]{2,1,0:T(8,128)(2,1)S(1)} %get-tuple-element.68), channel_id=1, source_target_pairs={{0,2},{2,0},{1,3},{3,1},{4,6},{6,4},{5,7},{7,5}} | collective-permute-start | bytes 1179656 | tf_op jit(solution)/shard_map/ppermute | solution.py:295
  25.2 56.3 %collective-permute-start.10 = (bf16[1024,256]{1,0:T(8,128)(2,1)}, bf16[1024,256]{1,0:T(8,128)(2,1)}, u32[]{:S(2)}, u32[]{:S(2)}) collective-permute-start(bf16[1024,256]{1,0:T(8,128)(2,1)} %collective-permute-done.9.wo_c), channel_id=1, source_target_pairs={{0,1},{1,0},{2,3},{3,2},{4,5},{5,4},{6,7},{7,6}} | collective-permute-start | bytes 1572872 | tf_op jit(solution)/shard_map/ppermute | solution.py:295
  27.8 5.2 %copy-start.13 = (s32[128]{0:T(128)S(1)}, s32[128]{0:T(128)}, u32[]{:S(2)}) copy-start(s32[128]{0:T(128)} %lens_ref.7) | copy-start | bytes 1540
  48.0 33.5 %copy-start.12 = (bf16[1,1024]{1,0:T(2,128)(2,1)S(1)}, bf16[1,1024]{1,0:T(2,128)(2,1)}, u32[]{:S(2)}) copy-start(bf16[1,1024]{1,0:T(2,128)(2,1)} %gain_ref.9) | copy-start | bytes 6148
  62.6 4.6 %collective-permute-start.20 = (bf16[64,512]{1,0:T(8,128)(2,1)S(1)}, bf16[64,512]{1,0:T(8,128)(2,1)}, u32[]{:S(2)}, u32[]{:S(2)}) collective-permute-start(bf16[64,512]{1,0:T(8,128)(2,1)S(1)} %get-tuple-element.90.o_own), channel_id=1, source_target_pairs={{0,4},{4,0},{1,5},{5,1},{2,6},{6,2},{3,7},{7,3}} | collective-permute-start | bytes 196616 | tf_op jit(solution)/shard_map/ppermute | solution.py:295
  64.1 5.5 %collective-permute-start.21 = (bf16[64,512]{1,0:T(8,128)(2,1)S(1)}, bf16[64,512]{1,0:T(8,128)(2,1)}, u32[]{:S(2)}, u32[]{:S(2)}) collective-permute-start(bf16[64,512]{1,0:T(8,128)(2,1)S(1)} %get-tuple-element.90.o_own), channel_id=1, source_target_pairs={{0,2},{2,0},{1,3},{3,1},{4,6},{6,4},{5,7},{7,5}} | collective-permute-start | bytes 196616 | tf_op jit(solution)/shard_map/ppermute | solution.py:295
  67.2 5.2 %collective-permute-start.22 = (bf16[64,512]{1,0:T(8,128)(2,1)S(1)}, bf16[64,512]{1,0:T(8,128)(2,1)S(1)}, u32[]{:S(2)}, u32[]{:S(2)}) collective-permute-start(bf16[64,512]{1,0:T(8,128)(2,1)S(1)} %get-tuple-element.90.o_own), channel_id=1, source_target_pairs={{0,6},{2,4},{4,2},{6,0},{1,7},{3,5},{5,3},{7,1}} | collective-permute-start | bytes 196616 | tf_op jit(solution)/shard_map/ppermute | solution.py:396
  69.6 4.5 %collective-permute-start.5 = (bf16[64,512]{1,0:T(8,128)(2,1)}, bf16[64,512]{1,0:T(8,128)(2,1)S(1)}, u32[]{:S(2)}, u32[]{:S(2)}) collective-permute-start(bf16[64,512]{1,0:T(8,128)(2,1)} %copy-done.19), channel_id=1, source_target_pairs={{0,4},{4,0},{1,5},{5,1},{2,6},{6,2},{3,7},{7,3}} | collective-permute-start | bytes 196616 | tf_op jit(solution)/shard_map/ppermute | solution.py:295
  72.4 4.9 %collective-permute-start.6 = (bf16[64,512]{1,0:T(8,128)(2,1)}, bf16[64,512]{1,0:T(8,128)(2,1)S(1)}, u32[]{:S(2)}, u32[]{:S(2)}) collective-permute-start(bf16[64,512]{1,0:T(8,128)(2,1)} %copy-done.19), channel_id=1, source_target_pairs={{0,2},{2,0},{1,3},{3,1},{4,6},{6,4},{5,7},{7,5}} | collective-permute-start | bytes 196616 | tf_op jit(solution)/shard_map/ppermute | solution.py:295
  74.1 5.4 %collective-permute-start.7 = (bf16[64,512]{1,0:T(8,128)(2,1)}, bf16[64,512]{1,0:T(8,128)(2,1)S(1)}, u32[]{:S(2)}, u32[]{:S(2)}) collective-permute-start(bf16[64,512]{1,0:T(8,128)(2,1)} %copy-done.19), channel_id=1, source_target_pairs={{0,6},{2,4},{4,2},{6,0},{1,7},{3,5},{5,3},{7,1}} | collective-permute-start | bytes 196616 | tf_op jit(solution)/shard_map/ppermute | solution.py:396
  77.3 21.7 %collective-permute-start.15 = (bf16[2,1024]{1,0:T(2,128)(2,1)S(1)}, bf16[2,1024]{1,0:T(2,128)(2,1)S(1)}, u32[]{:S(2)}, u32[]{:S(2)}) collective-permute-start(bf16[2,1024]{1,0:T(2,128)(2,1)S(1)} %pad_maximum_fusion.5), channel_id=1, source_target_pairs={{0,2},{2,0},{1,3},{3,1},{4,6},{6,4},{5,7},{7,5}} | collective-permute-start | bytes 12296 | tf_op jit(solution)/shard_map/ppermute | solution.py:295
  79.4 89.7 %collective-permute-start.48 = (bf16[160,1024]{1,0:T(8,128)(2,1)}, bf16[160,1024]{1,0:T(8,128)(2,1)}, u32[]{:S(2)}, u32[]{:S(2)}) collective-permute-start(bf16[160,1024]{1,0:T(8,128)(2,1)} %slice_bitcast_fusion), channel_id=1, source_target_pairs={{0,2},{2,0},{1,3},{3,1},{4,6},{6,4},{5,7},{7,5}} | collective-permute-start | bytes 983048 | tf_op jit(solution)/shard_map/ppermute | solution.py:295
  80.1 43.9 %collective-permute-start.18 = (bf16[2,3,64,1024]{3,2,1,0:T(8,128)(2,1)S(1)}, bf16[2,3,64,1024]{3,2,1,0:T(8,128)(2,1)S(1)}, u32[]{:S(2)}, u32[]{:S(2)}) collective-permute-start(bf16[2,3,64,1024]{3,2,1,0:T(8,128)(2,1)S(1)} %get-tuple-element.85), channel_id=1, source_target_pairs={{0,2},{2,0},{1,3},{3,1},{4,6},{6,4},{5,7},{7,5}} | collective-permute-start | bytes 2359304 | tf_op jit(solution)/shard_map/ppermute | solution.py:295
  81.5 1.4 copy-start.16
  82.9 1.0 copy-start.17
  90.8 8.8 %collective-permute-start.12 = (f32[64,1024]{1,0:T(8,128)S(1)}, f32[64,1024]{1,0:T(8,128)S(1)}, u32[]{:S(2)}, u32[]{:S(2)}) collective-permute-start(f32[64,1024]{1,0:T(8,128)S(1)} %get-tuple-element.81), channel_id=1, source_target_pairs={{0,4},{4,0},{1,5},{5,1},{2,6},{6,2},{3,7},{7,3}} | collective-permute-start | bytes 786440 | tf_op jit(solution)/shard_map/ppermute | solution.py:295
  98.3 6.4 %collective-permute-start.23 = (f32[64,1024]{1,0:T(8,128)S(1)}, f32[64,1024]{1,0:T(8,128)S(1)}, u32[]{:S(2)}, u32[]{:S(2)}) collective-permute-start(f32[64,1024]{1,0:T(8,128)S(1)} %get-tuple-element.97), channel_id=1, source_target_pairs={{0,4},{4,0},{1,5},{5,1},{2,6},{6,2},{3,7},{7,3}} | collective-permute-start | bytes 786440 | tf_op jit(solution)/shard_map/ppermute | solution.py:295
  99.0 26.0 %collective-permute-start.16 = (bf16[2,3,64,1024]{3,2,1,0:T(8,128)(2,1)S(1)}, bf16[2,3,64,1024]{3,2,1,0:T(8,128)(2,1)S(1)}, u32[]{:S(2)}, u32[]{:S(2)}) collective-permute-start(bf16[2,3,64,1024]{3,2,1,0:T(8,128)(2,1)S(1)} %get-tuple-element.83), channel_id=1, source_target_pairs={{0,2},{2,0},{1,3},{3,1},{4,6},{6,4},{5,7},{7,5}} | collective-permute-start | bytes 2359304 | tf_op jit(solution)/shard_map/ppermute | solution.py:295
  99.7 23.2 %collective-permute-start.13 = (bf16[32,1024]{1,0:T(8,128)(2,1)S(1)}, bf16[32,1024]{1,0:T(8,128)(2,1)S(1)}, u32[]{:S(2)}, u32[]{:S(2)}) collective-permute-start(bf16[32,1024]{1,0:T(8,128)(2,1)S(1)} %slice.87), channel_id=1, source_target_pairs={{0,2},{2,0},{1,3},{3,1},{4,6},{6,4},{5,7},{7,5}} | collective-permute-start | bytes 196616 | tf_op jit(solution)/shard_map/ppermute | solution.py:295
  104.7 19.3 %collective-permute-start.24 = (bf16[32,1024]{1,0:T(8,128)(2,1)S(1)}, bf16[32,1024]{1,0:T(8,128)(2,1)S(1)}, u32[]{:S(2)}, u32[]{:S(2)}) collective-permute-start(bf16[32,1024]{1,0:T(8,128)(2,1)S(1)} %slice.93), channel_id=1, source_target_pairs={{0,2},{2,0},{1,3},{3,1},{4,6},{6,4},{5,7},{7,5}} | collective-permute-start | bytes 196616 | tf_op jit(solution)/shard_map/ppermute | solution.py:295
  122.9 4.3 %collective-permute-start.14 = (bf16[32,1024]{1,0:T(8,128)(2,1)S(1)}, bf16[32,1024]{1,0:T(8,128)(2,1)S(1)}, u32[]{:S(2)}, u32[]{:S(2)}) collective-permute-start(bf16[32,1024]{1,0:T(8,128)(2,1)S(1)} %slice_select_fusion.3), channel_id=1, source_target_pairs={{0,4},{4,0},{1,5},{5,1},{2,6},{6,2},{3,7},{7,3}} | collective-permute-start | bytes 196616 | tf_op jit(solution)/shard_map/ppermute | solution.py:295
  124.0 4.6 %collective-permute-start.19 = (bf16[2,3,64,1024]{3,2,1,0:T(8,128)(2,1)S(1)}, bf16[2,3,64,1024]{3,2,1,0:T(8,128)(2,1)S(1)}, u32[]{:S(2)}, u32[]{:S(2)}) collective-permute-start(bf16[2,3,64,1024]{3,2,1,0:T(8,128)(2,1)S(1)} %collective-permute-done.18.refs_0_), channel_id=1, source_target_pairs={{0,1},{1,0},{2,3},{3,2},{4,5},{5,4},{6,7},{7,6}} | collective-permute-start | bytes 2359304 | tf_op jit(solution)/shard_map/ppermute | solution.py:295
  124.0 4.6 %collective-permute-start.25 = (bf16[32,1024]{1,0:T(8,128)(2,1)S(1)}, bf16[32,1024]{1,0:T(8,128)(2,1)S(1)}, u32[]{:S(2)}, u32[]{:S(2)}) collective-permute-start(bf16[32,1024]{1,0:T(8,128)(2,1)S(1)} %slice_select_fusion.2), channel_id=1, source_target_pairs={{0,4},{4,0},{1,5},{5,1},{2,6},{6,2},{3,7},{7,3}} | collective-permute-start | bytes 196616 | tf_op jit(solution)/shard_map/ppermute | solution.py:295
  125.0 5.6 %collective-permute-start.17 = (bf16[2,3,64,1024]{3,2,1,0:T(8,128)(2,1)S(1)}, bf16[2,3,64,1024]{3,2,1,0:T(8,128)(2,1)S(1)}, u32[]{:S(2)}, u32[]{:S(2)}) collective-permute-start(bf16[2,3,64,1024]{3,2,1,0:T(8,128)(2,1)S(1)} %collective-permute-done.16.refs_0_), channel_id=1, source_target_pairs={{0,1},{1,0},{2,3},{3,2},{4,5},{5,4},{6,7},{7,6}} | collective-permute-start | bytes 2359304 | tf_op jit(solution)/shard_map/ppermute | solution.py:295
  127.3 47.6 %collective-permute-start.29 = (bf16[64,1024]{1,0:T(8,128)(2,1)S(1)}, bf16[64,1024]{1,0:T(8,128)(2,1)S(1)}, u32[]{:S(2)}, u32[]{:S(2)}) collective-permute-start(bf16[64,1024]{1,0:T(8,128)(2,1)S(1)} %pad_maximum_fusion.1.rest_0_.hid_ref), channel_id=1, source_target_pairs={{0,2},{2,0},{1,3},{3,1},{4,6},{6,4},{5,7},{7,5}} | collective-permute-start | bytes 393224 | tf_op jit(solution)/shard_map/ppermute | solution.py:295
  149.0 23.1 %collective-permute-start.26 = (bf16[64,512]{1,0:T(8,128)(2,1)S(1)}, bf16[64,512]{1,0:T(8,128)(2,1)S(1)}, u32[]{:S(2)}, u32[]{:S(2)}) collective-permute-start(bf16[64,512]{1,0:T(8,128)(2,1)S(1)} %get-tuple-element.102.o_own), channel_id=1, source_target_pairs={{0,4},{4,0},{1,5},{5,1},{2,6},{6,2},{3,7},{7,3}} | collective-permute-start | bytes 196616 | tf_op jit(solution)/shard_map/ppermute | solution.py:295
  150.0 22.8 %collective-permute-start.27 = (bf16[64,512]{1,0:T(8,128)(2,1)S(1)}, bf16[64,512]{1,0:T(8,128)(2,1)S(1)}, u32[]{:S(2)}, u32[]{:S(2)}) collective-permute-start(bf16[64,512]{1,0:T(8,128)(2,1)S(1)} %get-tuple-element.102.o_own), channel_id=1, source_target_pairs={{0,2},{2,0},{1,3},{3,1},{4,6},{6,4},{5,7},{7,5}} | collective-permute-start | bytes 196616 | tf_op jit(solution)/shard_map/ppermute | solution.py:295
  150.9 23.2 %collective-permute-start.28 = (bf16[64,512]{1,0:T(8,128)(2,1)S(1)}, bf16[64,512]{1,0:T(8,128)(2,1)S(1)}, u32[]{:S(2)}, u32[]{:S(2)}) collective-permute-start(bf16[64,512]{1,0:T(8,128)(2,1)S(1)} %get-tuple-element.102.o_own), channel_id=1, source_target_pairs={{0,6},{2,4},{4,2},{6,0},{1,7},{3,5},{5,3},{7,1}} | collective-permute-start | bytes 196616 | tf_op jit(solution)/shard_map/ppermute | solution.py:396
  169.1 7.0 %collective-permute-start.33 = (bf16[64,512]{1,0:T(8,128)(2,1)S(1)}, bf16[64,512]{1,0:T(8,128)(2,1)S(1)}, u32[]{:S(2)}, u32[]{:S(2)}) collective-permute-start(bf16[64,512]{1,0:T(8,128)(2,1)S(1)} %get-tuple-element.109.o_own), channel_id=1, source_target_pairs={{0,4},{4,0},{1,5},{5,1},{2,6},{6,2},{3,7},{7,3}} | collective-permute-start | bytes 196616 | tf_op jit(solution)/shard_map/ppermute | solution.py:295
  172.0 53.0 %collective-permute-start.46 = (bf16[320,1024]{1,0:T(8,128)(2,1)}, bf16[320,1024]{1,0:T(8,128)(2,1)S(1)}, u32[]{:S(2)}, u32[]{:S(2)}) collective-permute-start(bf16[320,1024]{1,0:T(8,128)(2,1)} %slice.82), channel_id=1, source_target_pairs={{0,2},{2,0},{1,3},{3,1},{4,6},{6,4},{5,7},{7,5}} | collective-permute-start | bytes 1966088 | tf_op jit(solution)/shard_map/ppermute | solution.py:295
  172.9 50.5 %collective-permute-start.44 = (bf16[384,1024]{1,0:T(8,128)(2,1)}, bf16[384,1024]{1,0:T(8,128)(2,1)}, u32[]{:S(2)}, u32[]{:S(2)}) collective-permute-start(bf16[384,1024]{1,0:T(8,128)(2,1)} %slice.81), channel_id=1, source_target_pairs={{0,2},{2,0},{1,3},{3,1},{4,6},{6,4},{5,7},{7,5}} | collective-permute-start | bytes 2359304 | tf_op jit(solution)/shard_map/ppermute | solution.py:295
  174.1 36.3 %collective-permute-start.36 = (bf16[64,1024]{1,0:T(8,128)(2,1)S(1)}, bf16[64,1024]{1,0:T(8,128)(2,1)S(1)}, u32[]{:S(2)}, u32[]{:S(2)}) collective-permute-start(bf16[64,1024]{1,0:T(8,128)(2,1)S(1)} %pad_maximum_fusion.2.rest_0_.hid_ref), channel_id=1, source_target_pairs={{0,2},{2,0},{1,3},{3,1},{4,6},{6,4},{5,7},{7,5}} | collective-permute-start | bytes 393224 | tf_op jit(solution)/shard_map/ppermute | solution.py:295
  174.9 34.4 %collective-permute-start.34 = (bf16[64,512]{1,0:T(8,128)(2,1)S(1)}, bf16[64,512]{1,0:T(8,128)(2,1)S(1)}, u32[]{:S(2)}, u32[]{:S(2)}) collective-permute-start(bf16[64,512]{1,0:T(8,128)(2,1)S(1)} %get-tuple-element.109.o_own), channel_id=1, source_target_pairs={{0,2},{2,0},{1,3},{3,1},{4,6},{6,4},{5,7},{7,5}} | collective-permute-start | bytes 196616 | tf_op jit(solution)/shard_map/ppermute | solution.py:295
  176.1 34.2 %collective-permute-start.35 = (bf16[64,512]{1,0:T(8,128)(2,1)S(1)}, bf16[64,512]{1,0:T(8,128)(2,1)S(1)}, u32[]{:S(2)}, u32[]{:S(2)}) collective-permute-start(bf16[64,512]{1,0:T(8,128)(2,1)S(1)} %get-tuple-element.109.o_own), channel_id=1, source_target_pairs={{0,6},{2,4},{4,2},{6,0},{1,7},{3,5},{5,3},{7,1}} | collective-permute-start | bytes 196616 | tf_op jit(solution)/shard_map/ppermute | solution.py:396
  184.0 26.3 %copy-start.18 = (f32[64,1024]{1,0:T(8,128)}, f32[64,1024]{1,0:T(8,128)S(1)}, u32[]{:S(2)}) copy-start(f32[64,1024]{1,0:T(8,128)S(1)} %get-tuple-element.108) | copy-start | bytes 786436
  184.0 33.1 %copy-start.7 = (bf16[64,1024]{1,0:T(8,128)(2,1)}, bf16[64,1024]{1,0:T(8,128)(2,1)S(1)}, u32[]{:S(2)}) copy-start(bf16[64,1024]{1,0:T(8,128)(2,1)S(1)} %get-tuple-element.106) | copy-start | bytes 393220
  209.3 11.3 %collective-permute-start.49 = (bf16[160,1024]{1,0:T(8,128)(2,1)}, bf16[160,1024]{1,0:T(8,128)(2,1)}, u32[]{:S(2)}, u32[]{:S(2)}) collective-permute-start(bf16[160,1024]{1,0:T(8,128)(2,1)} %collective-permute-done.48.refs_0_), channel_id=1, source_target_pairs={{0,1},{1,0},{2,3},{3,2},{4,5},{5,4},{6,7},{7,6}} | collective-permute-start | bytes 983048 | tf_op jit(solution)/shard_map/ppermute | solution.py:295
  218.5 9.5 %collective-permute-start.37 = (f32[64,1024]{1,0:T(8,128)}, f32[64,1024]{1,0:T(8,128)}, u32[]{:S(2)}, u32[]{:S(2)}) collective-permute-start(f32[64,1024]{1,0:T(8,128)} %get-tuple-element.116), channel_id=1, source_target_pairs={{0,4},{4,0},{1,5},{5,1},{2,6},{6,2},{3,7},{7,3}} | collective-permute-start | bytes 786440 | tf_op jit(solution)/shard_map/ppermute | solution.py:295
  219.7 8.2 %copy-start.5 = (f32[64,1024]{1,0:T(8,128)S(1)}, f32[64,1024]{1,0:T(8,128)}, u32[]{:S(2)}) copy-start(f32[64,1024]{1,0:T(8,128)} %copy-done.4) | copy-start | bytes 786436
  219.7 8.2 %copy-start.10 = (bf16[64,1024]{1,0:T(8,128)(2,1)S(1)}, bf16[64,1024]{1,0:T(8,128)(2,1)}, u32[]{:S(2)}) copy-start(bf16[64,1024]{1,0:T(8,128)(2,1)} %copy-done.9) | copy-start | bytes 393220
  219.8 12.6 %copy-start.3 = (f32[64,1024]{1,0:T(8,128)S(1)}, f32[64,1024]{1,0:T(8,128)}, u32[]{:S(2)}) copy-start(f32[64,1024]{1,0:T(8,128)} %copy-done.2) | copy-start | bytes 786436
  219.8 12.6 %copy-start.8 = (bf16[64,1024]{1,0:T(8,128)(2,1)S(1)}, bf16[64,1024]{1,0:T(8,128)(2,1)}, u32[]{:S(2)}) copy-start(bf16[64,1024]{1,0:T(8,128)(2,1)} %copy-done.7) | copy-start | bytes 393220
  219.8 12.3 %collective-permute-start.30 = (f32[64,1024]{1,0:T(8,128)}, f32[64,1024]{1,0:T(8,128)S(1)}, u32[]{:S(2)}, u32[]{:S(2)}) collective-permute-start(f32[64,1024]{1,0:T(8,128)} %copy-done.18), channel_id=1, source_target_pairs={{0,4},{4,0},{1,5},{5,1},{2,6},{6,2},{3,7},{7,3}} | collective-permute-start | bytes 786440 | tf_op jit(solution)/shard_map/ppermute | solution.py:295
  223.0 40.4 %collective-permute-start.40 = (bf16[256,1024]{1,0:T(8,128)(2,1)S(1)}, bf16[256,1024]{1,0:T(8,128)(2,1)S(1)}, u32[]{:S(2)}, u32[]{:S(2)}) collective-permute-start(bf16[256,1024]{1,0:T(8,128)(2,1)S(1)} %slice.79), channel_id=1, source_target_pairs={{0,2},{2,0},{1,3},{3,1},{4,6},{6,4},{5,7},{7,5}} | collective-permute-start | bytes 1572872 | tf_op jit(solution)/shard_map/ppermute | solution.py:295
  223.4 35.9 %collective-permute-start.42 = (bf16[288,1024]{1,0:T(8,128)(2,1)S(1)}, bf16[288,1024]{1,0:T(8,128)(2,1)S(1)}, u32[]{:S(2)}, u32[]{:S(2)}) collective-permute-start(bf16[288,1024]{1,0:T(8,128)(2,1)S(1)} %slice.80), channel_id=1, source_target_pairs={{0,2},{2,0},{1,3},{3,1},{4,6},{6,4},{5,7},{7,5}} | collective-permute-start | bytes 1769480 | tf_op jit(solution)/shard_map/ppermute | solution.py:295
  225.1 40.5 %collective-permute-start.45 = (bf16[384,1024]{1,0:T(8,128)(2,1)}, bf16[384,1024]{1,0:T(8,128)(2,1)S(1)}, u32[]{:S(2)}, u32[]{:S(2)}) collective-permute-start(bf16[384,1024]{1,0:T(8,128)(2,1)} %collective-permute-done.44.refs_0_), channel_id=1, source_target_pairs={{0,1},{1,0},{2,3},{3,2},{4,5},{5,4},{6,7},{7,6}} | collective-permute-start | bytes 2359304 | tf_op jit(solution)/shard_map/ppermute | solution.py:295
  227.9 35.5 %collective-permute-start.47 = (bf16[320,1024]{1,0:T(8,128)(2,1)S(1)}, bf16[320,1024]{1,0:T(8,128)(2,1)S(1)}, u32[]{:S(2)}, u32[]{:S(2)}) collective-permute-start(bf16[320,1024]{1,0:T(8,128)(2,1)S(1)} %collective-permute-done.46.refs_0_), channel_id=1, source_target_pairs={{0,1},{1,0},{2,3},{3,2},{4,5},{5,4},{6,7},{7,6}} | collective-permute-start | bytes 1966088 | tf_op jit(solution)/shard_map/ppermute | solution.py:295
  232.1 17.9 %collective-permute-start.38 = (bf16[32,1024]{1,0:T(8,128)(2,1)S(1)}, bf16[32,1024]{1,0:T(8,128)(2,1)S(1)}, u32[]{:S(2)}, u32[]{:S(2)}) collective-permute-start(bf16[32,1024]{1,0:T(8,128)(2,1)S(1)} %slice.97), channel_id=1, source_target_pairs={{0,2},{2,0},{1,3},{3,1},{4,6},{6,4},{5,7},{7,5}} | collective-permute-start | bytes 196616 | tf_op jit(solution)/shard_map/ppermute | solution.py:295
  249.9 4.3 %collective-permute-start.31 = (bf16[32,1024]{1,0:T(8,128)(2,1)S(1)}, bf16[32,1024]{1,0:T(8,128)(2,1)S(1)}, u32[]{:S(2)}, u32[]{:S(2)}) collective-permute-start(bf16[32,1024]{1,0:T(8,128)(2,1)S(1)} %slice.95), channel_id=1, source_target_pairs={{0,2},{2,0},{1,3},{3,1},{4,6},{6,4},{5,7},{7,5}} | collective-permute-start | bytes 196616 | tf_op jit(solution)/shard_map/ppermute | solution.py:295
  254.2 4.3 %collective-permute-start.39 = (bf16[32,1024]{1,0:T(8,128)(2,1)S(1)}, bf16[32,1024]{1,0:T(8,128)(2,1)S(1)}, u32[]{:S(2)}, u32[]{:S(2)}) collective-permute-start(bf16[32,1024]{1,0:T(8,128)(2,1)S(1)} %slice_select_fusion), channel_id=1, source_target_pairs={{0,4},{4,0},{1,5},{5,1},{2,6},{6,2},{3,7},{7,3}} | collective-permute-start | bytes 196616 | tf_op jit(solution)/shard_map/ppermute | solution.py:295
  258.4 4.3 %collective-permute-start.32 = (bf16[32,1024]{1,0:T(8,128)(2,1)S(1)}, bf16[32,1024]{1,0:T(8,128)(2,1)S(1)}, u32[]{:S(2)}, u32[]{:S(2)}) collective-permute-start(bf16[32,1024]{1,0:T(8,128)(2,1)S(1)} %slice_select_fusion.1), channel_id=1, source_target_pairs={{0,4},{4,0},{1,5},{5,1},{2,6},{6,2},{3,7},{7,3}} | collective-permute-start | bytes 196616 | tf_op jit(solution)/shard_map/ppermute | solution.py:295
  259.3 9.0 %collective-permute-start.43 = (bf16[288,1024]{1,0:T(8,128)(2,1)S(1)}, bf16[288,1024]{1,0:T(8,128)(2,1)S(1)}, u32[]{:S(2)}, u32[]{:S(2)}) collective-permute-start(bf16[288,1024]{1,0:T(8,128)(2,1)S(1)} %collective-permute-done.42.refs_0_), channel_id=1, source_target_pairs={{0,1},{1,0},{2,3},{3,2},{4,5},{5,4},{6,7},{7,6}} | collective-permute-start | bytes 1769480 | tf_op jit(solution)/shard_map/ppermute | solution.py:295
  263.5 6.7 %collective-permute-start.41 = (bf16[256,1024]{1,0:T(8,128)(2,1)S(1)}, bf16[256,1024]{1,0:T(8,128)(2,1)S(1)}, u32[]{:S(2)}, u32[]{:S(2)}) collective-permute-start(bf16[256,1024]{1,0:T(8,128)(2,1)S(1)} %collective-permute-done.40.refs_0_), channel_id=1, source_target_pairs={{0,1},{1,0},{2,3},{3,2},{4,5},{5,4},{6,7},{7,6}} | collective-permute-start | bytes 1572872 | tf_op jit(solution)/shard_map/ppermute | solution.py:295
  (7 other events, 5.2 us)

commit v4 on v3

--- a/solution.py
+++ b/solution.py
@@ -11,9 +11,9 @@
 ROPE_THETA = 500000.0
 NORM_EPS = 1e-5
 MASK_FILL = -1e30
-UNROLL = 16
+PER = 8
 PARTS = 2
-GU_CUTS = (0, 10, 30, 54, 72, 88)
+GU_CUTS = (0, 10, 34, 76, 88)
 ROW_AXES = ("pp", "grp")
 TRAIN_AXES = ("tg", "grp")
 SWAP = ((0, 1), (1, 0))
@@ -157,39 +157,49 @@
     )(spot, *o_vals, hid, away, gain, *w_o, *gus, *downs)
 
 
-def attn_kernel(lens_ref, *rest, heads, head_dim, scale, row0, ready):
+def attn_kernel(lens_ref, *rest, heads, head_dim, scale, row0, ready, layer, per):
     heads_in, rest = rest[:1 if ready else 5], rest[1 if ready else 5:]
-    k_ref, v_ref = rest[:2]
+    k_hbm, v_hbm = rest[:2]
     if not ready:
-        rest = rest[:-6] + rest[-5:]
-    o_ref, ko_ref, vo_ref, q_s, kt_s, vt_s, o_s, p_s = rest[-8:]
+        w_s, w_sem = rest[-2:]
+        rest = rest[:-11] + rest[-10:-2]
+    o_ref, ko_hbm, vo_hbm, q_s, kt_s, vt_s, p_s, k_buf, v_buf, sem_in, sem_out = rest[-11:]
     rows = heads * head_dim
-    per = k_ref.shape[1]
-    seq = k_ref.shape[-1]
-    batch = seq
-    step = pl.program_id(0)
-
-    @pl.when(step == 0)
-    def _():
-        if ready:
-            for t, ref in enumerate((None, kt_s, vt_s)):
-                vals = heads_in[0][t].astype(F32)
-                if t:
-                    ref[...] = vals
-                else:
-                    q_s[...] = vals.T
-            return
-        h_ref, gain_ref, w_ref, cos_ref, sin_ref = heads_in
+    count, seq = k_buf.shape[0], k_buf.shape[-1]
+    blocks = count // per
+
+    def moves(blk, out):
+        here = pl.ds(blk * per, per)
+        there = (layer, pl.ds(row0 + blk * per, per))
+        for t, (src, buf, dst) in enumerate(((k_hbm, k_buf, ko_hbm), (v_hbm, v_buf, vo_hbm))):
+            if out:
+                yield pltpu.make_async_copy(buf.at[here], dst.at[there], sem_out.at[t, blk])
+            else:
+                yield pltpu.make_async_copy(src.at[there], buf.at[here], sem_in.at[t, blk])
+
+    if not ready:
+        fetch = pltpu.make_async_copy(heads_in[2].at[layer], w_s, w_sem)
+        fetch.start()
+    for blk in range(blocks):
+        for move in moves(blk, False):
+            move.start()
+
+    if ready:
+        q_s[...] = heads_in[0][0].astype(F32).T
+        kt_s[...] = heads_in[0][1].astype(F32)
+        vt_s[...] = heads_in[0][2].astype(F32)
+    else:
+        h_ref, gain_ref, _, cos_ref, sin_ref = heads_in
         normed = rms_norm(h_ref[...], gain_ref[...])
-        normed = jnp.concatenate([normed] * (batch // h_ref.shape[0]), axis=0)
-
+        normed = jnp.concatenate([normed] * (seq // count), axis=0)
+        fetch.wait()
 
         def proj(t, turn):
-            vals = lax.dot_general(w_ref[0, t * rows:(t + 1) * rows, :], normed, (((1,), (1,)), ((), ())),
+            vals = lax.dot_general(w_s[t * rows:(t + 1) * rows, :], normed, (((1,), (1,)), ((), ())),
                                    preferred_element_type=F32)
             if turn:
-                vals = rope_t(vals.reshape(heads, head_dim, batch), cos_ref[...], sin_ref[...])
-            return vals.reshape(rows, batch).astype(BF16).astype(F32)
+                vals = rope_t(vals.reshape(heads, head_dim, seq), cos_ref[...], sin_ref[...])
+            return vals.reshape(rows, seq).astype(BF16).astype(F32)
 
         q_s[...] = proj(0, True).T
         kt_s[...] = proj(1, True)
@@ -199,77 +209,75 @@
     head_of = lax.broadcasted_iota(jnp.int32, (heads, rows), 1) // head_dim
     mine = head_of == lax.broadcasted_iota(jnp.int32, (heads, rows), 0)
 
-    def insert(i, carry):
-        b = row0 + step * per + i
-        n = lens_ref[b]
-        shift = lax.rem(n - b + seq, seq)
-        at_n = jnp.broadcast_to(lane == n, (rows, seq))
-        k_new = pltpu.roll(kt_s[...], shift, 1).astype(BF16)
-        v_new = pltpu.roll(vt_s[...], shift, 1).astype(BF16)
-        k_all = jnp.where(at_n, k_new, k_ref[0, i].reshape(rows, seq))
-        v_all = jnp.where(at_n, v_new, v_ref[0, i].reshape(rows, seq))
-        ko_ref[0, i] = k_all.reshape(heads, head_dim, seq)
-        vo_ref[0, i] = v_all.reshape(heads, head_dim, seq)
-        q_diag = jnp.where(mine, q_s[pl.ds(b, 1), :], 0.0).astype(BF16)
-        scores = jnp.dot(q_diag, k_all, preferred_element_type=F32) * scale
-        p_s[pl.ds(pl.multiple_of(i * heads, heads), heads), :] = jnp.where(lane <= n, scores, MASK_FILL)
+    def one_block(blk, carry):
+        for move in moves(blk, False):
+            move.wait()
+        for i in range(per):
+            r = blk * per + i
+            b = row0 + r
+            n = lens_ref[b]
+            shift = lax.rem(n - b + seq, seq)
+            at_n = jnp.broadcast_to(lane == n, (rows, seq))
+            k_new = pltpu.roll(kt_s[...], shift, 1).astype(BF16)
+            v_new = pltpu.roll(vt_s[...], shift, 1).astype(BF16)
+            k_all = jnp.where(at_n, k_new, k_buf[r].reshape(rows, seq))
+            v_all = jnp.where(at_n, v_new, v_buf[r].reshape(rows, seq))
+            k_buf[r] = k_all.reshape(heads, head_dim, seq)
+            v_buf[r] = v_all.reshape(heads, head_dim, seq)
+            q_diag = jnp.where(mine, q_s[pl.ds(b, 1), :], 0.0).astype(BF16)
+            scores = jnp.dot(q_diag, k_all, preferred_element_type=F32) * scale
+            p_s[i * heads:(i + 1) * heads, :] = jnp.where(lane <= n, scores, MASK_FILL)
+        for move in moves(blk, True):
+            move.start()
+        scores = p_s[...]
+        expd = jnp.exp(scores - jnp.max(scores, axis=-1, keepdims=True))
+        probs = (expd / jnp.sum(expd, axis=-1, keepdims=True)).astype(BF16).astype(F32)
+        outs = []
+        for i in range(per):
+            out = lax.dot_general(probs[i * heads:(i + 1) * heads].astype(BF16), v_buf[blk * per + i].reshape(rows, seq),
+                                  (((1,), (1,)), ((), ())), preferred_element_type=F32)
+            outs.append(jnp.sum(jnp.where(mine, out, 0.0), axis=0, keepdims=True))
+        o_ref[pl.ds(pl.multiple_of(blk * per, per), per), :] = jnp.concatenate(outs, axis=0).astype(BF16)
         return carry
 
-    lax.fori_loop(0, per, insert, 0, unroll=UNROLL)
-    scores = p_s[...]
-    expd = jnp.exp(scores - jnp.max(scores, axis=-1, keepdims=True))
-    p_s[...] = (expd / jnp.sum(expd, axis=-1, keepdims=True)).astype(BF16).astype(F32)
-
-    def combine(i, carry):
-        probs = p_s[pl.ds(pl.multiple_of(i * heads, heads), heads), :].astype(BF16)
-        outs = lax.dot_general(probs, vo_ref[0, i].reshape(rows, seq), (((1,), (1,)), ((), ())),
-                               preferred_element_type=F32)
-        o_s[pl.ds(i, 1), :] = jnp.sum(jnp.where(mine, outs, 0.0), axis=0, keepdims=True)
-        return carry
-
-    lax.fori_loop(0, per, combine, 0, unroll=UNROLL)
-    o_ref[...] = o_s[...].astype(BF16)
+    lax.fori_loop(0, blocks, one_block, 0)
+    for blk in range(blocks):
+        for move in moves(blk, True):
+            move.wait()
 
 
 def attention(layer, part, parts, heads_in, seq_lens, kc, vc, outs):
     _, batch, heads, head_dim, seq = kc.shape
     rows = heads * head_dim
     count = batch // parts
+    per = PER
     ready = len(heads_in) == 1
-    per = 16
-    first = part * count // per
-    whole = lambda *shape: pl.BlockSpec(shape, lambda s, n: (0,) * len(shape))
-    cache_block = pl.BlockSpec((1, per, heads, head_dim, seq), lambda s, n: (layer, first + s, 0, 0, 0))
-    if ready:
-        in_specs = [whole(3, rows, seq)]
-    else:
-        model = heads_in[0].shape[1]
-        in_specs = [whole(count, model), whole(1, model), pl.BlockSpec((1, 3 * rows, model), lambda s, n: (layer, 0, 0)),
-                    whole(head_dim // 2, seq), whole(head_dim // 2, seq)]
-    in_specs += [cache_block, cache_block]
+    vmem, hbm = pl.BlockSpec(memory_space=pltpu.VMEM), pl.BlockSpec(memory_space=pl.ANY)
+    in_specs = [pl.BlockSpec(memory_space=pltpu.SMEM)] + (
+        [vmem] if ready else [vmem, vmem, hbm, vmem, vmem]) + [hbm, hbm]
     args = [seq_lens, *heads_in, kc, vc]
     aliases = {}
     if outs is not None:
-        in_specs += [pl.BlockSpec(memory_space=pl.ANY)] * 2
+        in_specs += [hbm, hbm]
         args += list(outs)
         aliases = {len(args) - 2: 1, len(args) - 1: 2}
+    scratch = [pltpu.VMEM((seq, rows), F32), pltpu.VMEM((rows, seq), F32), pltpu.VMEM((rows, seq), F32),
+               pltpu.VMEM((per * heads, seq), F32), pltpu.VMEM((count, heads, head_dim, seq), BF16),
+               pltpu.VMEM((count, heads, head_dim, seq), BF16),
+               pltpu.SemaphoreType.DMA((2, count // per)), pltpu.SemaphoreType.DMA((2, count // per))]
+    w_out = []
     if not ready:
         aliases[3] = 3
-    w_out = [] if ready else [jax.ShapeDtypeStruct(heads_in[2].shape, BF16)]
+        w_out = [jax.ShapeDtypeStruct(heads_in[2].shape, BF16)]
+        scratch += [pltpu.VMEM(heads_in[2].shape[1:], BF16), pltpu.SemaphoreType.DMA]
     cache_shape = jax.ShapeDtypeStruct(kc.shape, kc.dtype)
     return pl.pallas_call(
         functools.partial(attn_kernel, heads=heads, head_dim=head_dim, scale=head_dim ** -0.5, row0=part * count,
-                          ready=ready),
-        grid_spec=pltpu.PrefetchScalarGridSpec(
-            num_scalar_prefetch=1, grid=(count // per,), in_specs=in_specs,
-            out_specs=[pl.BlockSpec((per, rows), lambda s, n: (s, 0)), cache_block, cache_block] + [
-                pl.BlockSpec(memory_space=pl.ANY)] * len(w_out),
-            scratch_shapes=[pltpu.VMEM((seq, rows), F32), pltpu.VMEM((rows, seq), F32),
-                            pltpu.VMEM((rows, seq), F32), pltpu.VMEM((per, rows), F32),
-                            pltpu.VMEM((per * heads, seq), F32)]),
+                          ready=ready, layer=layer, per=per),
+        in_specs=in_specs, out_specs=[vmem, hbm, hbm] + [hbm] * len(w_out), scratch_shapes=scratch,
         out_shape=[jax.ShapeDtypeStruct((count, rows), BF16), cache_shape, cache_shape] + w_out,
         input_output_aliases=aliases,
-        compiler_params=pltpu.CompilerParams(dimension_semantics=("arbitrary",), vmem_limit_bytes=28 << 20),
+        compiler_params=pltpu.CompilerParams(vmem_limit_bytes=28 << 20),
         cost_estimate=pl.CostEstimate(flops=30_000_000_000 // parts, bytes_accessed=kc.size * 4 // parts,
                                       transcendentals=0),
     )(*args)
@@ -390,8 +398,6 @@
                     gen_qkv = caches.pop()
                 if layer == 0 and i == 0:
                     far_heads.append(qkv_send(1, o_part))
-                if layer == 1 and i == 0:
-                    sent.append(gu_send(3, o_part))
                 o_vals.append((o_part, swap(o_part, "tg"), swap(o_part, "pp"),
                                lax.ppermute(o_part, ("tg", "pp"), ((0, 3), (1, 2), (2, 1), (3, 0)))))
             last = o_vals[1][0]
@@ -401,11 +407,11 @@
                     gen_qkv = qkv_take(i, far_heads[i], gen_qkv)
                 sent.append(gu_send(1, last))
             else:
-                for c in (1, 2, 3):
+                for c in (1, 2):
                     sent[c] = after(sent[c], last)
                     gen_gu = gu_take(c, sent[c], gen_gu)
-                sent.append(gu_send(4, last))
-                gen_gu = gu_take(4, sent[4], gen_gu)
+                sent.append(gu_send(3, last))
+                gen_gu = gu_take(3, sent[3], gen_gu)
             backs, owns = [], []
             give = None
             for i in range(PARTS):

time: 273 us -> 235 us (0.86)
  waiting for transfers between devices: 96.2 us -> 58.6 us
    ppermute x46 -> x44, waiting for transfers between devices: 91.9 us -> 54 us  [swap(): return lax.ppermute(x, axis, SWAP)]
    ppermute x46 -> x44, starting transfers between devices: 36 us -> 39.9 us  [swap(): return lax.ppermute(x, axis, SWAP)]
    pallas_call x9 -> x8, Pallas kernels: 22.1 us -> 21.1 us  [place(): pl.pallas_call(functools.partial(place_kernel, count=count, blocks=blocks...]
    unnamed x42 -> x48, local copies, waits for them, and re-layouts: 11.6 us -> 11.1 us
  transfers between devices with their start and end apart: 50 -> 48, of which waited for: 19 -> 19; matrix products, arithmetic and copies ran while one was open for 4% -> 4% of each run, Pallas kernels for 40% -> 45%
where the time goes in v4:
time: 235 us
  Pallas kernels  108 us (46%)
  waiting for transfers between devices  58.6 us (25%)
  starting transfers between devices  45.2 us (19%)
  local copies, waits for them, and re-layouts  17.6 us (7%)
  other arithmetic  4.01 us (2%)
    pallas_call x4, Pallas kernels, attention(): pl.pallas_call(functools.partial(attn_kernel, heads=heads, head_dim=head_...  61 us
    ppermute x44, waiting for transfers between devices, swap(): return lax.ppermute(x, axis, SWAP)  54 us
    ppermute x44, starting transfers between devices, swap(): return lax.ppermute(x, axis, SWAP)  39.9 us
    pallas_call x4, Pallas kernels, block(): pl.pallas_call(block_kernel, in_specs=[pl.BlockSpec(memory_space=pltpu.SM...  24.8 us
    pallas_call x8, Pallas kernels, place(): pl.pallas_call(functools.partial(place_kernel, count=count, blocks=blocks...  21.1 us
    unnamed x48, local copies, waits for them, and re-layouts  11.1 us
    ppermute x4, starting transfers between devices, decode(): lax.ppermute(o_part, ('tg', 'pp'), ((0, 3), (1, 2), (2, 1), (3, 0)))  5.34 us
  transfers between devices with their start and end apart: 48, of which 19 were waited for; matrix products, arithmetic and copies ran while one was open for 4% of the time, Pallas kernels for 45%

profile of v4, /device:TPU:0, one launch (start us, length us, event | category | flops | bytes accessed | tf_op | source)
XLA Modules:
  0.0 234.8 jit_solution(13715559717992333998)
XLA Ops:
  1.5 2.5 %collective-permute-start = (bf16[128,1024]{1,0:T(8,128)(2,1)}, bf16[128,1024]{1,0:T(8,128)(2,1)S(1)}, u32[]{:S(2)}, u32[]{:S(2)}) collective-permute-start(bf16[128,1024]{1,0:T(8,128)(2,1)} %own_ref.1), channel_id=1, source_target_pairs={{0,2},{2,0},{1,3},{3,1},{4,6},{6,4},{5,7},{7,5}} | collective-permute-start | bytes 786440 | tf_op jit(solution)/shard_map/ppermute | solution.py:303
  5.6 1.0 fusion.2
  6.5 1.8 slice_bitcast_fusion
  9.0 2.3 collective-permute-done.2
  11.2 1.8 collective-permute-start.9
  13.3 2.0 copy-done.1
  15.3 0.9 copy-done.6
  16.9 1.2 project.1
  18.1 1.5 collective-permute-start.3
  19.6 5.6 %collective-permute-done.9.wo_c = bf16[1024,256]{1,0:T(8,128)(2,1)} collective-permute-done((bf16[1024,256]{1,0:T(8,128)(2,1)}, bf16[1024,256]{1,0:T(8,128)(2,1)}, u32[]{:S(2)}, u32[]{:S(2)}) %collective-permute-start.9) | collective-permute-done | bytes 524320 | tf_op jit(solution)/shard_map/ppermute | solution.py:303
  25.2 1.5 copy-done.16
  26.8 2.5 %place.8.refs_2_ = bf16[2,3,2,4,64,1024]{5,4,3,2,1,0:T(8,128)(2,1)} custom-call(s32[2,2]{1,0:T(2,128)S(1)} %pad_add_fusion.spots_ref, bf16[4,3,64,1024]{3,2,1,0:T(8,128)(2,1)S(1)} %bitcast.41, bf16[4,3,64,1024]{3,2,1,0:T(8,128)(2,1)S(1)} %copy-done.16), custom_call_target="tpu_custom_call" | custom-call | flops 4718592000 | bytes 6291456 | tf_op jit(solution)/shard_map/place/pallas_call | solution.py:58
  29.3 5.1 %place.9.refs_2_ = bf16[2,2,2,704,1024]{4,3,2,1,0:T(8,128)(2,1)} custom-call(s32[2,2]{1,0:T(2,128)S(1)} %pad_add_fusion.spots_ref, bf16[1408,1024]{1,0:T(8,128)(2,1)S(1)} %bitcast.30, bf16[1408,1024]{1,0:T(8,128)(2,1)} %bitcast.9.refs_1_), custom_call_target="tpu_custom_call" | custom-call | flops 8650752000 | bytes 11534336 | tf_op jit(solution)/shard_map/place/pallas_call | solution.py:58
  34.5 13.0 %shard_map.137 = (bf16[64,512]{1,0:T(8,128)(2,1)S(1)}, bf16[2,128,8,64,128]{4,3,2,1,0:T(8,128)(2,1)}, bf16[2,128,8,64,128]{4,3,2,1,0:T(8,128)(2,1)}) custom-call(s32[128]{0:T(128)S(1)} %copy-done.14, bf16[3,512,128]{2,1,0:T(8,128)(2,1)S(1)} %broadcast_select_fusion.rest_0_, bf16[2,128,8,64,128]{4,3,2,1,0:T(8,128)(2,1)} %bitcast.53, ...), custom_call_target="tpu_custom_call" | custom-call | flops 15000000512 | bytes 33554432 | tf_op jit(solution)/shard_map/pallas_call | solution.py:274
  48.2 13.0 %shard_map.138 = (bf16[64,512]{1,0:T(8,128)(2,1)S(1)}, bf16[2,128,8,64,128]{4,3,2,1,0:T(8,128)(2,1)}, bf16[2,128,8,64,128]{4,3,2,1,0:T(8,128)(2,1)}) custom-call(s32[128]{0:T(128)S(1)} %copy-done.14, bf16[3,512,128]{2,1,0:T(8,128)(2,1)S(1)} %broadcast_select_fusion.rest_0_, ...), custom_call_target="tpu_custom_call", output_to_operand_aliasing={{1}: (4, {}), {2}: (5, {})} | custom-call | flops 15000000512 | bytes 33554432 | tf_op jit(solution)/shard_map/pallas_call | solution.py:274
  61.2 1.5 collective-permute-start.20
  62.7 1.5 collective-permute-start.21
  64.2 1.4 collective-permute-done.20.o_own_peer
  65.6 2.4 %collective-permute-start.22 = (bf16[64,512]{1,0:T(8,128)(2,1)S(1)}, bf16[64,512]{1,0:T(8,128)(2,1)S(1)}, u32[]{:S(2)}, u32[]{:S(2)}) collective-permute-start(bf16[64,512]{1,0:T(8,128)(2,1)S(1)} %get-tuple-element.88.o_own), channel_id=1, source_target_pairs={{0,6},{2,4},{4,2},{6,0},{1,7},{3,5},{5,3},{7,1}} | collective-permute-start | bytes 196616 | tf_op jit(solution)/shard_map/ppermute | solution.py:402
  68.6 2.3 collective-permute-done.22.o_away_peer
  70.9 1.4 collective-permute-start.6
  72.5 1.2 collective-permute-start.7
  73.8 1.5 fusion
  75.6 1.3 collective-permute-start.15
  76.9 1.0 collective-permute-done.7.o_away_peer
  78.6 1.4 collective-permute-start.18
  80.0 1.4 copy-done.17
  81.3 1.0 copy-done.18
  83.2 6.0 %block.4 = (f32[64,1024]{1,0:T(8,128)S(1)}, f32[64,1024]{1,0:T(8,128)S(1)}, bf16[64,1024]{1,0:T(8,128)(2,1)S(1)}) custom-call(s32[2]{0:T(128)S(1)} %pad_add_fusion.2.place_ref, bf16[64,512]{1,0:T(8,128)(2,1)S(1)} %copy-done.23, bf16[64,512]{1,0:T(8,128)(2,1)S(1)} %collective-permute-done.5.o_own_peer, bf16[64,512]{1,0:T(8,128)(2,1)S(1)} %collective-permute-done.6.o_away, ...), custom_call_target="tpu_custom_call" | custom-call | flops 4000000000 | bytes 8650752 | tf_op jit(solution)/shard_map/block/pallas_call | solution.py:148
  89.3 1.4 collective-permute-start.12
  90.6 6.1 %block.5 = (f32[64,1024]{1,0:T(8,128)S(1)}, f32[64,1024]{1,0:T(8,128)S(1)}, bf16[64,1024]{1,0:T(8,128)(2,1)S(1)}) custom-call(s32[2]{0:T(128)S(1)} %pad_add_fusion.2.place_ref, bf16[64,512]{1,0:T(8,128)(2,1)S(1)} %copy-done.21, bf16[64,512]{1,0:T(8,128)(2,1)} %collective-permute-done.20.o_own_peer, bf16[64,512]{1,0:T(8,128)(2,1)} %collective-permute-done.21.o_away, ...), custom_call_target="tpu_custom_call" | custom-call | flops 4000000000 | bytes 8650752 | tf_op jit(solution)/shard_map/block/pallas_call | solution.py:148
  97.4 1.2 slice.77
  99.3 1.4 collective-permute-start.13
  100.8 2.4 %collective-permute-done.23 = f32[64,1024]{1,0:T(8,128)S(1)} collective-permute-done((f32[64,1024]{1,0:T(8,128)S(1)}, f32[64,1024]{1,0:T(8,128)S(1)}, u32[]{:S(2)}, u32[]{:S(2)}) %collective-permute-start.23) | collective-permute-done | bytes 262176 | tf_op jit(solution)/shard_map/ppermute | solution.py:303
  103.6 17.8 %collective-permute-done.13 = bf16[32,1024]{1,0:T(8,128)(2,1)S(1)} collective-permute-done((bf16[32,1024]{1,0:T(8,128)(2,1)S(1)}, bf16[32,1024]{1,0:T(8,128)(2,1)S(1)}, u32[]{:S(2)}, u32[]{:S(2)}) %collective-permute-start.13) | collective-permute-done | bytes 65568 | tf_op jit(solution)/shard_map/ppermute | solution.py:303
  122.2 1.4 collective-permute-start.25
  123.8 2.3 collective-permute-done.14
  127.5 1.9 place.10.refs_2_
  129.4 1.9 place.11
  131.3 17.5 %shard_map.139 = (bf16[64,512]{1,0:T(8,128)(2,1)S(1)}, bf16[2,128,8,64,128]{4,3,2,1,0:T(8,128)(2,1)}, bf16[2,128,8,64,128]{4,3,2,1,0:T(8,128)(2,1)}, bf16[2,1536,1024]{2,1,0:T(8,128)(2,1)}) custom-call(s32[128]{0:T(128)S(1)} %copy-done.14, ...), custom_call_target="tpu_custom_call", output_to_operand_aliasing={{1}: (8, {}), {2}: (9, {}), {3}: (3, {})} | custom-call | flops 15000000512 | bytes 33554432 | tf_op jit(solution)/shard_map/pallas_call | solution.py:274
  148.8 0.9 collective-permute-start.26
  149.7 1.7 collective-permute-start.27
  152.3 17.5 %shard_map.140 = (bf16[64,512]{1,0:T(8,128)(2,1)S(1)}, bf16[2,128,8,64,128]{4,3,2,1,0:T(8,128)(2,1)}, bf16[2,128,8,64,128]{4,3,2,1,0:T(8,128)(2,1)}, bf16[2,1536,1024]{2,1,0:T(8,128)(2,1)}) custom-call(s32[128]{0:T(128)S(1)} %copy-done.14, ...), custom_call_target="tpu_custom_call", output_to_operand_aliasing={{1}: (8, {}), {2}: (9, {}), {3}: (3, {})} | custom-call | flops 15000000512 | bytes 33554432 | tf_op jit(solution)/shard_map/pallas_call | solution.py:274
  170.7 0.9 slice.78
  171.7 1.7 collective-permute-start.44
  173.7 1.7 collective-permute-start.34
  176.3 6.0 %block.6 = (f32[64,1024]{1,0:T(8,128)S(1)}, f32[64,1024]{1,0:T(8,128)S(1)}, bf16[64,1024]{1,0:T(8,128)(2,1)S(1)}) custom-call(s32[2]{0:T(128)S(1)} %pad_add_fusion.2.place_ref, bf16[64,512]{1,0:T(8,128)(2,1)S(1)} %get-tuple-element.100.o_own, bf16[64,512]{1,0:T(8,128)(2,1)S(1)} %collective-permute-done.26.o_own_peer, ...), custom_call_target="tpu_custom_call" | custom-call | flops 4000000000 | bytes 8650752 | tf_op jit(solution)/shard_map/block/pallas_call | solution.py:148
  183.0 11.5 %collective-permute-done.34.o_away = bf16[64,512]{1,0:T(8,128)(2,1)S(1)} collective-permute-done((bf16[64,512]{1,0:T(8,128)(2,1)S(1)}, bf16[64,512]{1,0:T(8,128)(2,1)S(1)}, u32[]{:S(2)}, u32[]{:S(2)}) %collective-permute-start.34) | collective-permute-done | bytes 65568 | tf_op jit(solution)/shard_map/ppermute | solution.py:303
  194.5 1.3 collective-permute-done.35.o_away_peer
  195.8 6.7 %block.7 = (f32[64,1024]{1,0:T(8,128)S(1)}, f32[64,1024]{1,0:T(8,128)}, bf16[64,1024]{1,0:T(8,128)(2,1)S(1)}) custom-call(s32[2]{0:T(128)S(1)} %pad_add_fusion.2.place_ref, bf16[64,512]{1,0:T(8,128)(2,1)S(1)} %get-tuple-element.107.o_own, bf16[64,512]{1,0:T(8,128)(2,1)S(1)} %collective-permute-done.33.o_own_peer, ...), custom_call_target="tpu_custom_call" | custom-call | flops 4000000000 | bytes 8650752 | tf_op jit(solution)/shard_map/block/pallas_call | solution.py:148
  204.8 1.2 collective-permute-start.30
  206.0 1.6 place.12.refs_2_
  207.6 1.8 collective-permute-start.40
  209.9 3.5 %collective-permute-done.37 = f32[64,1024]{1,0:T(8,128)} collective-permute-done((f32[64,1024]{1,0:T(8,128)}, f32[64,1024]{1,0:T(8,128)}, u32[]{:S(2)}, u32[]{:S(2)}) %collective-permute-start.37) | collective-permute-done | bytes 262176 | tf_op jit(solution)/shard_map/ppermute | solution.py:303
  213.4 1.0 add_convert_fusion
  214.4 1.8 collective-permute-start.38
  216.1 1.0 collective-permute-done.30
  217.2 1.8 collective-permute-start.31
  220.2 1.3 collective-permute-done.31
  221.5 1.2 collective-permute-start.32
  223.6 2.2 collective-permute-done.32
  226.6 2.9 %place.13.refs_2_ = bf16[2,2,2,704,1024]{4,3,2,1,0:T(8,128)(2,1)} custom-call(s32[2,2]{1,0:T(2,128)S(1)} %pad_add_fusion.1.spots_ref, bf16[384,1024]{1,0:T(8,128)(2,1)} %collective-permute-done.44.refs_0_, bf16[384,1024]{1,0:T(8,128)(2,1)S(1)} %collective-permute-done.45.refs_1_, ...), custom_call_target="tpu_custom_call", output_to_operand_aliasing={{}: (3, {})} | custom-call | flops 2359296000 | bytes 3145728 | tf_op jit(solution)/shard_map/place/pallas_call | solution.py:58
  229.4 3.4 %place.14.refs_2_ = bf16[2,2,2,704,1024]{4,3,2,1,0:T(8,128)(2,1)} custom-call(s32[2,2]{1,0:T(2,128)S(1)} %pad_add_fusion.1.spots_ref, bf16[672,1024]{1,0:T(8,128)(2,1)} %collective-permute-done.42.refs_0_, bf16[672,1024]{1,0:T(8,128)(2,1)S(1)} %collective-permute-done.43.refs_1_, ...), custom_call_target="tpu_custom_call", output_to_operand_aliasing={{}: (3, {})} | custom-call | flops 4128768000 | bytes 5505024 | tf_op jit(solution)/shard_map/place/pallas_call | solution.py:58
  232.8 1.8 place.15
  (138 shorter events, 20.9 us)
Async XLA Ops:
  0.6 28.7 %collective-permute-start.4 = (bf16[2,704,1024]{2,1,0:T(8,128)(2,1)}, bf16[2,704,1024]{2,1,0:T(8,128)(2,1)}, u32[]{:S(2)}, u32[]{:S(2)}) collective-permute-start(bf16[2,704,1024]{2,1,0:T(8,128)(2,1)} %bitcast.29), channel_id=1, source_target_pairs={{0,1},{1,0},{2,3},{3,2},{4,5},{5,4},{6,7},{7,6}} | collective-permute-start | bytes 8650760 | tf_op jit(solution)/shard_map/ppermute | solution.py:303
  1.5 11.8 %collective-permute-start = (bf16[128,1024]{1,0:T(8,128)(2,1)}, bf16[128,1024]{1,0:T(8,128)(2,1)S(1)}, u32[]{:S(2)}, u32[]{:S(2)}) collective-permute-start(bf16[128,1024]{1,0:T(8,128)(2,1)} %own_ref.1), channel_id=1, source_target_pairs={{0,2},{2,0},{1,3},{3,1},{4,6},{6,4},{5,7},{7,5}} | collective-permute-start | bytes 786440 | tf_op jit(solution)/shard_map/ppermute | solution.py:303
  4.0 9.3 %collective-permute-start.1 = (bf16[4,3,64,1024]{3,2,1,0:T(8,128)(2,1)}, bf16[4,3,64,1024]{3,2,1,0:T(8,128)(2,1)S(1)}, u32[]{:S(2)}, u32[]{:S(2)}) collective-permute-start(bf16[4,3,64,1024]{3,2,1,0:T(8,128)(2,1)} %bitcast.38), channel_id=1, source_target_pairs={{0,1},{1,0},{2,3},{3,2},{4,5},{5,4},{6,7},{7,6}} | collective-permute-start | bytes 4718600 | tf_op jit(solution)/shard_map/ppermute | solution.py:303
  4.2 7.1 %collective-permute-start.2 = (s32[128]{0:T(128)}, s32[128]{0:T(128)S(1)}, u32[]{:S(2)}, u32[]{:S(2)}) collective-permute-start(s32[128]{0:T(128)} %lens_ref.7), channel_id=1, source_target_pairs={{0,2},{2,0},{1,3},{3,1},{4,6},{6,4},{5,7},{7,5}} | collective-permute-start | bytes 1544 | tf_op jit(solution)/shard_map/ppermute | solution.py:303
  4.5 74.1 %collective-permute-start.8 = (bf16[1024,256]{1,0:T(8,128)(2,1)}, bf16[1024,256]{1,0:T(8,128)(2,1)}, u32[]{:S(2)}, u32[]{:S(2)}) collective-permute-start(bf16[1024,256]{1,0:T(8,128)(2,1)} %bitcast.47), channel_id=1, source_target_pairs={{0,1},{1,0},{2,3},{3,2},{4,5},{5,4},{6,7},{7,6}} | collective-permute-start | bytes 1572872 | tf_op jit(solution)/shard_map/ppermute | solution.py:303
  11.2 14.0 %collective-permute-start.9 = (bf16[1024,256]{1,0:T(8,128)(2,1)}, bf16[1024,256]{1,0:T(8,128)(2,1)}, u32[]{:S(2)}, u32[]{:S(2)}) collective-permute-start(bf16[1024,256]{1,0:T(8,128)(2,1)} %bitcast.48), channel_id=1, source_target_pairs={{0,4},{4,0},{1,5},{5,1},{2,6},{6,2},{3,7},{7,3}} | collective-permute-start | bytes 1572872 | tf_op jit(solution)/shard_map/ppermute | solution.py:303
  13.2 66.7 %collective-permute-start.11 = (bf16[704,1024]{1,0:T(8,128)(2,1)}, bf16[704,1024]{1,0:T(8,128)(2,1)}, u32[]{:S(2)}, u32[]{:S(2)}) collective-permute-start(bf16[704,1024]{1,0:T(8,128)(2,1)} %bitcast.42), channel_id=1, source_target_pairs={{0,1},{1,0},{2,3},{3,2},{4,5},{5,4},{6,7},{7,6}} | collective-permute-start | bytes 4325384 | tf_op jit(solution)/shard_map/ppermute | solution.py:303
  13.3 11.9 %copy-start.15 = (bf16[4,3,64,1024]{3,2,1,0:T(8,128)(2,1)}, bf16[4,3,64,1024]{3,2,1,0:T(8,128)(2,1)S(1)}, u32[]{:S(2)}) copy-start(bf16[4,3,64,1024]{3,2,1,0:T(8,128)(2,1)S(1)} %collective-permute-done.1.wb_ref.refs_1_) | copy-start | bytes 4718596
  13.3 2.0 copy-start.1
  18.1 16.3 %collective-permute-start.3 = (bf16[3,512,128]{2,1,0:T(8,128)(2,1)S(1)}, bf16[3,512,128]{2,1,0:T(8,128)(2,1)S(1)}, u32[]{:S(2)}, u32[]{:S(2)}) collective-permute-start(bf16[3,512,128]{2,1,0:T(8,128)(2,1)S(1)} %get-tuple-element.66), channel_id=1, source_target_pairs={{0,2},{2,0},{1,3},{3,1},{4,6},{6,4},{5,7},{7,5}} | collective-permute-start | bytes 1179656 | tf_op jit(solution)/shard_map/ppermute | solution.py:303
  25.2 4.1 %copy-start = (bf16[1,1408,1024]{2,1,0:T(8,128)(2,1)S(1)}, bf16[1,1408,1024]{2,1,0:T(8,128)(2,1)}, u32[]{:S(2)}) copy-start(bf16[1,1408,1024]{2,1,0:T(8,128)(2,1)} %param.18) | copy-start | bytes 8650756
  25.2 54.8 %collective-permute-start.10 = (bf16[1024,256]{1,0:T(8,128)(2,1)}, bf16[1024,256]{1,0:T(8,128)(2,1)}, u32[]{:S(2)}, u32[]{:S(2)}) collective-permute-start(bf16[1024,256]{1,0:T(8,128)(2,1)} %collective-permute-done.9.wo_c), channel_id=1, source_target_pairs={{0,1},{1,0},{2,3},{3,2},{4,5},{5,4},{6,7},{7,6}} | collective-permute-start | bytes 1572872 | tf_op jit(solution)/shard_map/ppermute | solution.py:303
  25.2 1.6 copy-start.16
  29.3 5.2 %copy-start.14 = (s32[128]{0:T(128)S(1)}, s32[128]{0:T(128)}, u32[]{:S(2)}) copy-start(s32[128]{0:T(128)} %lens_ref.7) | copy-start | bytes 1540
  48.2 31.8 %copy-start.13 = (bf16[1,1024]{1,0:T(2,128)(2,1)S(1)}, bf16[1,1024]{1,0:T(2,128)(2,1)}, u32[]{:S(2)}) copy-start(bf16[1,1024]{1,0:T(2,128)(2,1)} %gain_ref.9) | copy-start | bytes 6148
  61.2 15.7 %copy-start.20 = (bf16[64,512]{1,0:T(8,128)(2,1)}, bf16[64,512]{1,0:T(8,128)(2,1)S(1)}, u32[]{:S(2)}) copy-start(bf16[64,512]{1,0:T(8,128)(2,1)S(1)} %get-tuple-element.88.o_own) | copy-start | bytes 196612
  61.2 4.5 %collective-permute-start.20 = (bf16[64,512]{1,0:T(8,128)(2,1)S(1)}, bf16[64,512]{1,0:T(8,128)(2,1)}, u32[]{:S(2)}, u32[]{:S(2)}) collective-permute-start(bf16[64,512]{1,0:T(8,128)(2,1)S(1)} %get-tuple-element.88.o_own), channel_id=1, source_target_pairs={{0,4},{4,0},{1,5},{5,1},{2,6},{6,2},{3,7},{7,3}} | collective-permute-start | bytes 196616 | tf_op jit(solution)/shard_map/ppermute | solution.py:303
  62.7 5.4 %collective-permute-start.21 = (bf16[64,512]{1,0:T(8,128)(2,1)S(1)}, bf16[64,512]{1,0:T(8,128)(2,1)}, u32[]{:S(2)}, u32[]{:S(2)}) collective-permute-start(bf16[64,512]{1,0:T(8,128)(2,1)S(1)} %get-tuple-element.88.o_own), channel_id=1, source_target_pairs={{0,2},{2,0},{1,3},{3,1},{4,6},{6,4},{5,7},{7,5}} | collective-permute-start | bytes 196616 | tf_op jit(solution)/shard_map/ppermute | solution.py:303
  65.6 5.3 %collective-permute-start.22 = (bf16[64,512]{1,0:T(8,128)(2,1)S(1)}, bf16[64,512]{1,0:T(8,128)(2,1)S(1)}, u32[]{:S(2)}, u32[]{:S(2)}) collective-permute-start(bf16[64,512]{1,0:T(8,128)(2,1)S(1)} %get-tuple-element.88.o_own), channel_id=1, source_target_pairs={{0,6},{2,4},{4,2},{6,0},{1,7},{3,5},{5,3},{7,1}} | collective-permute-start | bytes 196616 | tf_op jit(solution)/shard_map/ppermute | solution.py:402
  68.1 4.5 %collective-permute-start.5 = (bf16[64,512]{1,0:T(8,128)(2,1)}, bf16[64,512]{1,0:T(8,128)(2,1)S(1)}, u32[]{:S(2)}, u32[]{:S(2)}) collective-permute-start(bf16[64,512]{1,0:T(8,128)(2,1)} %copy-done.22), channel_id=1, source_target_pairs={{0,4},{4,0},{1,5},{5,1},{2,6},{6,2},{3,7},{7,3}} | collective-permute-start | bytes 196616 | tf_op jit(solution)/shard_map/ppermute | solution.py:303
  70.9 4.7 %collective-permute-start.6 = (bf16[64,512]{1,0:T(8,128)(2,1)}, bf16[64,512]{1,0:T(8,128)(2,1)S(1)}, u32[]{:S(2)}, u32[]{:S(2)}) collective-permute-start(bf16[64,512]{1,0:T(8,128)(2,1)} %copy-done.22), channel_id=1, source_target_pairs={{0,2},{2,0},{1,3},{3,1},{4,6},{6,4},{5,7},{7,5}} | collective-permute-start | bytes 196616 | tf_op jit(solution)/shard_map/ppermute | solution.py:303
  72.5 5.4 %collective-permute-start.7 = (bf16[64,512]{1,0:T(8,128)(2,1)}, bf16[64,512]{1,0:T(8,128)(2,1)S(1)}, u32[]{:S(2)}, u32[]{:S(2)}) collective-permute-start(bf16[64,512]{1,0:T(8,128)(2,1)} %copy-done.22), channel_id=1, source_target_pairs={{0,6},{2,4},{4,2},{6,0},{1,7},{3,5},{5,3},{7,1}} | collective-permute-start | bytes 196616 | tf_op jit(solution)/shard_map/ppermute | solution.py:402
  75.6 21.8 %collective-permute-start.15 = (bf16[2,1024]{1,0:T(2,128)(2,1)S(1)}, bf16[2,1024]{1,0:T(2,128)(2,1)S(1)}, u32[]{:S(2)}, u32[]{:S(2)}) collective-permute-start(bf16[2,1024]{1,0:T(2,128)(2,1)S(1)} %pad_maximum_fusion.5), channel_id=1, source_target_pairs={{0,2},{2,0},{1,3},{3,1},{4,6},{6,4},{5,7},{7,5}} | collective-permute-start | bytes 12296 | tf_op jit(solution)/shard_map/ppermute | solution.py:303
  77.9 73.5 %collective-permute-start.46 = (bf16[160,1024]{1,0:T(8,128)(2,1)}, bf16[160,1024]{1,0:T(8,128)(2,1)S(1)}, u32[]{:S(2)}, u32[]{:S(2)}) collective-permute-start(bf16[160,1024]{1,0:T(8,128)(2,1)} %slice_bitcast_fusion), channel_id=1, source_target_pairs={{0,2},{2,0},{1,3},{3,1},{4,6},{6,4},{5,7},{7,5}} | collective-permute-start | bytes 983048 | tf_op jit(solution)/shard_map/ppermute | solution.py:303
  78.6 43.6 %collective-permute-start.18 = (bf16[2,3,64,1024]{3,2,1,0:T(8,128)(2,1)S(1)}, bf16[2,3,64,1024]{3,2,1,0:T(8,128)(2,1)S(1)}, u32[]{:S(2)}, u32[]{:S(2)}) collective-permute-start(bf16[2,3,64,1024]{3,2,1,0:T(8,128)(2,1)S(1)} %get-tuple-element.83), channel_id=1, source_target_pairs={{0,2},{2,0},{1,3},{3,1},{4,6},{6,4},{5,7},{7,5}} | collective-permute-start | bytes 2359304 | tf_op jit(solution)/shard_map/ppermute | solution.py:303
  80.0 1.4 copy-start.17
  83.2 7.4 %copy-start.21 = (bf16[64,512]{1,0:T(8,128)(2,1)S(1)}, bf16[64,512]{1,0:T(8,128)(2,1)}, u32[]{:S(2)}) copy-start(bf16[64,512]{1,0:T(8,128)(2,1)} %copy-done.20) | copy-start | bytes 196612
  89.3 10.0 %collective-permute-start.12 = (f32[64,1024]{1,0:T(8,128)S(1)}, f32[64,1024]{1,0:T(8,128)S(1)}, u32[]{:S(2)}, u32[]{:S(2)}) collective-permute-start(f32[64,1024]{1,0:T(8,128)S(1)} %get-tuple-element.79), channel_id=1, source_target_pairs={{0,4},{4,0},{1,5},{5,1},{2,6},{6,2},{3,7},{7,3}} | collective-permute-start | bytes 786440 | tf_op jit(solution)/shard_map/ppermute | solution.py:303
  90.6 6.8 %copy-start.12 = (bf16[1,1024]{1,0:T(2,128)(2,1)S(1)}, bf16[1,1024]{1,0:T(2,128)(2,1)}, u32[]{:S(2)}) copy-start(bf16[1,1024]{1,0:T(2,128)(2,1)} %gain_ref.5) | copy-start | bytes 6148
  96.7 6.4 %collective-permute-start.23 = (f32[64,1024]{1,0:T(8,128)S(1)}, f32[64,1024]{1,0:T(8,128)S(1)}, u32[]{:S(2)}, u32[]{:S(2)}) collective-permute-start(f32[64,1024]{1,0:T(8,128)S(1)} %get-tuple-element.95), channel_id=1, source_target_pairs={{0,4},{4,0},{1,5},{5,1},{2,6},{6,2},{3,7},{7,3}} | collective-permute-start | bytes 786440 | tf_op jit(solution)/shard_map/ppermute | solution.py:303
  98.7 24.9 %collective-permute-start.16 = (bf16[2,3,64,1024]{3,2,1,0:T(8,128)(2,1)S(1)}, bf16[2,3,64,1024]{3,2,1,0:T(8,128)(2,1)S(1)}, u32[]{:S(2)}, u32[]{:S(2)}) collective-permute-start(bf16[2,3,64,1024]{3,2,1,0:T(8,128)(2,1)S(1)} %get-tuple-element.81), channel_id=1, source_target_pairs={{0,2},{2,0},{1,3},{3,1},{4,6},{6,4},{5,7},{7,5}} | collective-permute-start | bytes 2359304 | tf_op jit(solution)/shard_map/ppermute | solution.py:303
  99.3 22.1 %collective-permute-start.13 = (bf16[32,1024]{1,0:T(8,128)(2,1)S(1)}, bf16[32,1024]{1,0:T(8,128)(2,1)S(1)}, u32[]{:S(2)}, u32[]{:S(2)}) collective-permute-start(bf16[32,1024]{1,0:T(8,128)(2,1)S(1)} %slice.83), channel_id=1, source_target_pairs={{0,2},{2,0},{1,3},{3,1},{4,6},{6,4},{5,7},{7,5}} | collective-permute-start | bytes 196616 | tf_op jit(solution)/shard_map/ppermute | solution.py:303
  103.2 19.0 %collective-permute-start.24 = (bf16[32,1024]{1,0:T(8,128)(2,1)S(1)}, bf16[32,1024]{1,0:T(8,128)(2,1)S(1)}, u32[]{:S(2)}, u32[]{:S(2)}) collective-permute-start(bf16[32,1024]{1,0:T(8,128)(2,1)S(1)} %slice.89), channel_id=1, source_target_pairs={{0,2},{2,0},{1,3},{3,1},{4,6},{6,4},{5,7},{7,5}} | collective-permute-start | bytes 196616 | tf_op jit(solution)/shard_map/ppermute | solution.py:303
  121.4 4.7 %collective-permute-start.14 = (bf16[32,1024]{1,0:T(8,128)(2,1)S(1)}, bf16[32,1024]{1,0:T(8,128)(2,1)S(1)}, u32[]{:S(2)}, u32[]{:S(2)}) collective-permute-start(bf16[32,1024]{1,0:T(8,128)(2,1)S(1)} %slice_select_fusion.3), channel_id=1, source_target_pairs={{0,4},{4,0},{1,5},{5,1},{2,6},{6,2},{3,7},{7,3}} | collective-permute-start | bytes 196616 | tf_op jit(solution)/shard_map/ppermute | solution.py:303
  122.1 5.3 %collective-permute-start.19 = (bf16[2,3,64,1024]{3,2,1,0:T(8,128)(2,1)S(1)}, bf16[2,3,64,1024]{3,2,1,0:T(8,128)(2,1)S(1)}, u32[]{:S(2)}, u32[]{:S(2)}) collective-permute-start(bf16[2,3,64,1024]{3,2,1,0:T(8,128)(2,1)S(1)} %collective-permute-done.18.refs_0_), channel_id=1, source_target_pairs={{0,1},{1,0},{2,3},{3,2},{4,5},{5,4},{6,7},{7,6}} | collective-permute-start | bytes 2359304 | tf_op jit(solution)/shard_map/ppermute | solution.py:303
  122.2 5.0 %collective-permute-start.25 = (bf16[32,1024]{1,0:T(8,128)(2,1)S(1)}, bf16[32,1024]{1,0:T(8,128)(2,1)S(1)}, u32[]{:S(2)}, u32[]{:S(2)}) collective-permute-start(bf16[32,1024]{1,0:T(8,128)(2,1)S(1)} %slice_select_fusion.2), channel_id=1, source_target_pairs={{0,4},{4,0},{1,5},{5,1},{2,6},{6,2},{3,7},{7,3}} | collective-permute-start | bytes 196616 | tf_op jit(solution)/shard_map/ppermute | solution.py:303
  123.5 85.8 %collective-permute-start.42 = (bf16[672,1024]{1,0:T(8,128)(2,1)}, bf16[672,1024]{1,0:T(8,128)(2,1)}, u32[]{:S(2)}, u32[]{:S(2)}) collective-permute-start(bf16[672,1024]{1,0:T(8,128)(2,1)} %slice.77), channel_id=1, source_target_pairs={{0,2},{2,0},{1,3},{3,1},{4,6},{6,4},{5,7},{7,5}} | collective-permute-start | bytes 4128776 | tf_op jit(solution)/shard_map/ppermute | solution.py:303
  126.2 3.2 %collective-permute-start.17 = (bf16[2,3,64,1024]{3,2,1,0:T(8,128)(2,1)S(1)}, bf16[2,3,64,1024]{3,2,1,0:T(8,128)(2,1)S(1)}, u32[]{:S(2)}, u32[]{:S(2)}) collective-permute-start(bf16[2,3,64,1024]{3,2,1,0:T(8,128)(2,1)S(1)} %collective-permute-done.16.refs_0_), channel_id=1, source_target_pairs={{0,1},{1,0},{2,3},{3,2},{4,5},{5,4},{6,7},{7,6}} | collective-permute-start | bytes 2359304 | tf_op jit(solution)/shard_map/ppermute | solution.py:303
  127.1 46.6 %collective-permute-start.29 = (bf16[64,1024]{1,0:T(8,128)(2,1)S(1)}, bf16[64,1024]{1,0:T(8,128)(2,1)S(1)}, u32[]{:S(2)}, u32[]{:S(2)}) collective-permute-start(bf16[64,1024]{1,0:T(8,128)(2,1)S(1)} %pad_maximum_fusion.1.rest_0_.hid_ref), channel_id=1, source_target_pairs={{0,2},{2,0},{1,3},{3,1},{4,6},{6,4},{5,7},{7,5}} | collective-permute-start | bytes 393224 | tf_op jit(solution)/shard_map/ppermute | solution.py:303
  148.8 21.0 %collective-permute-start.26 = (bf16[64,512]{1,0:T(8,128)(2,1)S(1)}, bf16[64,512]{1,0:T(8,128)(2,1)S(1)}, u32[]{:S(2)}, u32[]{:S(2)}) collective-permute-start(bf16[64,512]{1,0:T(8,128)(2,1)S(1)} %get-tuple-element.100.o_own), channel_id=1, source_target_pairs={{0,4},{4,0},{1,5},{5,1},{2,6},{6,2},{3,7},{7,3}} | collective-permute-start | bytes 196616 | tf_op jit(solution)/shard_map/ppermute | solution.py:303
  149.7 21.9 %collective-permute-start.27 = (bf16[64,512]{1,0:T(8,128)(2,1)S(1)}, bf16[64,512]{1,0:T(8,128)(2,1)S(1)}, u32[]{:S(2)}, u32[]{:S(2)}) collective-permute-start(bf16[64,512]{1,0:T(8,128)(2,1)S(1)} %get-tuple-element.100.o_own), channel_id=1, source_target_pairs={{0,2},{2,0},{1,3},{3,1},{4,6},{6,4},{5,7},{7,5}} | collective-permute-start | bytes 196616 | tf_op jit(solution)/shard_map/ppermute | solution.py:303
  151.5 21.9 %collective-permute-start.28 = (bf16[64,512]{1,0:T(8,128)(2,1)S(1)}, bf16[64,512]{1,0:T(8,128)(2,1)S(1)}, u32[]{:S(2)}, u32[]{:S(2)}) collective-permute-start(bf16[64,512]{1,0:T(8,128)(2,1)S(1)} %get-tuple-element.100.o_own), channel_id=1, source_target_pairs={{0,6},{2,4},{4,2},{6,0},{1,7},{3,5},{5,3},{7,1}} | collective-permute-start | bytes 196616 | tf_op jit(solution)/shard_map/ppermute | solution.py:402
  169.8 5.6 %collective-permute-start.33 = (bf16[64,512]{1,0:T(8,128)(2,1)S(1)}, bf16[64,512]{1,0:T(8,128)(2,1)S(1)}, u32[]{:S(2)}, u32[]{:S(2)}) collective-permute-start(bf16[64,512]{1,0:T(8,128)(2,1)S(1)} %get-tuple-element.107.o_own), channel_id=1, source_target_pairs={{0,4},{4,0},{1,5},{5,1},{2,6},{6,2},{3,7},{7,3}} | collective-permute-start | bytes 196616 | tf_op jit(solution)/shard_map/ppermute | solution.py:303
  171.7 37.7 %collective-permute-start.44 = (bf16[384,1024]{1,0:T(8,128)(2,1)}, bf16[384,1024]{1,0:T(8,128)(2,1)}, u32[]{:S(2)}, u32[]{:S(2)}) collective-permute-start(bf16[384,1024]{1,0:T(8,128)(2,1)} %slice.78), channel_id=1, source_target_pairs={{0,2},{2,0},{1,3},{3,1},{4,6},{6,4},{5,7},{7,5}} | collective-permute-start | bytes 2359304 | tf_op jit(solution)/shard_map/ppermute | solution.py:303
  173.4 22.4 %collective-permute-start.36 = (bf16[64,1024]{1,0:T(8,128)(2,1)S(1)}, bf16[64,1024]{1,0:T(8,128)(2,1)S(1)}, u32[]{:S(2)}, u32[]{:S(2)}) collective-permute-start(bf16[64,1024]{1,0:T(8,128)(2,1)S(1)} %pad_maximum_fusion.2.rest_0_.hid_ref), channel_id=1, source_target_pairs={{0,2},{2,0},{1,3},{3,1},{4,6},{6,4},{5,7},{7,5}} | collective-permute-start | bytes 393224 | tf_op jit(solution)/shard_map/ppermute | solution.py:303
  173.7 20.8 %collective-permute-start.34 = (bf16[64,512]{1,0:T(8,128)(2,1)S(1)}, bf16[64,512]{1,0:T(8,128)(2,1)S(1)}, u32[]{:S(2)}, u32[]{:S(2)}) collective-permute-start(bf16[64,512]{1,0:T(8,128)(2,1)S(1)} %get-tuple-element.107.o_own), channel_id=1, source_target_pairs={{0,2},{2,0},{1,3},{3,1},{4,6},{6,4},{5,7},{7,5}} | collective-permute-start | bytes 196616 | tf_op jit(solution)/shard_map/ppermute | solution.py:303
  175.4 20.3 %collective-permute-start.35 = (bf16[64,512]{1,0:T(8,128)(2,1)S(1)}, bf16[64,512]{1,0:T(8,128)(2,1)S(1)}, u32[]{:S(2)}, u32[]{:S(2)}) collective-permute-start(bf16[64,512]{1,0:T(8,128)(2,1)S(1)} %get-tuple-element.107.o_own), channel_id=1, source_target_pairs={{0,6},{2,4},{4,2},{6,0},{1,7},{3,5},{5,3},{7,1}} | collective-permute-start | bytes 196616 | tf_op jit(solution)/shard_map/ppermute | solution.py:402
  183.0 12.8 %copy-start.19 = (f32[64,1024]{1,0:T(8,128)}, f32[64,1024]{1,0:T(8,128)S(1)}, u32[]{:S(2)}) copy-start(f32[64,1024]{1,0:T(8,128)S(1)} %get-tuple-element.106) | copy-start | bytes 786436
  183.0 19.5 %copy-start.7 = (bf16[64,1024]{1,0:T(8,128)(2,1)}, bf16[64,1024]{1,0:T(8,128)(2,1)S(1)}, u32[]{:S(2)}) copy-start(bf16[64,1024]{1,0:T(8,128)(2,1)S(1)} %get-tuple-element.104) | copy-start | bytes 393220
  194.5 11.5 %collective-permute-start.47 = (bf16[160,1024]{1,0:T(8,128)(2,1)S(1)}, bf16[160,1024]{1,0:T(8,128)(2,1)S(1)}, u32[]{:S(2)}, u32[]{:S(2)}) collective-permute-start(bf16[160,1024]{1,0:T(8,128)(2,1)S(1)} %collective-permute-done.46.refs_0_), channel_id=1, source_target_pairs={{0,1},{1,0},{2,3},{3,2},{4,5},{5,4},{6,7},{7,6}} | collective-permute-start | bytes 983048 | tf_op jit(solution)/shard_map/ppermute | solution.py:303
  203.9 9.5 %collective-permute-start.37 = (f32[64,1024]{1,0:T(8,128)}, f32[64,1024]{1,0:T(8,128)}, u32[]{:S(2)}, u32[]{:S(2)}) collective-permute-start(f32[64,1024]{1,0:T(8,128)} %get-tuple-element.114), channel_id=1, source_target_pairs={{0,4},{4,0},{1,5},{5,1},{2,6},{6,2},{3,7},{7,3}} | collective-permute-start | bytes 786440 | tf_op jit(solution)/shard_map/ppermute | solution.py:303
  204.8 8.6 %copy-start.5 = (f32[64,1024]{1,0:T(8,128)S(1)}, f32[64,1024]{1,0:T(8,128)}, u32[]{:S(2)}) copy-start(f32[64,1024]{1,0:T(8,128)} %copy-done.4) | copy-start | bytes 786436
  204.8 8.6 %copy-start.10 = (bf16[64,1024]{1,0:T(8,128)(2,1)S(1)}, bf16[64,1024]{1,0:T(8,128)(2,1)}, u32[]{:S(2)}) copy-start(bf16[64,1024]{1,0:T(8,128)(2,1)} %copy-done.9) | copy-start | bytes 393220
  204.8 12.4 %copy-start.3 = (f32[64,1024]{1,0:T(8,128)S(1)}, f32[64,1024]{1,0:T(8,128)}, u32[]{:S(2)}) copy-start(f32[64,1024]{1,0:T(8,128)} %copy-done.2) | copy-start | bytes 786436
  204.8 12.4 %copy-start.8 = (bf16[64,1024]{1,0:T(8,128)(2,1)S(1)}, bf16[64,1024]{1,0:T(8,128)(2,1)}, u32[]{:S(2)}) copy-start(bf16[64,1024]{1,0:T(8,128)(2,1)} %copy-done.7) | copy-start | bytes 393220
  204.8 12.3 %collective-permute-start.30 = (f32[64,1024]{1,0:T(8,128)}, f32[64,1024]{1,0:T(8,128)S(1)}, u32[]{:S(2)}, u32[]{:S(2)}) collective-permute-start(f32[64,1024]{1,0:T(8,128)} %copy-done.19), channel_id=1, source_target_pairs={{0,4},{4,0},{1,5},{5,1},{2,6},{6,2},{3,7},{7,3}} | collective-permute-start | bytes 786440 | tf_op jit(solution)/shard_map/ppermute | solution.py:303
  207.6 15.1 %collective-permute-start.40 = (bf16[192,1024]{1,0:T(8,128)(2,1)S(1)}, bf16[192,1024]{1,0:T(8,128)(2,1)S(1)}, u32[]{:S(2)}, u32[]{:S(2)}) collective-permute-start(bf16[192,1024]{1,0:T(8,128)(2,1)S(1)} %slice.76), channel_id=1, source_target_pairs={{0,2},{2,0},{1,3},{3,1},{4,6},{6,4},{5,7},{7,5}} | collective-permute-start | bytes 1179656 | tf_op jit(solution)/shard_map/ppermute | solution.py:303
  209.4 17.2 %collective-permute-start.45 = (bf16[384,1024]{1,0:T(8,128)(2,1)}, bf16[384,1024]{1,0:T(8,128)(2,1)S(1)}, u32[]{:S(2)}, u32[]{:S(2)}) collective-permute-start(bf16[384,1024]{1,0:T(8,128)(2,1)} %collective-permute-done.44.refs_0_), channel_id=1, source_target_pairs={{0,1},{1,0},{2,3},{3,2},{4,5},{5,4},{6,7},{7,6}} | collective-permute-start | bytes 2359304 | tf_op jit(solution)/shard_map/ppermute | solution.py:303
  209.4 20.0 %collective-permute-start.43 = (bf16[672,1024]{1,0:T(8,128)(2,1)}, bf16[672,1024]{1,0:T(8,128)(2,1)S(1)}, u32[]{:S(2)}, u32[]{:S(2)}) collective-permute-start(bf16[672,1024]{1,0:T(8,128)(2,1)} %collective-permute-done.42.refs_0_), channel_id=1, source_target_pairs={{0,1},{1,0},{2,3},{3,2},{4,5},{5,4},{6,7},{7,6}} | collective-permute-start | bytes 4128776 | tf_op jit(solution)/shard_map/ppermute | solution.py:303
  214.4 4.9 %collective-permute-start.38 = (bf16[32,1024]{1,0:T(8,128)(2,1)S(1)}, bf16[32,1024]{1,0:T(8,128)(2,1)S(1)}, u32[]{:S(2)}, u32[]{:S(2)}) collective-permute-start(bf16[32,1024]{1,0:T(8,128)(2,1)S(1)} %slice.93), channel_id=1, source_target_pairs={{0,2},{2,0},{1,3},{3,1},{4,6},{6,4},{5,7},{7,5}} | collective-permute-start | bytes 196616 | tf_op jit(solution)/shard_map/ppermute | solution.py:303
  217.2 4.3 %collective-permute-start.31 = (bf16[32,1024]{1,0:T(8,128)(2,1)S(1)}, bf16[32,1024]{1,0:T(8,128)(2,1)S(1)}, u32[]{:S(2)}, u32[]{:S(2)}) collective-permute-start(bf16[32,1024]{1,0:T(8,128)(2,1)S(1)} %slice.91), channel_id=1, source_target_pairs={{0,2},{2,0},{1,3},{3,1},{4,6},{6,4},{5,7},{7,5}} | collective-permute-start | bytes 196616 | tf_op jit(solution)/shard_map/ppermute | solution.py:303
  219.3 4.3 %collective-permute-start.39 = (bf16[32,1024]{1,0:T(8,128)(2,1)S(1)}, bf16[32,1024]{1,0:T(8,128)(2,1)S(1)}, u32[]{:S(2)}, u32[]{:S(2)}) collective-permute-start(bf16[32,1024]{1,0:T(8,128)(2,1)S(1)} %slice_select_fusion), channel_id=1, source_target_pairs={{0,4},{4,0},{1,5},{5,1},{2,6},{6,2},{3,7},{7,3}} | collective-permute-start | bytes 196616 | tf_op jit(solution)/shard_map/ppermute | solution.py:303
  221.5 4.3 %collective-permute-start.32 = (bf16[32,1024]{1,0:T(8,128)(2,1)S(1)}, bf16[32,1024]{1,0:T(8,128)(2,1)S(1)}, u32[]{:S(2)}, u32[]{:S(2)}) collective-permute-start(bf16[32,1024]{1,0:T(8,128)(2,1)S(1)} %slice_select_fusion.1), channel_id=1, source_target_pairs={{0,4},{4,0},{1,5},{5,1},{2,6},{6,2},{3,7},{7,3}} | collective-permute-start | bytes 196616 | tf_op jit(solution)/shard_map/ppermute | solution.py:303
  222.7 10.1 %collective-permute-start.41 = (bf16[192,1024]{1,0:T(8,128)(2,1)S(1)}, bf16[192,1024]{1,0:T(8,128)(2,1)S(1)}, u32[]{:S(2)}, u32[]{:S(2)}) collective-permute-start(bf16[192,1024]{1,0:T(8,128)(2,1)S(1)} %collective-permute-done.40.refs_0_), channel_id=1, source_target_pairs={{0,1},{1,0},{2,3},{3,2},{4,5},{5,4},{6,7},{7,6}} | collective-permute-start | bytes 1179656 | tf_op jit(solution)/shard_map/ppermute | solution.py:303
  (8 other events, 6.2 us)

commit v5 on v4

--- a/solution.py
+++ b/solution.py
@@ -13,7 +13,7 @@
 MASK_FILL = -1e30
 PER = 8
 PARTS = 2
-GU_CUTS = (0, 10, 34, 76, 88)
+GU_CUTS = (0, 10, 30, 54, 72, 88)
 ROW_AXES = ("pp", "grp")
 TRAIN_AXES = ("tg", "grp")
 SWAP = ((0, 1), (1, 0))
@@ -180,7 +180,8 @@
     if not ready:
         fetch = pltpu.make_async_copy(heads_in[2].at[layer], w_s, w_sem)
         fetch.start()
-    for blk in range(blocks):
+    head_start = blocks if ready else 2
+    for blk in range(head_start):
         for move in moves(blk, False):
             move.start()
 
@@ -193,6 +194,9 @@
         normed = rms_norm(h_ref[...], gain_ref[...])
         normed = jnp.concatenate([normed] * (seq // count), axis=0)
         fetch.wait()
+        for blk in range(head_start, blocks):
+            for move in moves(blk, False):
+                move.start()
 
         def proj(t, turn):
             vals = lax.dot_general(w_s[t * rows:(t + 1) * rows, :], normed, (((1,), (1,)), ((), ())),
@@ -398,6 +402,8 @@
                     gen_qkv = caches.pop()
                 if layer == 0 and i == 0:
                     far_heads.append(qkv_send(1, o_part))
+                if layer == 1 and i == 0:
+                    sent.append(gu_send(3, o_part))
                 o_vals.append((o_part, swap(o_part, "tg"), swap(o_part, "pp"),
                                lax.ppermute(o_part, ("tg", "pp"), ((0, 3), (1, 2), (2, 1), (3, 0)))))
             last = o_vals[1][0]
@@ -407,11 +413,11 @@
                     gen_qkv = qkv_take(i, far_heads[i], gen_qkv)
                 sent.append(gu_send(1, last))
             else:
-                for c in (1, 2):
+                for c in (1, 2, 3):
                     sent[c] = after(sent[c], last)
                     gen_gu = gu_take(c, sent[c], gen_gu)
-                sent.append(gu_send(3, last))
-                gen_gu = gu_take(3, sent[3], gen_gu)
+                sent.append(gu_send(4, last))
+                gen_gu = gu_take(4, sent[4], gen_gu)
             backs, owns = [], []
             give = None
             for i in range(PARTS):

time: 235 us -> 265 us (1.13)
  waiting for transfers between devices: 58.6 us -> 96.1 us
  Pallas kernels: 108 us -> 102 us
    ppermute x44 -> x46, waiting for transfers between devices: 54 us -> 91.8 us  [swap(): return lax.ppermute(x, axis, SWAP)]
    pallas_call x4, Pallas kernels: 61 us -> 54.1 us  [attention(): pl.pallas_call(functools.partial(attn_kernel, heads=heads, head_dim=head_...]
    ppermute x44 -> x46, starting transfers between devices: 39.9 us -> 36.1 us  [swap(): return lax.ppermute(x, axis, SWAP)]
    pallas_call x8 -> x9, Pallas kernels: 21.1 us -> 22.1 us  [place(): pl.pallas_call(functools.partial(place_kernel, count=count, blocks=blocks...]
    unnamed x48 -> x42, local copies, waits for them, and re-layouts: 11.1 us -> 11.6 us
  transfers between devices with their start and end apart: 48 -> 50, of which waited for: 19 -> 19; matrix products, arithmetic and copies ran while one was open for 4% -> 4% of each run, Pallas kernels for 45% -> 38%
where the time goes in v5:
time: 265 us; the launch traced here: 264 us
  Pallas kernels  102 us (38%)
  waiting for transfers between devices  96.1 us (36%)
  starting transfers between devices  42.6 us (16%)
  local copies, waits for them, and re-layouts  17.7 us (7%)
  other arithmetic  4.04 us (2%)
    ppermute x46, waiting for transfers between devices, swap(): return lax.ppermute(x, axis, SWAP)  91.8 us
    pallas_call x4, Pallas kernels, attention(): pl.pallas_call(functools.partial(attn_kernel, heads=heads, head_dim=head_...  54.1 us
    ppermute x46, starting transfers between devices, swap(): return lax.ppermute(x, axis, SWAP)  36.1 us
    pallas_call x4, Pallas kernels, block(): pl.pallas_call(block_kernel, in_specs=[pl.BlockSpec(memory_space=pltpu.SM...  25 us
    pallas_call x9, Pallas kernels, place(): pl.pallas_call(functools.partial(place_kernel, count=count, blocks=blocks...  22.1 us
    unnamed x42, local copies, waits for them, and re-layouts  11.6 us
    ppermute x4, starting transfers between devices, decode(): lax.ppermute(o_part, ('tg', 'pp'), ((0, 3), (1, 2), (2, 1), (3, 0)))  6.43 us
  transfers between devices with their start and end apart: 50, of which 19 were waited for; matrix products, arithmetic and copies ran while one was open for 4% of the time, Pallas kernels for 38%

profile of v5, /device:TPU:0, one launch (start us, length us, event | category | flops | bytes accessed | tf_op | source)
XLA Modules:
  0.0 264.1 jit_solution(14896751084309981272)
XLA Ops:
  1.5 2.5 collective-permute-start
  5.6 1.0 fusion.2
  6.5 1.7 slice_bitcast_fusion
  8.9 2.3 collective-permute-done.2
  11.2 1.8 collective-permute-start.9
  13.3 1.1 copy-done.14
  14.4 1.4 copy-done.1
  17.5 1.4 copy-done.15
  18.9 1.2 project.1
  20.1 1.5 collective-permute-start.3
  21.6 3.6 %collective-permute-done.9.wo_c = bf16[1024,256]{1,0:T(8,128)(2,1)} collective-permute-done((bf16[1024,256]{1,0:T(8,128)(2,1)}, bf16[1024,256]{1,0:T(8,128)(2,1)}, u32[]{:S(2)}, u32[]{:S(2)}) %collective-permute-start.9) | collective-permute-done | bytes 524320 | tf_op jit(solution)/shard_map/ppermute | solution.py:307
  25.2 2.5 place.9.refs_2_
  27.8 5.1 %place.10.refs_2_ = bf16[2,2,2,704,1024]{4,3,2,1,0:T(8,128)(2,1)} custom-call(s32[2,2]{1,0:T(2,128)S(1)} %pad_add_fusion.spots_ref, bf16[1408,1024]{1,0:T(8,128)(2,1)S(1)} %bitcast.30, bf16[1408,1024]{1,0:T(8,128)(2,1)} %bitcast.9.refs_1_), custom_call_target="tpu_custom_call" | custom-call | flops 8650752000 | bytes 11534336 | tf_op jit(solution)/shard_map/place/pallas_call | solution.py:58
  32.9 13.0 %shard_map.137 = (bf16[64,512]{1,0:T(8,128)(2,1)S(1)}, bf16[2,128,8,64,128]{4,3,2,1,0:T(8,128)(2,1)}, bf16[2,128,8,64,128]{4,3,2,1,0:T(8,128)(2,1)}) custom-call(s32[128]{0:T(128)S(1)} %copy-done.13, bf16[3,512,128]{2,1,0:T(8,128)(2,1)S(1)} %broadcast_select_fusion.rest_0_, bf16[2,128,8,64,128]{4,3,2,1,0:T(8,128)(2,1)} %bitcast.54, ...), custom_call_target="tpu_custom_call" | custom-call | flops 15000000512 | bytes 33554432 | tf_op jit(solution)/shard_map/pallas_call | solution.py:278
  46.6 13.0 %shard_map.138 = (bf16[64,512]{1,0:T(8,128)(2,1)S(1)}, bf16[2,128,8,64,128]{4,3,2,1,0:T(8,128)(2,1)}, bf16[2,128,8,64,128]{4,3,2,1,0:T(8,128)(2,1)}) custom-call(s32[128]{0:T(128)S(1)} %copy-done.13, bf16[3,512,128]{2,1,0:T(8,128)(2,1)S(1)} %broadcast_select_fusion.rest_0_, ...), custom_call_target="tpu_custom_call", output_to_operand_aliasing={{1}: (4, {}), {2}: (5, {})} | custom-call | flops 15000000512 | bytes 33554432 | tf_op jit(solution)/shard_map/pallas_call | solution.py:278
  59.6 1.5 collective-permute-start.20
  61.1 1.5 collective-permute-start.21
  62.7 1.5 collective-permute-done.20.o_own_peer
  64.2 2.4 collective-permute-start.22
  67.2 2.3 collective-permute-done.22.o_away_peer
  69.5 1.5 collective-permute-start.6
  71.1 1.3 collective-permute-start.7
  72.4 1.5 fusion
  74.4 1.1 collective-permute-start.15
  75.5 1.0 collective-permute-done.7.o_away_peer
  77.1 1.4 collective-permute-start.18
  78.6 1.4 copy-done.16
  79.9 1.0 copy-done.17
  81.8 6.1 %block.4 = (f32[64,1024]{1,0:T(8,128)S(1)}, f32[64,1024]{1,0:T(8,128)S(1)}, bf16[64,1024]{1,0:T(8,128)(2,1)S(1)}) custom-call(s32[2]{0:T(128)S(1)} %pad_add_fusion.2.place_ref, bf16[64,512]{1,0:T(8,128)(2,1)S(1)} %copy-done.20, bf16[64,512]{1,0:T(8,128)(2,1)S(1)} %collective-permute-done.5.o_own_peer, bf16[64,512]{1,0:T(8,128)(2,1)S(1)} %collective-permute-done.6.o_away, ...), custom_call_target="tpu_custom_call" | custom-call | flops 4000000000 | bytes 8650752 | tf_op jit(solution)/shard_map/block/pallas_call | solution.py:148
  87.9 1.4 collective-permute-start.12
  89.2 6.1 %block.5 = (f32[64,1024]{1,0:T(8,128)S(1)}, f32[64,1024]{1,0:T(8,128)S(1)}, bf16[64,1024]{1,0:T(8,128)(2,1)S(1)}) custom-call(s32[2]{0:T(128)S(1)} %pad_add_fusion.2.place_ref, bf16[64,512]{1,0:T(8,128)(2,1)S(1)} %get-tuple-element.90.o_own, bf16[64,512]{1,0:T(8,128)(2,1)} %collective-permute-done.20.o_own_peer, ...), custom_call_target="tpu_custom_call" | custom-call | flops 4000000000 | bytes 8650752 | tf_op jit(solution)/shard_map/block/pallas_call | solution.py:148
  96.8 1.4 collective-permute-start.13
  98.2 3.5 %collective-permute-done.23 = f32[64,1024]{1,0:T(8,128)S(1)} collective-permute-done((f32[64,1024]{1,0:T(8,128)S(1)}, f32[64,1024]{1,0:T(8,128)S(1)}, u32[]{:S(2)}, u32[]{:S(2)}) %collective-permute-start.23) | collective-permute-done | bytes 262176 | tf_op jit(solution)/shard_map/ppermute | solution.py:307
  102.3 17.7 %collective-permute-done.13 = bf16[32,1024]{1,0:T(8,128)(2,1)S(1)} collective-permute-done((bf16[32,1024]{1,0:T(8,128)(2,1)S(1)}, bf16[32,1024]{1,0:T(8,128)(2,1)S(1)}, u32[]{:S(2)}, u32[]{:S(2)}) %collective-permute-start.13) | collective-permute-done | bytes 65568 | tf_op jit(solution)/shard_map/ppermute | solution.py:307
  120.0 1.1 collective-permute-start.14
  121.1 1.0 collective-permute-start.25
  122.3 2.0 collective-permute-done.14
  125.7 1.9 place.11.refs_2_
  127.6 1.9 place.12
  129.6 14.1 %shard_map.139 = (bf16[64,512]{1,0:T(8,128)(2,1)S(1)}, bf16[2,128,8,64,128]{4,3,2,1,0:T(8,128)(2,1)}, bf16[2,128,8,64,128]{4,3,2,1,0:T(8,128)(2,1)}, bf16[2,1536,1024]{2,1,0:T(8,128)(2,1)}) custom-call(s32[128]{0:T(128)S(1)} %copy-done.13, ...), custom_call_target="tpu_custom_call", output_to_operand_aliasing={{1}: (8, {}), {2}: (9, {}), {3}: (3, {})} | custom-call | flops 15000000512 | bytes 33554432 | tf_op jit(solution)/shard_map/pallas_call | solution.py:278
  143.6 1.1 collective-permute-start.26
  145.6 1.6 collective-permute-start.28
  147.1 14.1 %shard_map.140 = (bf16[64,512]{1,0:T(8,128)(2,1)S(1)}, bf16[2,128,8,64,128]{4,3,2,1,0:T(8,128)(2,1)}, bf16[2,128,8,64,128]{4,3,2,1,0:T(8,128)(2,1)}, bf16[2,1536,1024]{2,1,0:T(8,128)(2,1)}) custom-call(s32[128]{0:T(128)S(1)} %copy-done.13, ...), custom_call_target="tpu_custom_call", output_to_operand_aliasing={{1}: (8, {}), {2}: (9, {}), {3}: (3, {})} | custom-call | flops 15000000512 | bytes 33554432 | tf_op jit(solution)/shard_map/pallas_call | solution.py:278
  161.2 1.1 collective-permute-start.33
  165.0 1.2 collective-permute-start.44
  167.0 1.2 collective-permute-start.34
  168.2 1.1 collective-permute-start.35
  169.3 6.1 %block.6 = (f32[64,1024]{1,0:T(8,128)S(1)}, f32[64,1024]{1,0:T(8,128)S(1)}, bf16[64,1024]{1,0:T(8,128)(2,1)S(1)}) custom-call(s32[2]{0:T(128)S(1)} %pad_add_fusion.2.place_ref, bf16[64,512]{1,0:T(8,128)(2,1)S(1)} %get-tuple-element.102.o_own, bf16[64,512]{1,0:T(8,128)(2,1)S(1)} %collective-permute-done.26.o_own_peer, ...), custom_call_target="tpu_custom_call" | custom-call | flops 4000000000 | bytes 8650752 | tf_op jit(solution)/shard_map/block/pallas_call | solution.py:148
  176.1 25.3 %collective-permute-done.34.o_away = bf16[64,512]{1,0:T(8,128)(2,1)S(1)} collective-permute-done((bf16[64,512]{1,0:T(8,128)(2,1)S(1)}, bf16[64,512]{1,0:T(8,128)(2,1)S(1)}, u32[]{:S(2)}, u32[]{:S(2)}) %collective-permute-start.34) | collective-permute-done | bytes 65568 | tf_op jit(solution)/shard_map/ppermute | solution.py:307
  202.4 6.8 %block.7 = (f32[64,1024]{1,0:T(8,128)S(1)}, f32[64,1024]{1,0:T(8,128)}, bf16[64,1024]{1,0:T(8,128)(2,1)S(1)}) custom-call(s32[2]{0:T(128)S(1)} %pad_add_fusion.2.place_ref, bf16[64,512]{1,0:T(8,128)(2,1)S(1)} %get-tuple-element.109.o_own, bf16[64,512]{1,0:T(8,128)(2,1)S(1)} %collective-permute-done.33.o_own_peer, ...), custom_call_target="tpu_custom_call" | custom-call | flops 4000000000 | bytes 8650752 | tf_op jit(solution)/shard_map/block/pallas_call | solution.py:148
  210.6 1.2 collective-permute-start.37
  212.7 2.4 place.13.refs_2_
  215.5 1.7 collective-permute-start.42
  217.2 2.9 %collective-permute-done.37 = f32[64,1024]{1,0:T(8,128)} collective-permute-done((f32[64,1024]{1,0:T(8,128)}, f32[64,1024]{1,0:T(8,128)}, u32[]{:S(2)}, u32[]{:S(2)}) %collective-permute-start.37) | collective-permute-done | bytes 262176 | tf_op jit(solution)/shard_map/ppermute | solution.py:307
  220.1 1.0 add_convert_fusion
  221.1 3.1 %collective-permute-done.30 = f32[64,1024]{1,0:T(8,128)S(1)} collective-permute-done((f32[64,1024]{1,0:T(8,128)}, f32[64,1024]{1,0:T(8,128)S(1)}, u32[]{:S(2)}, u32[]{:S(2)}) %collective-permute-start.30) | collective-permute-done | bytes 262176 | tf_op jit(solution)/shard_map/ppermute | solution.py:307
  224.5 17.5 %collective-permute-done.38 = bf16[32,1024]{1,0:T(8,128)(2,1)S(1)} collective-permute-done((bf16[32,1024]{1,0:T(8,128)(2,1)S(1)}, bf16[32,1024]{1,0:T(8,128)(2,1)S(1)}, u32[]{:S(2)}, u32[]{:S(2)}) %collective-permute-start.38) | collective-permute-done | bytes 65568 | tf_op jit(solution)/shard_map/ppermute | solution.py:307
  242.3 4.0 %collective-permute-done.31 = bf16[32,1024]{1,0:T(8,128)(2,1)S(1)} collective-permute-done((bf16[32,1024]{1,0:T(8,128)(2,1)S(1)}, bf16[32,1024]{1,0:T(8,128)(2,1)S(1)}, u32[]{:S(2)}, u32[]{:S(2)}) %collective-permute-start.31) | collective-permute-done | bytes 65568 | tf_op jit(solution)/shard_map/ppermute | solution.py:307
  247.1 3.4 %collective-permute-done.39 = bf16[32,1024]{1,0:T(8,128)(2,1)S(1)} collective-permute-done((bf16[32,1024]{1,0:T(8,128)(2,1)S(1)}, bf16[32,1024]{1,0:T(8,128)(2,1)S(1)}, u32[]{:S(2)}, u32[]{:S(2)}) %collective-permute-start.39) | collective-permute-done | bytes 65568 | tf_op jit(solution)/shard_map/ppermute | solution.py:307
  251.4 3.4 %collective-permute-done.32 = bf16[32,1024]{1,0:T(8,128)(2,1)S(1)} collective-permute-done((bf16[32,1024]{1,0:T(8,128)(2,1)S(1)}, bf16[32,1024]{1,0:T(8,128)(2,1)S(1)}, u32[]{:S(2)}, u32[]{:S(2)}) %collective-permute-start.32) | collective-permute-done | bytes 65568 | tf_op jit(solution)/shard_map/ppermute | solution.py:307
  255.6 2.1 place.14.refs_2_
  257.6 2.8 %place.15.refs_2_ = bf16[2,2,2,704,1024]{4,3,2,1,0:T(8,128)(2,1)} custom-call(s32[2,2]{1,0:T(2,128)S(1)} %pad_add_fusion.1.spots_ref, bf16[384,1024]{1,0:T(8,128)(2,1)} %collective-permute-done.44.refs_0_, bf16[384,1024]{1,0:T(8,128)(2,1)S(1)} %collective-permute-done.45.refs_1_, ...), custom_call_target="tpu_custom_call", output_to_operand_aliasing={{}: (3, {})} | custom-call | flops 2359296000 | bytes 3145728 | tf_op jit(solution)/shard_map/place/pallas_call | solution.py:58
  260.4 1.8 place.16.refs_2_
  262.3 1.6 place.17
  (138 shorter events, 23.9 us)
Async XLA Ops:
  0.6 27.1 %collective-permute-start.4 = (bf16[2,704,1024]{2,1,0:T(8,128)(2,1)}, bf16[2,704,1024]{2,1,0:T(8,128)(2,1)}, u32[]{:S(2)}, u32[]{:S(2)}) collective-permute-start(bf16[2,704,1024]{2,1,0:T(8,128)(2,1)} %bitcast.29), channel_id=1, source_target_pairs={{0,1},{1,0},{2,3},{3,2},{4,5},{5,4},{6,7},{7,6}} | collective-permute-start | bytes 8650760 | tf_op jit(solution)/shard_map/ppermute | solution.py:307
  1.5 11.8 %collective-permute-start = (bf16[128,1024]{1,0:T(8,128)(2,1)}, bf16[128,1024]{1,0:T(8,128)(2,1)S(1)}, u32[]{:S(2)}, u32[]{:S(2)}) collective-permute-start(bf16[128,1024]{1,0:T(8,128)(2,1)} %own_ref.1), channel_id=1, source_target_pairs={{0,2},{2,0},{1,3},{3,1},{4,6},{6,4},{5,7},{7,5}} | collective-permute-start | bytes 786440 | tf_op jit(solution)/shard_map/ppermute | solution.py:307
  4.0 9.3 %collective-permute-start.1 = (bf16[4,3,64,1024]{3,2,1,0:T(8,128)(2,1)}, bf16[4,3,64,1024]{3,2,1,0:T(8,128)(2,1)S(1)}, u32[]{:S(2)}, u32[]{:S(2)}) collective-permute-start(bf16[4,3,64,1024]{3,2,1,0:T(8,128)(2,1)} %bitcast.39), channel_id=1, source_target_pairs={{0,1},{1,0},{2,3},{3,2},{4,5},{5,4},{6,7},{7,6}} | collective-permute-start | bytes 4718600 | tf_op jit(solution)/shard_map/ppermute | solution.py:307
  4.2 7.1 %collective-permute-start.2 = (s32[128]{0:T(128)}, s32[128]{0:T(128)S(1)}, u32[]{:S(2)}, u32[]{:S(2)}) collective-permute-start(s32[128]{0:T(128)} %lens_ref.7), channel_id=1, source_target_pairs={{0,2},{2,0},{1,3},{3,1},{4,6},{6,4},{5,7},{7,5}} | collective-permute-start | bytes 1544 | tf_op jit(solution)/shard_map/ppermute | solution.py:307
  4.5 72.7 %collective-permute-start.8 = (bf16[1024,256]{1,0:T(8,128)(2,1)}, bf16[1024,256]{1,0:T(8,128)(2,1)}, u32[]{:S(2)}, u32[]{:S(2)}) collective-permute-start(bf16[1024,256]{1,0:T(8,128)(2,1)} %bitcast.48), channel_id=1, source_target_pairs={{0,1},{1,0},{2,3},{3,2},{4,5},{5,4},{6,7},{7,6}} | collective-permute-start | bytes 1572872 | tf_op jit(solution)/shard_map/ppermute | solution.py:307
  11.2 14.0 %collective-permute-start.9 = (bf16[1024,256]{1,0:T(8,128)(2,1)}, bf16[1024,256]{1,0:T(8,128)(2,1)}, u32[]{:S(2)}, u32[]{:S(2)}) collective-permute-start(bf16[1024,256]{1,0:T(8,128)(2,1)} %bitcast.49), channel_id=1, source_target_pairs={{0,4},{4,0},{1,5},{5,1},{2,6},{6,2},{3,7},{7,3}} | collective-permute-start | bytes 1572872 | tf_op jit(solution)/shard_map/ppermute | solution.py:307
  13.2 65.3 %collective-permute-start.11 = (bf16[704,1024]{1,0:T(8,128)(2,1)}, bf16[704,1024]{1,0:T(8,128)(2,1)}, u32[]{:S(2)}, u32[]{:S(2)}) collective-permute-start(bf16[704,1024]{1,0:T(8,128)(2,1)} %bitcast.43), channel_id=1, source_target_pairs={{0,1},{1,0},{2,3},{3,2},{4,5},{5,4},{6,7},{7,6}} | collective-permute-start | bytes 4325384 | tf_op jit(solution)/shard_map/ppermute | solution.py:307
  13.3 1.1 copy-start.14
  14.4 1.4 copy-start.1
  17.5 1.4 copy-start.15
  18.9 8.9 %copy-start = (bf16[1,1408,1024]{2,1,0:T(8,128)(2,1)S(1)}, bf16[1,1408,1024]{2,1,0:T(8,128)(2,1)}, u32[]{:S(2)}) copy-start(bf16[1,1408,1024]{2,1,0:T(8,128)(2,1)} %param.18) | copy-start | bytes 8650756
  20.1 12.8 %collective-permute-start.3 = (bf16[3,512,128]{2,1,0:T(8,128)(2,1)S(1)}, bf16[3,512,128]{2,1,0:T(8,128)(2,1)S(1)}, u32[]{:S(2)}, u32[]{:S(2)}) collective-permute-start(bf16[3,512,128]{2,1,0:T(8,128)(2,1)S(1)} %get-tuple-element.68), channel_id=1, source_target_pairs={{0,2},{2,0},{1,3},{3,1},{4,6},{6,4},{5,7},{7,5}} | collective-permute-start | bytes 1179656 | tf_op jit(solution)/shard_map/ppermute | solution.py:307
  25.2 53.4 %collective-permute-start.10 = (bf16[1024,256]{1,0:T(8,128)(2,1)}, bf16[1024,256]{1,0:T(8,128)(2,1)}, u32[]{:S(2)}, u32[]{:S(2)}) collective-permute-start(bf16[1024,256]{1,0:T(8,128)(2,1)} %collective-permute-done.9.wo_c), channel_id=1, source_target_pairs={{0,1},{1,0},{2,3},{3,2},{4,5},{5,4},{6,7},{7,6}} | collective-permute-start | bytes 1572872 | tf_op jit(solution)/shard_map/ppermute | solution.py:307
  27.8 5.2 %copy-start.13 = (s32[128]{0:T(128)S(1)}, s32[128]{0:T(128)}, u32[]{:S(2)}) copy-start(s32[128]{0:T(128)} %lens_ref.7) | copy-start | bytes 1540
  46.6 31.9 %copy-start.12 = (bf16[1,1024]{1,0:T(2,128)(2,1)S(1)}, bf16[1,1024]{1,0:T(2,128)(2,1)}, u32[]{:S(2)}) copy-start(bf16[1,1024]{1,0:T(2,128)(2,1)} %gain_ref.9) | copy-start | bytes 6148
  59.6 4.6 %collective-permute-start.20 = (bf16[64,512]{1,0:T(8,128)(2,1)S(1)}, bf16[64,512]{1,0:T(8,128)(2,1)}, u32[]{:S(2)}, u32[]{:S(2)}) collective-permute-start(bf16[64,512]{1,0:T(8,128)(2,1)S(1)} %get-tuple-element.90.o_own), channel_id=1, source_target_pairs={{0,4},{4,0},{1,5},{5,1},{2,6},{6,2},{3,7},{7,3}} | collective-permute-start | bytes 196616 | tf_op jit(solution)/shard_map/ppermute | solution.py:307
  61.1 5.5 %collective-permute-start.21 = (bf16[64,512]{1,0:T(8,128)(2,1)S(1)}, bf16[64,512]{1,0:T(8,128)(2,1)}, u32[]{:S(2)}, u32[]{:S(2)}) collective-permute-start(bf16[64,512]{1,0:T(8,128)(2,1)S(1)} %get-tuple-element.90.o_own), channel_id=1, source_target_pairs={{0,2},{2,0},{1,3},{3,1},{4,6},{6,4},{5,7},{7,5}} | collective-permute-start | bytes 196616 | tf_op jit(solution)/shard_map/ppermute | solution.py:307
  64.2 5.2 %collective-permute-start.22 = (bf16[64,512]{1,0:T(8,128)(2,1)S(1)}, bf16[64,512]{1,0:T(8,128)(2,1)S(1)}, u32[]{:S(2)}, u32[]{:S(2)}) collective-permute-start(bf16[64,512]{1,0:T(8,128)(2,1)S(1)} %get-tuple-element.90.o_own), channel_id=1, source_target_pairs={{0,6},{2,4},{4,2},{6,0},{1,7},{3,5},{5,3},{7,1}} | collective-permute-start | bytes 196616 | tf_op jit(solution)/shard_map/ppermute | solution.py:408
  66.7 4.5 %collective-permute-start.5 = (bf16[64,512]{1,0:T(8,128)(2,1)}, bf16[64,512]{1,0:T(8,128)(2,1)S(1)}, u32[]{:S(2)}, u32[]{:S(2)}) collective-permute-start(bf16[64,512]{1,0:T(8,128)(2,1)} %copy-done.19), channel_id=1, source_target_pairs={{0,4},{4,0},{1,5},{5,1},{2,6},{6,2},{3,7},{7,3}} | collective-permute-start | bytes 196616 | tf_op jit(solution)/shard_map/ppermute | solution.py:307
  69.5 4.9 %collective-permute-start.6 = (bf16[64,512]{1,0:T(8,128)(2,1)}, bf16[64,512]{1,0:T(8,128)(2,1)S(1)}, u32[]{:S(2)}, u32[]{:S(2)}) collective-permute-start(bf16[64,512]{1,0:T(8,128)(2,1)} %copy-done.19), channel_id=1, source_target_pairs={{0,2},{2,0},{1,3},{3,1},{4,6},{6,4},{5,7},{7,5}} | collective-permute-start | bytes 196616 | tf_op jit(solution)/shard_map/ppermute | solution.py:307
  71.1 5.4 %collective-permute-start.7 = (bf16[64,512]{1,0:T(8,128)(2,1)}, bf16[64,512]{1,0:T(8,128)(2,1)S(1)}, u32[]{:S(2)}, u32[]{:S(2)}) collective-permute-start(bf16[64,512]{1,0:T(8,128)(2,1)} %copy-done.19), channel_id=1, source_target_pairs={{0,6},{2,4},{4,2},{6,0},{1,7},{3,5},{5,3},{7,1}} | collective-permute-start | bytes 196616 | tf_op jit(solution)/shard_map/ppermute | solution.py:408
  74.4 21.7 %collective-permute-start.15 = (bf16[2,1024]{1,0:T(2,128)(2,1)S(1)}, bf16[2,1024]{1,0:T(2,128)(2,1)S(1)}, u32[]{:S(2)}, u32[]{:S(2)}) collective-permute-start(bf16[2,1024]{1,0:T(2,128)(2,1)S(1)} %pad_maximum_fusion.5), channel_id=1, source_target_pairs={{0,2},{2,0},{1,3},{3,1},{4,6},{6,4},{5,7},{7,5}} | collective-permute-start | bytes 12296 | tf_op jit(solution)/shard_map/ppermute | solution.py:307
  76.5 84.7 %collective-permute-start.48 = (bf16[160,1024]{1,0:T(8,128)(2,1)}, bf16[160,1024]{1,0:T(8,128)(2,1)}, u32[]{:S(2)}, u32[]{:S(2)}) collective-permute-start(bf16[160,1024]{1,0:T(8,128)(2,1)} %slice_bitcast_fusion), channel_id=1, source_target_pairs={{0,2},{2,0},{1,3},{3,1},{4,6},{6,4},{5,7},{7,5}} | collective-permute-start | bytes 983048 | tf_op jit(solution)/shard_map/ppermute | solution.py:307
  77.1 43.9 %collective-permute-start.18 = (bf16[2,3,64,1024]{3,2,1,0:T(8,128)(2,1)S(1)}, bf16[2,3,64,1024]{3,2,1,0:T(8,128)(2,1)S(1)}, u32[]{:S(2)}, u32[]{:S(2)}) collective-permute-start(bf16[2,3,64,1024]{3,2,1,0:T(8,128)(2,1)S(1)} %get-tuple-element.85), channel_id=1, source_target_pairs={{0,2},{2,0},{1,3},{3,1},{4,6},{6,4},{5,7},{7,5}} | collective-permute-start | bytes 2359304 | tf_op jit(solution)/shard_map/ppermute | solution.py:307
  78.6 1.4 copy-start.16
  79.9 1.0 copy-start.17
  87.9 8.8 %collective-permute-start.12 = (f32[64,1024]{1,0:T(8,128)S(1)}, f32[64,1024]{1,0:T(8,128)S(1)}, u32[]{:S(2)}, u32[]{:S(2)}) collective-permute-start(f32[64,1024]{1,0:T(8,128)S(1)} %get-tuple-element.81), channel_id=1, source_target_pairs={{0,4},{4,0},{1,5},{5,1},{2,6},{6,2},{3,7},{7,3}} | collective-permute-start | bytes 786440 | tf_op jit(solution)/shard_map/ppermute | solution.py:307
  95.3 6.4 %collective-permute-start.23 = (f32[64,1024]{1,0:T(8,128)S(1)}, f32[64,1024]{1,0:T(8,128)S(1)}, u32[]{:S(2)}, u32[]{:S(2)}) collective-permute-start(f32[64,1024]{1,0:T(8,128)S(1)} %get-tuple-element.97), channel_id=1, source_target_pairs={{0,4},{4,0},{1,5},{5,1},{2,6},{6,2},{3,7},{7,3}} | collective-permute-start | bytes 786440 | tf_op jit(solution)/shard_map/ppermute | solution.py:307
  96.0 26.0 %collective-permute-start.16 = (bf16[2,3,64,1024]{3,2,1,0:T(8,128)(2,1)S(1)}, bf16[2,3,64,1024]{3,2,1,0:T(8,128)(2,1)S(1)}, u32[]{:S(2)}, u32[]{:S(2)}) collective-permute-start(bf16[2,3,64,1024]{3,2,1,0:T(8,128)(2,1)S(1)} %get-tuple-element.83), channel_id=1, source_target_pairs={{0,2},{2,0},{1,3},{3,1},{4,6},{6,4},{5,7},{7,5}} | collective-permute-start | bytes 2359304 | tf_op jit(solution)/shard_map/ppermute | solution.py:307
  96.8 23.2 %collective-permute-start.13 = (bf16[32,1024]{1,0:T(8,128)(2,1)S(1)}, bf16[32,1024]{1,0:T(8,128)(2,1)S(1)}, u32[]{:S(2)}, u32[]{:S(2)}) collective-permute-start(bf16[32,1024]{1,0:T(8,128)(2,1)S(1)} %slice.87), channel_id=1, source_target_pairs={{0,2},{2,0},{1,3},{3,1},{4,6},{6,4},{5,7},{7,5}} | collective-permute-start | bytes 196616 | tf_op jit(solution)/shard_map/ppermute | solution.py:307
  101.8 19.3 %collective-permute-start.24 = (bf16[32,1024]{1,0:T(8,128)(2,1)S(1)}, bf16[32,1024]{1,0:T(8,128)(2,1)S(1)}, u32[]{:S(2)}, u32[]{:S(2)}) collective-permute-start(bf16[32,1024]{1,0:T(8,128)(2,1)S(1)} %slice.93), channel_id=1, source_target_pairs={{0,2},{2,0},{1,3},{3,1},{4,6},{6,4},{5,7},{7,5}} | collective-permute-start | bytes 196616 | tf_op jit(solution)/shard_map/ppermute | solution.py:307
  120.0 4.3 %collective-permute-start.14 = (bf16[32,1024]{1,0:T(8,128)(2,1)S(1)}, bf16[32,1024]{1,0:T(8,128)(2,1)S(1)}, u32[]{:S(2)}, u32[]{:S(2)}) collective-permute-start(bf16[32,1024]{1,0:T(8,128)(2,1)S(1)} %slice_select_fusion.3), channel_id=1, source_target_pairs={{0,4},{4,0},{1,5},{5,1},{2,6},{6,2},{3,7},{7,3}} | collective-permute-start | bytes 196616 | tf_op jit(solution)/shard_map/ppermute | solution.py:307
  121.1 4.6 %collective-permute-start.19 = (bf16[2,3,64,1024]{3,2,1,0:T(8,128)(2,1)S(1)}, bf16[2,3,64,1024]{3,2,1,0:T(8,128)(2,1)S(1)}, u32[]{:S(2)}, u32[]{:S(2)}) collective-permute-start(bf16[2,3,64,1024]{3,2,1,0:T(8,128)(2,1)S(1)} %collective-permute-done.18.refs_0_), channel_id=1, source_target_pairs={{0,1},{1,0},{2,3},{3,2},{4,5},{5,4},{6,7},{7,6}} | collective-permute-start | bytes 2359304 | tf_op jit(solution)/shard_map/ppermute | solution.py:307
  121.1 4.6 %collective-permute-start.25 = (bf16[32,1024]{1,0:T(8,128)(2,1)S(1)}, bf16[32,1024]{1,0:T(8,128)(2,1)S(1)}, u32[]{:S(2)}, u32[]{:S(2)}) collective-permute-start(bf16[32,1024]{1,0:T(8,128)(2,1)S(1)} %slice_select_fusion.2), channel_id=1, source_target_pairs={{0,4},{4,0},{1,5},{5,1},{2,6},{6,2},{3,7},{7,3}} | collective-permute-start | bytes 196616 | tf_op jit(solution)/shard_map/ppermute | solution.py:307
  122.1 5.6 %collective-permute-start.17 = (bf16[2,3,64,1024]{3,2,1,0:T(8,128)(2,1)S(1)}, bf16[2,3,64,1024]{3,2,1,0:T(8,128)(2,1)S(1)}, u32[]{:S(2)}, u32[]{:S(2)}) collective-permute-start(bf16[2,3,64,1024]{3,2,1,0:T(8,128)(2,1)S(1)} %collective-permute-done.16.refs_0_), channel_id=1, source_target_pairs={{0,1},{1,0},{2,3},{3,2},{4,5},{5,4},{6,7},{7,6}} | collective-permute-start | bytes 2359304 | tf_op jit(solution)/shard_map/ppermute | solution.py:307
  124.4 42.7 %collective-permute-start.29 = (bf16[64,1024]{1,0:T(8,128)(2,1)S(1)}, bf16[64,1024]{1,0:T(8,128)(2,1)S(1)}, u32[]{:S(2)}, u32[]{:S(2)}) collective-permute-start(bf16[64,1024]{1,0:T(8,128)(2,1)S(1)} %pad_maximum_fusion.1.rest_0_.hid_ref), channel_id=1, source_target_pairs={{0,2},{2,0},{1,3},{3,1},{4,6},{6,4},{5,7},{7,5}} | collective-permute-start | bytes 393224 | tf_op jit(solution)/shard_map/ppermute | solution.py:307
  143.6 20.5 %collective-permute-start.26 = (bf16[64,512]{1,0:T(8,128)(2,1)S(1)}, bf16[64,512]{1,0:T(8,128)(2,1)S(1)}, u32[]{:S(2)}, u32[]{:S(2)}) collective-permute-start(bf16[64,512]{1,0:T(8,128)(2,1)S(1)} %get-tuple-element.102.o_own), channel_id=1, source_target_pairs={{0,4},{4,0},{1,5},{5,1},{2,6},{6,2},{3,7},{7,3}} | collective-permute-start | bytes 196616 | tf_op jit(solution)/shard_map/ppermute | solution.py:307
  144.7 20.3 %collective-permute-start.27 = (bf16[64,512]{1,0:T(8,128)(2,1)S(1)}, bf16[64,512]{1,0:T(8,128)(2,1)S(1)}, u32[]{:S(2)}, u32[]{:S(2)}) collective-permute-start(bf16[64,512]{1,0:T(8,128)(2,1)S(1)} %get-tuple-element.102.o_own), channel_id=1, source_target_pairs={{0,2},{2,0},{1,3},{3,1},{4,6},{6,4},{5,7},{7,5}} | collective-permute-start | bytes 196616 | tf_op jit(solution)/shard_map/ppermute | solution.py:307
  145.6 20.6 %collective-permute-start.28 = (bf16[64,512]{1,0:T(8,128)(2,1)S(1)}, bf16[64,512]{1,0:T(8,128)(2,1)S(1)}, u32[]{:S(2)}, u32[]{:S(2)}) collective-permute-start(bf16[64,512]{1,0:T(8,128)(2,1)S(1)} %get-tuple-element.102.o_own), channel_id=1, source_target_pairs={{0,6},{2,4},{4,2},{6,0},{1,7},{3,5},{5,3},{7,1}} | collective-permute-start | bytes 196616 | tf_op jit(solution)/shard_map/ppermute | solution.py:408
  161.2 7.0 %collective-permute-start.33 = (bf16[64,512]{1,0:T(8,128)(2,1)S(1)}, bf16[64,512]{1,0:T(8,128)(2,1)S(1)}, u32[]{:S(2)}, u32[]{:S(2)}) collective-permute-start(bf16[64,512]{1,0:T(8,128)(2,1)S(1)} %get-tuple-element.109.o_own), channel_id=1, source_target_pairs={{0,4},{4,0},{1,5},{5,1},{2,6},{6,2},{3,7},{7,3}} | collective-permute-start | bytes 196616 | tf_op jit(solution)/shard_map/ppermute | solution.py:307
  164.1 53.1 %collective-permute-start.46 = (bf16[320,1024]{1,0:T(8,128)(2,1)}, bf16[320,1024]{1,0:T(8,128)(2,1)S(1)}, u32[]{:S(2)}, u32[]{:S(2)}) collective-permute-start(bf16[320,1024]{1,0:T(8,128)(2,1)} %slice.82), channel_id=1, source_target_pairs={{0,2},{2,0},{1,3},{3,1},{4,6},{6,4},{5,7},{7,5}} | collective-permute-start | bytes 1966088 | tf_op jit(solution)/shard_map/ppermute | solution.py:307
  165.0 50.5 %collective-permute-start.44 = (bf16[384,1024]{1,0:T(8,128)(2,1)}, bf16[384,1024]{1,0:T(8,128)(2,1)}, u32[]{:S(2)}, u32[]{:S(2)}) collective-permute-start(bf16[384,1024]{1,0:T(8,128)(2,1)} %slice.81), channel_id=1, source_target_pairs={{0,2},{2,0},{1,3},{3,1},{4,6},{6,4},{5,7},{7,5}} | collective-permute-start | bytes 2359304 | tf_op jit(solution)/shard_map/ppermute | solution.py:307
  166.2 36.3 %collective-permute-start.36 = (bf16[64,1024]{1,0:T(8,128)(2,1)S(1)}, bf16[64,1024]{1,0:T(8,128)(2,1)S(1)}, u32[]{:S(2)}, u32[]{:S(2)}) collective-permute-start(bf16[64,1024]{1,0:T(8,128)(2,1)S(1)} %pad_maximum_fusion.2.rest_0_.hid_ref), channel_id=1, source_target_pairs={{0,2},{2,0},{1,3},{3,1},{4,6},{6,4},{5,7},{7,5}} | collective-permute-start | bytes 393224 | tf_op jit(solution)/shard_map/ppermute | solution.py:307
  167.0 34.4 %collective-permute-start.34 = (bf16[64,512]{1,0:T(8,128)(2,1)S(1)}, bf16[64,512]{1,0:T(8,128)(2,1)S(1)}, u32[]{:S(2)}, u32[]{:S(2)}) collective-permute-start(bf16[64,512]{1,0:T(8,128)(2,1)S(1)} %get-tuple-element.109.o_own), channel_id=1, source_target_pairs={{0,2},{2,0},{1,3},{3,1},{4,6},{6,4},{5,7},{7,5}} | collective-permute-start | bytes 196616 | tf_op jit(solution)/shard_map/ppermute | solution.py:307
  168.2 34.2 %collective-permute-start.35 = (bf16[64,512]{1,0:T(8,128)(2,1)S(1)}, bf16[64,512]{1,0:T(8,128)(2,1)S(1)}, u32[]{:S(2)}, u32[]{:S(2)}) collective-permute-start(bf16[64,512]{1,0:T(8,128)(2,1)S(1)} %get-tuple-element.109.o_own), channel_id=1, source_target_pairs={{0,6},{2,4},{4,2},{6,0},{1,7},{3,5},{5,3},{7,1}} | collective-permute-start | bytes 196616 | tf_op jit(solution)/shard_map/ppermute | solution.py:408
  176.1 26.3 %copy-start.18 = (f32[64,1024]{1,0:T(8,128)}, f32[64,1024]{1,0:T(8,128)S(1)}, u32[]{:S(2)}) copy-start(f32[64,1024]{1,0:T(8,128)S(1)} %get-tuple-element.108) | copy-start | bytes 786436
  176.1 33.1 %copy-start.7 = (bf16[64,1024]{1,0:T(8,128)(2,1)}, bf16[64,1024]{1,0:T(8,128)(2,1)S(1)}, u32[]{:S(2)}) copy-start(bf16[64,1024]{1,0:T(8,128)(2,1)S(1)} %get-tuple-element.106) | copy-start | bytes 393220
  201.4 11.3 %collective-permute-start.49 = (bf16[160,1024]{1,0:T(8,128)(2,1)}, bf16[160,1024]{1,0:T(8,128)(2,1)}, u32[]{:S(2)}, u32[]{:S(2)}) collective-permute-start(bf16[160,1024]{1,0:T(8,128)(2,1)} %collective-permute-done.48.refs_0_), channel_id=1, source_target_pairs={{0,1},{1,0},{2,3},{3,2},{4,5},{5,4},{6,7},{7,6}} | collective-permute-start | bytes 983048 | tf_op jit(solution)/shard_map/ppermute | solution.py:307
  210.6 9.5 %collective-permute-start.37 = (f32[64,1024]{1,0:T(8,128)}, f32[64,1024]{1,0:T(8,128)}, u32[]{:S(2)}, u32[]{:S(2)}) collective-permute-start(f32[64,1024]{1,0:T(8,128)} %get-tuple-element.116), channel_id=1, source_target_pairs={{0,4},{4,0},{1,5},{5,1},{2,6},{6,2},{3,7},{7,3}} | collective-permute-start | bytes 786440 | tf_op jit(solution)/shard_map/ppermute | solution.py:307
  211.8 8.2 %copy-start.5 = (f32[64,1024]{1,0:T(8,128)S(1)}, f32[64,1024]{1,0:T(8,128)}, u32[]{:S(2)}) copy-start(f32[64,1024]{1,0:T(8,128)} %copy-done.4) | copy-start | bytes 786436
  211.8 8.2 %copy-start.10 = (bf16[64,1024]{1,0:T(8,128)(2,1)S(1)}, bf16[64,1024]{1,0:T(8,128)(2,1)}, u32[]{:S(2)}) copy-start(bf16[64,1024]{1,0:T(8,128)(2,1)} %copy-done.9) | copy-start | bytes 393220
  211.9 12.6 %copy-start.3 = (f32[64,1024]{1,0:T(8,128)S(1)}, f32[64,1024]{1,0:T(8,128)}, u32[]{:S(2)}) copy-start(f32[64,1024]{1,0:T(8,128)} %copy-done.2) | copy-start | bytes 786436
  211.9 12.6 %copy-start.8 = (bf16[64,1024]{1,0:T(8,128)(2,1)S(1)}, bf16[64,1024]{1,0:T(8,128)(2,1)}, u32[]{:S(2)}) copy-start(bf16[64,1024]{1,0:T(8,128)(2,1)} %copy-done.7) | copy-start | bytes 393220
  211.9 12.3 %collective-permute-start.30 = (f32[64,1024]{1,0:T(8,128)}, f32[64,1024]{1,0:T(8,128)S(1)}, u32[]{:S(2)}, u32[]{:S(2)}) collective-permute-start(f32[64,1024]{1,0:T(8,128)} %copy-done.18), channel_id=1, source_target_pairs={{0,4},{4,0},{1,5},{5,1},{2,6},{6,2},{3,7},{7,3}} | collective-permute-start | bytes 786440 | tf_op jit(solution)/shard_map/ppermute | solution.py:307
  215.1 40.4 %collective-permute-start.40 = (bf16[256,1024]{1,0:T(8,128)(2,1)S(1)}, bf16[256,1024]{1,0:T(8,128)(2,1)S(1)}, u32[]{:S(2)}, u32[]{:S(2)}) collective-permute-start(bf16[256,1024]{1,0:T(8,128)(2,1)S(1)} %slice.79), channel_id=1, source_target_pairs={{0,2},{2,0},{1,3},{3,1},{4,6},{6,4},{5,7},{7,5}} | collective-permute-start | bytes 1572872 | tf_op jit(solution)/shard_map/ppermute | solution.py:307
  215.5 35.9 %collective-permute-start.42 = (bf16[288,1024]{1,0:T(8,128)(2,1)S(1)}, bf16[288,1024]{1,0:T(8,128)(2,1)S(1)}, u32[]{:S(2)}, u32[]{:S(2)}) collective-permute-start(bf16[288,1024]{1,0:T(8,128)(2,1)S(1)} %slice.80), channel_id=1, source_target_pairs={{0,2},{2,0},{1,3},{3,1},{4,6},{6,4},{5,7},{7,5}} | collective-permute-start | bytes 1769480 | tf_op jit(solution)/shard_map/ppermute | solution.py:307
  217.2 40.4 %collective-permute-start.45 = (bf16[384,1024]{1,0:T(8,128)(2,1)}, bf16[384,1024]{1,0:T(8,128)(2,1)S(1)}, u32[]{:S(2)}, u32[]{:S(2)}) collective-permute-start(bf16[384,1024]{1,0:T(8,128)(2,1)} %collective-permute-done.44.refs_0_), channel_id=1, source_target_pairs={{0,1},{1,0},{2,3},{3,2},{4,5},{5,4},{6,7},{7,6}} | collective-permute-start | bytes 2359304 | tf_op jit(solution)/shard_map/ppermute | solution.py:307
  220.1 35.5 %collective-permute-start.47 = (bf16[320,1024]{1,0:T(8,128)(2,1)S(1)}, bf16[320,1024]{1,0:T(8,128)(2,1)S(1)}, u32[]{:S(2)}, u32[]{:S(2)}) collective-permute-start(bf16[320,1024]{1,0:T(8,128)(2,1)S(1)} %collective-permute-done.46.refs_0_), channel_id=1, source_target_pairs={{0,1},{1,0},{2,3},{3,2},{4,5},{5,4},{6,7},{7,6}} | collective-permute-start | bytes 1966088 | tf_op jit(solution)/shard_map/ppermute | solution.py:307
  224.2 17.9 %collective-permute-start.38 = (bf16[32,1024]{1,0:T(8,128)(2,1)S(1)}, bf16[32,1024]{1,0:T(8,128)(2,1)S(1)}, u32[]{:S(2)}, u32[]{:S(2)}) collective-permute-start(bf16[32,1024]{1,0:T(8,128)(2,1)S(1)} %slice.97), channel_id=1, source_target_pairs={{0,2},{2,0},{1,3},{3,1},{4,6},{6,4},{5,7},{7,5}} | collective-permute-start | bytes 196616 | tf_op jit(solution)/shard_map/ppermute | solution.py:307
  242.0 4.3 %collective-permute-start.31 = (bf16[32,1024]{1,0:T(8,128)(2,1)S(1)}, bf16[32,1024]{1,0:T(8,128)(2,1)S(1)}, u32[]{:S(2)}, u32[]{:S(2)}) collective-permute-start(bf16[32,1024]{1,0:T(8,128)(2,1)S(1)} %slice.95), channel_id=1, source_target_pairs={{0,2},{2,0},{1,3},{3,1},{4,6},{6,4},{5,7},{7,5}} | collective-permute-start | bytes 196616 | tf_op jit(solution)/shard_map/ppermute | solution.py:307
  246.3 4.3 %collective-permute-start.39 = (bf16[32,1024]{1,0:T(8,128)(2,1)S(1)}, bf16[32,1024]{1,0:T(8,128)(2,1)S(1)}, u32[]{:S(2)}, u32[]{:S(2)}) collective-permute-start(bf16[32,1024]{1,0:T(8,128)(2,1)S(1)} %slice_select_fusion), channel_id=1, source_target_pairs={{0,4},{4,0},{1,5},{5,1},{2,6},{6,2},{3,7},{7,3}} | collective-permute-start | bytes 196616 | tf_op jit(solution)/shard_map/ppermute | solution.py:307
  250.6 4.3 %collective-permute-start.32 = (bf16[32,1024]{1,0:T(8,128)(2,1)S(1)}, bf16[32,1024]{1,0:T(8,128)(2,1)S(1)}, u32[]{:S(2)}, u32[]{:S(2)}) collective-permute-start(bf16[32,1024]{1,0:T(8,128)(2,1)S(1)} %slice_select_fusion.1), channel_id=1, source_target_pairs={{0,4},{4,0},{1,5},{5,1},{2,6},{6,2},{3,7},{7,3}} | collective-permute-start | bytes 196616 | tf_op jit(solution)/shard_map/ppermute | solution.py:307
  251.4 9.0 %collective-permute-start.43 = (bf16[288,1024]{1,0:T(8,128)(2,1)S(1)}, bf16[288,1024]{1,0:T(8,128)(2,1)S(1)}, u32[]{:S(2)}, u32[]{:S(2)}) collective-permute-start(bf16[288,1024]{1,0:T(8,128)(2,1)S(1)} %collective-permute-done.42.refs_0_), channel_id=1, source_target_pairs={{0,1},{1,0},{2,3},{3,2},{4,5},{5,4},{6,7},{7,6}} | collective-permute-start | bytes 1769480 | tf_op jit(solution)/shard_map/ppermute | solution.py:307
  255.6 6.7 %collective-permute-start.41 = (bf16[256,1024]{1,0:T(8,128)(2,1)S(1)}, bf16[256,1024]{1,0:T(8,128)(2,1)S(1)}, u32[]{:S(2)}, u32[]{:S(2)}) collective-permute-start(bf16[256,1024]{1,0:T(8,128)(2,1)S(1)} %collective-permute-done.40.refs_0_), channel_id=1, source_target_pairs={{0,1},{1,0},{2,3},{3,2},{4,5},{5,4},{6,7},{7,6}} | collective-permute-start | bytes 1572872 | tf_op jit(solution)/shard_map/ppermute | solution.py:307
  (7 other events, 5.2 us)
